TPU v7x, 32 devices: a whole 2x2x4 slice. The times are simulated.
32 devices in a mesh: section: 2 (over x), seq: 8 (over z, y), rep: 2 (over core).
Axes of the slice: x: 2, y: 2, z: 4, core: 2. Of those that a mesh axis runs over, the one named last changes fastest.
Arguments:
- queries: bfloat16 [512, 2560], P('seq', ('section', 'rep')), may hold values from -5 to 5
- keys: bfloat16 [512, 2560], P('seq', ('section', 'rep')), may hold values from -5 to 5
- values: bfloat16 [512, 2560], P('seq', ('section', 'rep')), may hold values from -6 to 6
- block_order: int32 [16], replicated, may hold values from 0 to 15, each once
- wo: bfloat16 [2560, 5120], P(('section', 'rep'), 'seq'), may hold values from -0.125 to 0.125
- resid: bfloat16 [4, 5120, 128], P(('section', 'rep'), 'seq'), may hold values from -60 to 60
- gain: bfloat16 [5120], P('seq'), may hold values from 0.099609375 to 1.8984375
- w_gate: bfloat16 [13824, 5120], P('seq'), may hold values from -0.078125 to 0.078125
- w_up: bfloat16 [13824, 5120], P('seq'), may hold values from -0.078125 to 0.078125
- w_down: bfloat16 [13824, 5120], P('seq'), may hold values from -0.0625 to 0.0625
Outputs:
- mixed: bfloat16 [4, 5120, 128], P(('section', 'rep'), 'seq')
Inputs may be any that keep to these rules, and one draw needn't show every extreme that they name: `block_order`: each number once.
All inputs are finite; a program needn't handle non-finite values.
Results may differ from a plain program's by a relative error of at most 0.0055.
Values may be sent and summed in bfloat16 or wider, within the bound.
No kernel may reach another device: no remote copies, remote signals or barrier semaphores. Data moves between devices by JAX's collectives and lax.ppermute only.
A program may use at most 128 MiB of HBM per device.

v0:
```python
import jax
import jax.numpy as jnp
from jax import lax
from jax.sharding import PartitionSpec as P

D = 5120
HEAD_DIM = 128


def key_positions(order, start, count, block_rows):
    row_ids = start + jnp.arange(count, dtype=jnp.int32)
    owners = row_ids // block_rows
    match = owners[:, None] == jnp.arange(order.shape[0], dtype=jnp.int32)[None, :]
    first = jnp.sum(jnp.where(match, order[None, :], 0), axis=1)
    return first * block_rows + row_ids % block_rows


def on_device(queries, keys, values, block_order, wo, resid, gain, w_gate, w_up, w_down):
    seq_dev = queries.shape[0]
    heads_dev = queries.shape[1] // HEAD_DIM
    groups = lax.axis_size("section") * lax.axis_size("rep")
    n_seq = lax.axis_size("seq")
    sub_rows = seq_dev // groups
    block_rows = seq_dev // 2
    query_start = lax.axis_index("seq") * seq_dev
    query_pos = key_positions(block_order, query_start, seq_dev, block_rows)
    query_heads = queries.reshape(seq_dev, heads_dev, HEAD_DIM)
    scale = HEAD_DIM ** (-0.5)
    running_max = jnp.full((seq_dev, heads_dev), -1e30, jnp.float32)
    key_piece = lax.all_gather(keys, "seq", axis=0, tiled=True)
    value_piece = lax.all_gather(values, "seq", axis=0, tiled=True)
    count = key_piece.shape[0]
    key_pos = key_positions(block_order, jnp.int32(0), count, block_rows)
    scores = (
        jnp.einsum(
            "qhd,khd->qhk",
            query_heads,
            key_piece.reshape(count, heads_dev, HEAD_DIM),
            preferred_element_type=jnp.float32,
        )
        * scale
    )
    visible = (key_pos[None, :] <= query_pos[:, None])[:, None, :]
    new_max = jnp.maximum(running_max, jnp.max(jnp.where(visible, scores, -1e30), axis=-1))
    probs = jnp.where(visible, jnp.exp(scores - new_max[..., None]), 0.0)
    total = jnp.sum(probs, axis=-1)
    weighted = jnp.einsum(
        "qhk,khd->qhd",
        probs.astype(jnp.bfloat16),
        value_piece.reshape(count, heads_dev, HEAD_DIM),
        preferred_element_type=jnp.float32,
    )
    running_max, total, weighted = (new_max, total, weighted)
    attended = (
        (weighted / total[..., None]).astype(jnp.bfloat16).reshape(seq_dev, heads_dev * HEAD_DIM)
    )
    columns = wo.shape[1]
    token_count = n_seq * sub_rows
    parts = attended.reshape(groups, sub_rows, heads_dev * HEAD_DIM)
    group_rows = lax.all_to_all(parts, ("section", "rep"), split_axis=0, concat_axis=2, tiled=True)
    wo_columns = lax.all_gather(wo, ("section", "rep"), axis=0, tiled=True)
    piece = lax.all_gather(group_rows, "seq", axis=0, tiled=True)
    flat = piece.reshape(piece.shape[0] * piece.shape[1], piece.shape[2])
    product = jnp.dot(flat, wo_columns, preferred_element_type=jnp.float32)
    projected = product.reshape(piece.shape[0], piece.shape[1], columns)
    projected_cols = projected.reshape(token_count, columns).T
    carried = resid.reshape(columns, token_count).astype(jnp.float32) + projected_cols
    squares = lax.psum(jnp.sum(carried * carried, axis=0), "seq")
    normed = (
        carried * lax.rsqrt(squares / D + 1e-05)[None, :] * gain.astype(jnp.float32)[:, None]
    ).astype(jnp.bfloat16)
    piece = lax.all_gather(normed, "seq", axis=0, tiled=True)
    gate_sum = jnp.dot(w_gate, piece, preferred_element_type=jnp.float32)
    up_sum = jnp.dot(w_up, piece, preferred_element_type=jnp.float32)
    hidden = (jax.nn.silu(gate_sum) * up_sum).astype(jnp.bfloat16)
    term = lax.dot_general(
        w_down, hidden, (((0,), (0,)), ((), ())), preferred_element_type=jnp.float32
    )
    down = lax.psum_scatter(term, "seq", scatter_dimension=0, tiled=True)
    return (carried + down).astype(jnp.bfloat16).reshape(resid.shape)


def solution(mesh):
    return jax.shard_map(
        on_device,
        mesh=mesh,
        in_specs=(
            P("seq", ("section", "rep")),
            P("seq", ("section", "rep")),
            P("seq", ("section", "rep")),
            P(),
            P(("section", "rep"), "seq"),
            P(("section", "rep"), "seq", None),
            P("seq"),
            P("seq", None),
            P("seq", None),
            P("seq", None),
        ),
        out_specs=P(("section", "rep"), "seq", None),
        check_vma=False,
    )
```

profile of v0, /device:TPU:0, one launch (start us, length us, event | category | flops | bytes accessed | tf_op | source)
XLA Modules:
  0.0 288.4 jit_solution(9217807981591576571)
XLA Ops:
  6.5 0.7 all-gather.3.cloned.1.call-update
  7.3 33.6 %all_gather.15 = bf16[512,640]{1,0:T(8,128)(2,1)S(1)} all-gather(bf16[64,640]{1,0:T(8,128)(2,1)} %param.11), channel_id=1, replica_groups=mesh['section'=2,'seq'=8,'rep'=2] {'seq'}, dimensions={0}, use_global_device_ids=true | all-gather | bytes 737280 | tf_op jit(solution)/shard_map/all_gather | solution.py:30
  40.9 0.3 copy.33
  41.1 0.0 copy-start.3
  41.2 31.9 %all_gather.16 = bf16[512,640]{1,0:T(8,128)(2,1)S(1)} all-gather(bf16[64,640]{1,0:T(8,128)(2,1)} %param.12), channel_id=1, replica_groups=mesh['section'=2,'seq'=8,'rep'=2] {'seq'}, dimensions={0}, use_global_device_ids=true | all-gather | bytes 737280 | tf_op jit(solution)/shard_map/all_gather | solution.py:31
  73.1 0.3 copy.36
  73.4 0.1 select_reduce_fusion.2
  73.5 0.1 select_reduce_fusion.1
  73.6 0.1 broadcast_compare_fusion
  73.7 0.3 select_reduce_fusion
  74.0 0.3 fusion.6
  74.3 0.4 fusion.5
  74.7 0.1 copy.38
  74.7 0.7 reshape_reshape.3
  75.5 3.3 %all-to-all-start = ((bf16[4,16,640]{2,1,0:T(8,128)(2,1)}), bf16[4,16,640]{2,1,0:T(8,128)(2,1)S(1)}, u32[]{:S(2)}, u32[]{:S(2)}) async-start(bf16[4,16,640]{2,1,0:T(8,128)(2,1)} %reshape_reshape.3), calls=%async_computation | async-start | bytes 163840 | tf_op jit(solution)/shard_map/all_to_all | solution.py:60
  78.8 0.0 all-gather.5.cloned.1.call-start
  78.9 0.2 copy.32
  79.0 3.9 %all-to-all-done = bf16[4,16,640]{2,1,0:T(8,128)(2,1)S(1)} async-done(((bf16[4,16,640]{2,1,0:T(8,128)(2,1)}), bf16[4,16,640]{2,1,0:T(8,128)(2,1)S(1)}, u32[]{:S(2)}, u32[]{:S(2)}) %all-to-all-start) | async-done | bytes 81952 | tf_op jit(solution)/shard_map/all_to_all | solution.py:60
  83.0 31.7 %all_gather.17 = bf16[8,16,2560]{2,1,0:T(8,128)(2,1)S(1)} all-gather(bf16[1,16,2560]{2,1,0:T(8,128)(2,1)S(1)} %bitcast.59), channel_id=1, replica_groups=mesh['section'=2,'seq'=8,'rep'=2] {'seq'}, dimensions={0}, use_global_device_ids=true | all-gather | bytes 737280 | tf_op jit(solution)/shard_map/all_gather | solution.py:62
  114.6 2.7 multiply_reduce_fusion
  117.3 21.5 %psum.7 = f32[128]{0:T(128)S(1)} all-reduce(f32[128]{0:T(128)S(1)} %get-tuple-element.7), channel_id=1, replica_groups=mesh['section'=2,'seq'=8,'rep'=2] {'seq'}, use_global_device_ids=true, to_apply=%region_5.6 | all-reduce | flops 128 | bytes 1024 | tf_op jit(solution)/shard_map/psum | solution.py:68
  138.9 0.8 multiply_convert_fusion
  139.6 0.0 all-gather.5.cloned.1.call-update
  139.7 0.0 reduce-scatter.2.cloned.1.call-start
  139.7 38.9 %all-gather.5.cloned.1.call-done = bf16[5120,128]{0,1:T(8,128)(2,1)} async-done(((bf16[640,128]{0,1:T(8,128)(2,1)}), bf16[5120,128]{0,1:T(8,128)(2,1)}) %all-gather.5.cloned.1.call-update) | async-done | bytes 1310736 | tf_op jit(solution)/shard_map/all_gather | solution.py:72
  178.6 11.1 %convolution_bitcast_fusion.2 = f32[1728,128]{1,0:T(8,128)S(1)} fusion(bf16[5120,128]{0,1:T(8,128)(2,1)} %all-gather.5.cloned.1.call-done, bf16[1728,5120]{1,0:T(8,128)(2,1)} %param.17), kind=kOutput, calls=%fused_computation.3 | convolution fusion | flops 2264924160 | bytes 19890176 | tf_op jit(solution)/shard_map/dot_general | solution.py:73
  189.7 0.0 copy-start.1
  189.7 20.6 %convolution_bitcast_fusion = f32[5120,128]{0,1:T(8,128)} fusion(bf16[1728,5120]{1,0:T(8,128)(2,1)} %param.19, bf16[5120,128]{0,1:T(8,128)(2,1)S(1)} %copy-done.2, bf16[1728,5120]{1,0:T(8,128)(2,1)} %param.18, f32[1728,128]{1,0:T(8,128)S(1)} %convolution_bitcast_fusion.2), kind=kOutput, calls=%fused_computation | convolution fusion | flops 4531175424 | bytes 40206336 | tf_op jit(solution)/shard_map/dot_general | solution.py:76
  210.4 0.0 reduce-scatter.2.cloned.1.call-update
  210.4 69.7 %reduce-scatter.2.cloned.1.call-done = f32[640,128]{0,1:T(8,128)} async-done(((f32[5120,128]{0,1:T(8,128)}), f32[640,128]{0,1:T(8,128)}) %reduce-scatter.2.cloned.1.call-update) | async-done | bytes 327696 | tf_op jit(solution)/shard_map/reduce_scatter | solution.py:79
  280.1 1.0 fusion.13
  281.1 0.8 copy.40
  (20 shorter events, 0.1 us)
Async XLA Ops:
  6.5 67.1 %copy-start = (bf16[64,640]{1,0:T(8,128)(2,1)S(1)}, bf16[64,640]{1,0:T(8,128)(2,1)}, u32[]{:S(2)}) copy-start(bf16[64,640]{1,0:T(8,128)(2,1)} %param.10) | copy-start | bytes 245764
  6.5 66.8 %copy-start.5 = (s32[16]{0:T(128)S(1)}, s32[16]{0:T(128)}, u32[]{:S(2)}) copy-start(s32[16]{0:T(128)} %param.13) | copy-start | bytes 196
  6.5 108.1 %all-gather.3.cloned.1.call-start = ((), (), s32[]{:S(2)}) async-start(), calls=%async_computation.2 | async-start | bytes 4096000 | tf_op jit(solution)/shard_map/all_gather | solution.py:61
  41.1 37.7 %copy-start.3 = (bf16[1,640,128]{2,1,0:T(8,128)(2,1)S(1)}, bf16[1,640,128]{2,1,0:T(8,128)(2,1)}, u32[]{:S(2)}) copy-start(bf16[1,640,128]{2,1,0:T(8,128)(2,1)} %param.15) | copy-start | bytes 491524
  73.1 5.9 %copy-start.4 = (bf16[640]{0:T(1024)(128)(2,1)S(1)}, bf16[640]{0:T(1024)(128)(2,1)}, u32[]{:S(2)}) copy-start(bf16[640]{0:T(1024)(128)(2,1)} %param.16) | copy-start | bytes 3844
  75.5 7.5 %all-to-all-start = ((bf16[4,16,640]{2,1,0:T(8,128)(2,1)}), bf16[4,16,640]{2,1,0:T(8,128)(2,1)S(1)}, u32[]{:S(2)}, u32[]{:S(2)}) async-start(bf16[4,16,640]{2,1,0:T(8,128)(2,1)} %reshape_reshape.3), calls=%async_computation | async-start | bytes 163840 | tf_op jit(solution)/shard_map/all_to_all | solution.py:60
  78.8 99.8 %all-gather.5.cloned.1.call-start = ((), (), s32[]{:S(2)}) async-start(), calls=%async_computation.3 | async-start | bytes 1474560 | tf_op jit(solution)/shard_map/all_gather | solution.py:72
  139.7 140.4 %reduce-scatter.2.cloned.1.call-start = ((), (), s32[]{:S(2)}) async-start(), calls=%async_computation.4 | async-start | bytes 2949120 | tf_op jit(solution)/shard_map/reduce_scatter | solution.py:79
  178.6 11.1 %copy-start.2 = (bf16[5120,128]{0,1:T(8,128)(2,1)S(1)}, bf16[5120,128]{0,1:T(8,128)(2,1)}, u32[]{:S(2)}) copy-start(bf16[5120,128]{0,1:T(8,128)(2,1)} %all-gather.5.cloned.1.call-done) | copy-start | bytes 3932164
  189.7 92.2 %copy-start.1 = (bf16[64,640]{1,0:T(8,128)(2,1)S(1)}, bf16[64,640]{1,0:T(8,128)(2,1)}, u32[]{:S(2)}) copy-start(bf16[64,640]{1,0:T(8,128)(2,1)} %param.10) | copy-start | bytes 245764
Sparse Core Ops, SparseCore 0:
  8.9 31.9 all-gather.2
  139.8 38.8 all-gather.4
  210.5 69.5 reduce-scatter.1
where the time goes:
time: 289 us; the launch traced here: 288 us
  blocking collectives  119 us (41%)
  waiting for transfers between devices  113 us (39%)
  matrix products  35.1 us (12%)
  between operations  13.3 us (5%)
  starting transfers between devices  3.38 us (1%)
    reduce_scatter x1, waiting for transfers between devices, on_device(): down = lax.psum_scatter(term, 'seq', scatter_dimension=0, tiled=True)  69.7 us
    all_gather x1, waiting for transfers between devices, on_device(): piece = lax.all_gather(normed, 'seq', axis=0, tiled=True)  38.9 us
    all_gather x1, blocking collectives, on_device(): key_piece = lax.all_gather(keys, 'seq', axis=0, tiled=True)  33.6 us
    all_gather x1, blocking collectives, on_device(): value_piece = lax.all_gather(values, 'seq', axis=0, tiled=True)  31.9 us
    all_gather x1, blocking collectives, on_device(): piece = lax.all_gather(group_rows, 'seq', axis=0, tiled=True)  31.7 us
    psum x1, blocking collectives, on_device(): squares = lax.psum(jnp.sum(carried * carried, axis=0), 'seq')  21.5 us
    dot_general x1, matrix products, on_device(): lax.dot_general(w_down, hidden, (((0,), (0,)), ((), ())), preferred_eleme...  20.6 us
    dot_general x1, matrix products, on_device(): gate_sum = jnp.dot(w_gate, piece, preferred_element_type=jnp.float32)  11.1 us
  transfers between devices with their start and end apart: 4, of which 3 were waited for; matrix products, arithmetic and copies ran while one was open for 1% of the time, Pallas kernels for 0%

commit v1 on v0

--- a/solution.py
+++ b/solution.py
@@ -1,10 +1,21 @@
+import math
+
 import jax
 import jax.numpy as jnp
 from jax import lax
+from jax.experimental import pallas as pl
+from jax.experimental.pallas import tpu as pltpu
 from jax.sharding import PartitionSpec as P
 
 D = 5120
 HEAD_DIM = 128
+EPS = 1e-05
+LOG2E = 1.4426950408889634
+MIB = 1 << 20
+FETCH_FLOPS = 300
+VMEM = pl.BlockSpec(memory_space=pltpu.VMEM)
+HBM = pl.BlockSpec(memory_space=pltpu.MemorySpace.HBM)
+SMEM = pl.BlockSpec(memory_space=pltpu.SMEM)
 
 
 def key_positions(order, start, count, block_rows):
@@ -15,7 +26,7 @@
     return first * block_rows + row_ids % block_rows
 
 
-def on_device(queries, keys, values, block_order, wo, resid, gain, w_gate, w_up, w_down):
+def gathered(queries, keys, values, block_order, wo, resid, gain, w_gate, w_up, w_down):
     seq_dev = queries.shape[0]
     heads_dev = queries.shape[1] // HEAD_DIM
     groups = lax.axis_size("section") * lax.axis_size("rep")
@@ -80,6 +91,305 @@
     return (carried + down).astype(jnp.bfloat16).reshape(resid.shape)
 
 
+def call(body, outs, args, scalars=0, scratch=(), limit=7, flops=0, nbytes=0, aliases=None, in_place=()):
+    spaces = [SMEM] * scalars + [VMEM] * (len(args) - scalars)
+    for i in in_place:
+        spaces[i] = HBM
+    return pl.pallas_call(
+        body,
+        out_shape=outs,
+        in_specs=spaces,
+        out_specs=jax.tree.map(lambda _: VMEM, outs),
+        scratch_shapes=list(scratch),
+        input_output_aliases=aliases or {},
+        compiler_params=pltpu.CompilerParams(vmem_limit_bytes=limit * MIB),
+        cost_estimate=pl.CostEstimate(flops=flops, bytes_accessed=nbytes, transcendentals=0),
+    )(*args)
+
+
+def struct(shape, dtype):
+    return jax.ShapeDtypeStruct(shape, dtype)
+
+
+def swap(x, offset, n_seq):
+    return lax.ppermute(x, "seq", [(i, i ^ offset) for i in range(n_seq)])
+
+
+def gather(x, n_seq):
+    got = {4: swap(x, 4, n_seq), 2: swap(x, 2, n_seq), 1: swap(x, 1, n_seq)}
+    got[6] = swap(got[4], 2, n_seq)
+    for r in (2, 4, 6):
+        got[r + 1] = swap(got[r], 1, n_seq)
+    return [x] + [got[r] for r in range(1, n_seq)]
+
+
+def in_hbm(x):
+    return pltpu.with_memory_space_constraint(x, pltpu.MemorySpace.HBM)
+
+
+def fetch(arrays, outs):
+    def body(*refs):
+        ins, refs = refs[: len(arrays)], refs[len(arrays) :]
+        tiles, sems = refs[:-1], refs[-1]
+        rows_of = [(ref, k) for ref in ins for k in range(ref.shape[0] // step)]
+        spots = [(tile, k) for tile in tiles for k in range(tile.shape[0] // step)]
+        copies = [
+            pltpu.make_async_copy(a.at[pl.ds(i * step, step)], b.at[pl.ds(k * step, step)], sems.at[n])
+            for n, ((a, i), (b, k)) in enumerate(zip(rows_of, spots))
+        ]
+        for c in copies:
+            c.start()
+        for c in copies:
+            c.wait()
+
+    step = math.gcd(*outs, *(a.shape[0] for a in arrays))
+    width, dtype = arrays[0].shape[1], arrays[0].dtype
+    nbytes = 2 * sum(outs) * width
+    return pl.pallas_call(
+        body,
+        out_shape=[pltpu.VMEM((rows, width), dtype) for rows in outs],
+        in_specs=[HBM] * len(arrays),
+        out_specs=[VMEM] * len(outs),
+        scratch_shapes=[pltpu.SemaphoreType.DMA((sum(outs) // step,))],
+        compiler_params=pltpu.CompilerParams(vmem_limit_bytes=MIB),
+        cost_estimate=pl.CostEstimate(flops=FETCH_FLOPS * nbytes, bytes_accessed=nbytes, transcendentals=0),
+    )(*(in_hbm(a) for a in arrays))
+
+
+def attend_body(n_seq, seq_dev, heads_dev, groups, reps):
+    sub = seq_dev // groups
+    half = seq_dev // 2
+    tokens = n_seq * seq_dev
+    per_group = n_seq * sub
+
+    def body(place, *refs):
+        blocks, wo_t, send, keep, att = refs[:n_seq], *refs[n_seq:]
+        me, section, rep = place[0], place[1], place[2]
+        lane = lax.broadcasted_iota(jnp.int32, (1, tokens), 1)
+        row = lax.broadcasted_iota(jnp.int32, (seq_dev, 1), 0)
+        key_pos = jnp.zeros((1, tokens), jnp.int32)
+        query_pos = []
+        for r in range(n_seq):
+            source = me ^ r
+            low, high = place[3 + 2 * source] * half, place[4 + 2 * source] * half
+            key_pos = jnp.where(lane >= r * seq_dev, low + lane - r * seq_dev, key_pos)
+            key_pos = jnp.where(lane >= r * seq_dev + half, high + lane - r * seq_dev - half, key_pos)
+            query_pos.append(jnp.where(row < half, low + row, high + row - half))
+        query_pos = jnp.concatenate(query_pos, axis=0)
+        for h in range(heads_dev):
+            cols = pl.ds(h * HEAD_DIM, HEAD_DIM)
+            q, k, v = (
+                jnp.concatenate([b[pl.ds(i * seq_dev, seq_dev), cols] for b in blocks], axis=0)
+                for i in range(3)
+            )
+            scores = lax.dot_general(q, k, (((1,), (1,)), ((), ())), preferred_element_type=jnp.float32)
+            scores = jnp.where(key_pos <= query_pos, scores, -1e30)
+            top = jnp.max(scores, axis=-1, keepdims=True)
+            probs = jnp.exp2((scores - top) * (HEAD_DIM**-0.5 * LOG2E))
+            total = jnp.sum(probs, axis=-1, keepdims=True)
+            out = jnp.dot(probs.astype(jnp.bfloat16), v, preferred_element_type=jnp.float32)
+            out = (out / total).astype(jnp.bfloat16)
+            for r in range(n_seq):
+                source = me ^ r
+                for g in range(groups):
+                    slot = ((g % reps) ^ rep) * (groups // reps) + ((g // reps) ^ section)
+                    start = pl.multiple_of(slot * per_group + source * sub, sub)
+                    at = r * seq_dev + g * sub
+                    att[pl.ds(start, sub), cols] = out[at : at + sub]
+        product = lax.dot_general(
+            wo_t[...], att[...], (((1,), (1,)), ((), ())), preferred_element_type=jnp.float32
+        )
+        keep[...] = product[:, : tokens // 2]
+        send[...] = product[:, tokens // 2 :].astype(jnp.bfloat16)
+
+    return body
+
+
+def halve_body(keep, got, send, rest):
+    half = rest.shape[1]
+    rest[...] = keep[:, :half] + got[:, :half].astype(jnp.float32)
+    send[...] = (keep[:, half:] + got[:, half:].astype(jnp.float32)).astype(jnp.bfloat16)
+
+
+def carry_body(rest, got, resid, gain, carried, out):
+    columns = rest.shape[0]
+    total = rest[...] + got[...].astype(jnp.float32) + resid[...].astype(jnp.float32)
+    carried[...] = total
+    squares = jnp.sum(total * total, axis=0, keepdims=True)
+    high = squares.astype(jnp.bfloat16)
+    low = (squares - high.astype(jnp.float32)).astype(jnp.bfloat16)
+    pick = lax.broadcasted_iota(jnp.int32, (16, total.shape[1]), 0)
+    both = jnp.where(pick == 0, high.astype(jnp.float32), jnp.where(pick == 1, low.astype(jnp.float32), 0.0))
+    out[pl.ds(0, columns), :] = (total * gain[...]).astype(jnp.bfloat16)
+    out[pl.ds(columns, 16), :] = both.astype(jnp.bfloat16)
+
+
+def row_tile(rows):
+    return max(t for t in range(16, 601, 16) if rows % t == 0)
+
+
+def gate_body(offsets, columns, tiles, first, last):
+    n = len(offsets)
+
+    def body(place, *refs):
+        xs, refs = refs[:n], refs[n:]
+        weights, refs = (refs[: len(tiles)], refs[len(tiles) : 2 * len(tiles)]), refs[2 * len(tiles) :]
+        sums, refs = (None, refs) if first else (refs[:3], refs[3:])
+        spots = [pl.ds(pl.multiple_of((place[0] ^ r) * columns, 128), columns) for r in offsets]
+        squares = [jnp.sum(x[pl.ds(columns, 16), :].astype(jnp.float32), axis=0, keepdims=True) for x in xs]
+        squares = sum(squares[1:], squares[0])
+        if not first:
+            squares = squares + sums[2][pl.ds(0, 1), :]
+        scale = lax.rsqrt(squares / D + EPS) if last else None
+        for i, tile in enumerate(tiles):
+            rows = pl.ds(sum(tiles[:i]), tile)
+            products = []
+            for j, weight in enumerate(weights):
+                total = None if first else sums[j][rows, :]
+                for x, at in zip(xs, spots):
+                    part = jnp.dot(weight[i][:, at], x[pl.ds(0, columns), :], preferred_element_type=jnp.float32)
+                    total = part if total is None else total + part
+                products.append(total)
+            if last:
+                gate, up = products[0] * scale, products[1] * scale
+                refs[1][rows, :] = gate / (1.0 + jnp.exp(-gate)) * up
+            else:
+                refs[0][rows, :], refs[1][rows, :] = products
+        if last:
+            refs[0][...] = refs[1][...].T.astype(jnp.bfloat16)
+        else:
+            refs[2][...] = jnp.broadcast_to(squares, refs[2].shape)
+
+    return body
+
+
+def down_body(offsets, columns, tiles):
+    def body(place, hidden, *refs):
+        weights, outs = refs[: len(tiles)], refs[len(tiles) :]
+        for r, out in zip(offsets, outs):
+            at = pl.ds(pl.multiple_of((place[0] ^ r) * columns, 128), columns)
+            total = None
+            for i, tile in enumerate(tiles):
+                part = jnp.dot(hidden[:, sum(tiles[:i]) : sum(tiles[: i + 1])], weights[i][:, at], preferred_element_type=jnp.float32)
+                total = part if total is None else total + part
+            out[...] = total.astype(out.dtype)
+
+    return body
+
+
+def add_body(mine, got, out):
+    out[...] = (mine[...].astype(jnp.float32) + got[...].astype(jnp.float32)).astype(out.dtype)
+
+
+def finish_body(carried, mine, *refs):
+    total = mine[...]
+    for got in refs[:-1]:
+        total = total + got[...].astype(jnp.float32)
+    refs[-1][...] = (carried[...] + total.T).astype(jnp.bfloat16)
+
+
+def exchanged(queries, keys, values, block_order, wo, resid, gain, w_gate, w_up, w_down):
+    f32, bf16 = jnp.float32, jnp.bfloat16
+    seq_dev, heads_features = queries.shape
+    n_seq, reps = lax.axis_size("seq"), lax.axis_size("rep")
+    groups = lax.axis_size("section") * reps
+    tokens = n_seq * seq_dev
+    group_tokens = tokens // groups
+    columns = wo.shape[1]
+    units = w_gate.shape[0]
+    place = jnp.stack([lax.axis_index(a).astype(jnp.int32) for a in ("seq", "section", "rep")])
+    place = jnp.concatenate([place, block_order])
+
+    blocks = gather(fetch([queries, keys, values], [3 * seq_dev])[0], n_seq)
+    tile = row_tile(units)
+    tiles = [tile] * (units // tile)
+    w_gate, w_up, w_down = (fetch([w], tiles) for w in (w_gate, w_up, w_down))
+    send, keep = call(
+        attend_body(n_seq, seq_dev, heads_features // HEAD_DIM, groups, reps),
+        (struct((columns, tokens // 2), bf16), struct((columns, tokens // 2), f32)),
+        (place, *blocks, wo.T),
+        scalars=1,
+        scratch=[pltpu.VMEM((tokens, heads_features), bf16)],
+        limit=7,
+        flops=6 * 10**9,
+    )
+    got = lax.ppermute(send, "rep", [(0, 1), (1, 0)])
+    send, rest = call(
+        halve_body, (struct((columns, group_tokens), bf16), struct((columns, group_tokens), f32)), (keep, got), limit=3
+    )
+    got = lax.ppermute(send, "section", [(0, 1), (1, 0)])
+    gain_wide = jnp.broadcast_to(gain.astype(f32)[:, None], (columns, group_tokens))
+    carried, x = call(
+        carry_body,
+        (struct((columns, group_tokens), f32), struct((columns + 16, group_tokens), bf16)),
+        (rest, got, resid.reshape(columns, group_tokens), gain_wide),
+        limit=3,
+    )
+    xs = gather(x, n_seq)
+    acc = ()
+    shares = ((0, 1, 2), (3, 4), (6, 5), (7,))
+    for i, share in enumerate(shares):
+        last = i == len(shares) - 1
+        n = len(share)
+        if last:
+            outs = struct((group_tokens, units), bf16)
+        else:
+            outs = (struct((units, group_tokens), f32),) * 2 + (struct((8, group_tokens), f32),)
+        acc = call(
+            gate_body(share, columns, tiles, i == 0, last),
+            outs,
+            (place, *(xs[r] for r in share), *w_gate, *w_up, *acc),
+            scalars=1,
+            scratch=[pltpu.VMEM((units, group_tokens), f32)] if last else [],
+            limit=4,
+            flops=4 * units * columns * group_tokens * n,
+            aliases={} if last or i == 0 else {1 + n + 2 * len(tiles) + j: j for j in range(3)},
+        )
+    hidden = acc
+
+    def down(*offsets_types):
+        return call(
+            down_body([r for r, _ in offsets_types], columns, tiles),
+            tuple(struct((group_tokens, columns), t) for _, t in offsets_types),
+            (place, hidden, *w_down),
+            scalars=1,
+            limit=3,
+            flops=2 * units * columns * group_tokens * len(offsets_types),
+        )
+
+    def plus(mine, got):
+        return call(add_body, struct((group_tokens, columns), bf16), (mine, got), limit=3)
+
+    own, far = {}, {}
+    far[6], = down((7, bf16))
+    own[6], far[4] = down((6, f32), (5, bf16))
+    own[4], far[2] = down((4, f32), (3, bf16))
+    own[2], far[0], own[0] = down((2, f32), (1, bf16), (0, f32))
+    got = {r: swap(far[r], 1, n_seq) for r in (6, 4, 2, 0)}
+    sums = {6: plus(own[6], got[6])}
+    onward = swap(sums[6], 2, n_seq)
+    sums[2] = plus(own[2], got[2])
+    sums[4] = plus(plus(own[4], got[4]), onward)
+    parts = [got[0], swap(sums[2], 2, n_seq), swap(sums[4], 4, n_seq)]
+    out = call(finish_body, struct((columns, group_tokens), bf16), (carried, own[0], *parts), limit=3)
+    return out.reshape(resid.shape)
+
+
+def on_device(queries, keys, values, block_order, wo, resid, gain, w_gate, w_up, w_down):
+    groups = lax.axis_size("section") * lax.axis_size("rep")
+    n_seq = lax.axis_size("seq")
+    fits = (
+        n_seq == 8
+        and groups == 4
+        and lax.axis_size("rep") == 2
+        and wo.shape[1] % 128 == 0
+        and (queries.shape[0] // groups) % 16 == 0
+        and (queries.shape[0] * n_seq // groups) % 128 == 0
+    )
+    form = exchanged if fits else gathered
+    return form(queries, keys, values, block_order, wo, resid, gain, w_gate, w_up, w_down)
+
+
 def solution(mesh):
     return jax.shard_map(
         on_device,

time: 289 us -> 114 us (0.39)
  blocking collectives: 119 us -> 0 us
  waiting for transfers between devices: 113 us -> 34.9 us
  Pallas kernels: 0 us -> 44.8 us
  matrix products: 35.1 us -> 0 us
  starting transfers between devices: 3.38 us -> 31.4 us
  between operations: 13.3 us -> 0.22 us
    all_gather x3 -> x0, blocking collectives: 97.2 us -> none  [the longest x1 33.6 us: on_device(): key_piece = lax.all_gather(keys, 'seq', axis=0, tiled=True)]
    reduce_scatter x1 -> x0, waiting for transfers between devices: 69.7 us -> none  [on_device(): down = lax.psum_scatter(term, 'seq', scatter_dimension=0, tiled=True)]
    pallas_call x0 -> x20, Pallas kernels: none -> 44.8 us  [the longest x16 25.5 us: call(): pl.pallas_call(body, out_shape=outs, in_specs=spaces, out_specs=jax.tree....]
    all_gather x2 -> x0, waiting for transfers between devices: 38.9 us -> none  [the longest x1 38.9 us: on_device(): piece = lax.all_gather(normed, 'seq', axis=0, tiled=True)]
    dot_general x5 -> x0, matrix products: 35.1 us -> none  [the longest x1 20.6 us: on_device(): lax.dot_general(w_down, hidden, (((0,), (0,)), ((), ())), preferred_eleme...]
    ppermute x0 -> x23, waiting for transfers between devices: none -> 34.9 us  [the longest x21 33.2 us: swap(): return lax.ppermute(x, 'seq', [(i, i ^ offset) for i in range(n_seq)])]
    ppermute x0 -> x23, starting transfers between devices: none -> 31.4 us  [the longest x21 29.8 us: swap(): return lax.ppermute(x, 'seq', [(i, i ^ offset) for i in range(n_seq)])]
    psum x1 -> x0, blocking collectives: 21.5 us -> none  [on_device(): squares = lax.psum(jnp.sum(carried * carried, axis=0), 'seq')]
  transfers between devices with their start and end apart: 4 -> 23, of which waited for: 3 -> 9; matrix products, arithmetic and copies ran while one was open for 1% -> 2% of each run, Pallas kernels for 0% -> 31%
where the time goes in v1:
time: 114 us
  Pallas kernels  44.8 us (39%)
  waiting for transfers between devices  34.9 us (31%)
  starting transfers between devices  31.4 us (28%)
  local copies, waits for them, and re-layouts  1.98 us (2%)
    ppermute x21, waiting for transfers between devices, swap(): return lax.ppermute(x, 'seq', [(i, i ^ offset) for i in range(n_seq)])  33.2 us
    ppermute x21, starting transfers between devices, swap(): return lax.ppermute(x, 'seq', [(i, i ^ offset) for i in range(n_seq)])  29.8 us
    pallas_call x16, Pallas kernels, call(): pl.pallas_call(body, out_shape=outs, in_specs=spaces, out_specs=jax.tree....  25.5 us
    pallas_call x4, Pallas kernels, fetch(): pl.pallas_call(body, out_shape=[pltpu.VMEM((rows, width), dtype) for rows...  19.3 us
  transfers between devices with their start and end apart: 23, of which 9 were waited for; matrix products, arithmetic and copies ran while one was open for 2% of the time, Pallas kernels for 31%

profile of v1, /device:TPU:0, one launch (start us, length us, event | category | flops | bytes accessed | tf_op | source)
XLA Modules:
  0.0 114.0 jit_solution(907875070489682925)
XLA Ops:
  1.0 4.1 %collective-permute-start.3 = (bf16[192,640]{1,0:T(8,128)(2,1)S(1)}, bf16[192,640]{1,0:T(8,128)(2,1)S(1)}, u32[]{:S(2)}, u32[]{:S(2)}) collective-permute-start(bf16[192,640]{1,0:T(8,128)(2,1)S(1)} %shard_map.100.refs_0_), channel_id=1, source_target_pairs={{0,8},{2,10},{4,12},{6,14},{8,0},{10,2},{12,4},{14,6},{1,9},{3,11}... | collective-permute-start | bytes 737288 | tf_op jit(solution)/shard_map/ppermute | solution.py:115
  5.1 1.6 %collective-permute-start.1 = (bf16[192,640]{1,0:T(8,128)(2,1)S(1)}, bf16[192,640]{1,0:T(8,128)(2,1)S(1)}, u32[]{:S(2)}, u32[]{:S(2)}) collective-permute-start(bf16[192,640]{1,0:T(8,128)(2,1)S(1)} %shard_map.100.refs_0_), channel_id=1, source_target_pairs={{0,4},{2,6},{4,0},{6,2},{8,12},{10,14},{12,8},{14,10},{1,5},{3,7},... | collective-permute-start | bytes 737288 | tf_op jit(solution)/shard_map/ppermute | solution.py:115
  6.7 9.7 %collective-permute-done.3.refs_4_ = bf16[192,640]{1,0:T(8,128)(2,1)S(1)} collective-permute-done((bf16[192,640]{1,0:T(8,128)(2,1)S(1)}, bf16[192,640]{1,0:T(8,128)(2,1)S(1)}, u32[]{:S(2)}, u32[]{:S(2)}) %collective-permute-start.3) | collective-permute-done | bytes 245792 | tf_op jit(solution)/shard_map/ppermute | solution.py:115
  20.6 2.9 %collective-permute-done.5.refs_6_ = bf16[192,640]{1,0:T(8,128)(2,1)S(1)} collective-permute-done((bf16[192,640]{1,0:T(8,128)(2,1)S(1)}, bf16[192,640]{1,0:T(8,128)(2,1)S(1)}, u32[]{:S(2)}, u32[]{:S(2)}) %collective-permute-start.5) | collective-permute-done | bytes 245792 | tf_op jit(solution)/shard_map/ppermute | solution.py:115
  24.8 1.8 %copy.17 = bf16[640,640]{0,1:T(8,128)(2,1)S(1)} copy(bf16[640,640]{1,0:T(8,128)(2,1)} %param.14) | data formatting | bytes 1638400 | tf_op args[4]
  27.4 3.8 %collective-permute-done.4.refs_5_ = bf16[192,640]{1,0:T(8,128)(2,1)S(1)} collective-permute-done((bf16[192,640]{1,0:T(8,128)(2,1)S(1)}, bf16[192,640]{1,0:T(8,128)(2,1)S(1)}, u32[]{:S(2)}, u32[]{:S(2)}) %collective-permute-start.4) | collective-permute-done | bytes 245792 | tf_op jit(solution)/shard_map/ppermute | solution.py:115
  31.2 5.3 %collective-permute-done.2.refs_3_ = bf16[192,640]{1,0:T(8,128)(2,1)S(1)} collective-permute-done((bf16[192,640]{1,0:T(8,128)(2,1)S(1)}, bf16[192,640]{1,0:T(8,128)(2,1)S(1)}, u32[]{:S(2)}, u32[]{:S(2)}) %collective-permute-start.2) | collective-permute-done | bytes 245792 | tf_op jit(solution)/shard_map/ppermute | solution.py:115
  36.4 4.0 %collective-permute-done.6.refs_7_ = bf16[192,640]{1,0:T(8,128)(2,1)S(1)} collective-permute-done((bf16[192,640]{1,0:T(8,128)(2,1)S(1)}, bf16[192,640]{1,0:T(8,128)(2,1)S(1)}, u32[]{:S(2)}, u32[]{:S(2)}) %collective-permute-start.6) | collective-permute-done | bytes 245792 | tf_op jit(solution)/shard_map/ppermute | solution.py:115
  40.5 3.7 %shard_map.101 = (bf16[640,256]{1,0:T(8,128)(2,1)S(1)}, f32[640,256]{1,0:T(8,128)S(1)}) custom-call(s32[19]{0:T(128)S(1)} %pad_add_fusion.place, bf16[192,640]{1,0:T(8,128)(2,1)S(1)} %shard_map.100.refs_0_, bf16[192,640]{1,0:T(8,128)(2,1)S(1)} %collective-permute-done.refs_1_, bf16[192,640]{1,0:T(8,128)(2,1)S(1)} %collective-permute-done.1.refs_2_, ...), custom_call_target="tpu_custom_call" | custom-call | flops 6000000000 | tf_op jit(solution)/shard_map/pallas_call | solution.py:98
  44.2 1.6 %collective-permute-done.7.got = bf16[640,256]{1,0:T(8,128)(2,1)S(1)} collective-permute-done((bf16[640,256]{1,0:T(8,128)(2,1)S(1)}, bf16[640,256]{1,0:T(8,128)(2,1)S(1)}, u32[]{:S(2)}, u32[]{:S(2)}) %collective-permute-start.7) | collective-permute-done | bytes 327712 | tf_op jit(solution)/shard_map/ppermute | solution.py:316
  45.9 1.6 %collective-permute-start.8 = (bf16[640,128]{1,0:T(8,128)(2,1)S(1)}, bf16[640,128]{1,0:T(8,128)(2,1)S(1)}, u32[]{:S(2)}, u32[]{:S(2)}) collective-permute-start(bf16[640,128]{1,0:T(8,128)(2,1)S(1)} %get-tuple-element.39), channel_id=1, source_target_pairs={{0,16},{16,0},{1,17},{17,1},{2,18},{18,2},{3,19},{19,3},{4,20},{20... | collective-permute-start | bytes 491528 | tf_op jit(solution)/shard_map/ppermute | solution.py:320
  47.5 6.1 %shard_map.104 = (bf16[576,5120]{1,0:T(8,128)(2,1)S(1)}, bf16[576,5120]{1,0:T(8,128)(2,1)S(1)}, bf16[576,5120]{1,0:T(8,128)(2,1)S(1)}) custom-call(bf16[1728,5120]{1,0:T(8,128)(2,1)} %refs_0_.5), custom_call_target="tpu_custom_call" | custom-call | flops 5308416000 | bytes 17694720 | tf_op jit(solution)/shard_map/pallas_call | solution.py:148
  54.3 3.3 %collective-permute-start.9 = (bf16[656,128]{1,0:T(8,128)(2,1)S(1)}, bf16[656,128]{1,0:T(8,128)(2,1)S(1)}, u32[]{:S(2)}, u32[]{:S(2)}) collective-permute-start(bf16[656,128]{1,0:T(8,128)(2,1)S(1)} %get-tuple-element.41.refs_0_), channel_id=1, source_target_pairs={{0,8},{2,10},{4,12},{6,14},{8,0},{10,2},{12,4},{14,6},{1,9},{3,11}... | collective-permute-start | bytes 503816 | tf_op jit(solution)/shard_map/ppermute | solution.py:115
  57.6 6.1 %shard_map.105 = (bf16[576,5120]{1,0:T(8,128)(2,1)S(1)}, bf16[576,5120]{1,0:T(8,128)(2,1)S(1)}, bf16[576,5120]{1,0:T(8,128)(2,1)S(1)}) custom-call(bf16[1728,5120]{1,0:T(8,128)(2,1)} %refs_0_.6), custom_call_target="tpu_custom_call" | custom-call | flops 5308416000 | bytes 17694720 | tf_op jit(solution)/shard_map/pallas_call | solution.py:148
  63.7 1.6 %collective-permute-start.15 = (bf16[656,128]{1,0:T(8,128)(2,1)S(1)}, bf16[656,128]{1,0:T(8,128)(2,1)S(1)}, u32[]{:S(2)}, u32[]{:S(2)}) collective-permute-start(bf16[656,128]{1,0:T(8,128)(2,1)S(1)} %get-tuple-element.41.refs_0_), channel_id=1, source_target_pairs={{0,2},{2,0},{4,6},{6,4},{8,10},{10,8},{12,14},{14,12},{1,3},{3,1},... | collective-permute-start | bytes 503816 | tf_op jit(solution)/shard_map/ppermute | solution.py:115
  65.8 1.7 %collective-permute-start.10 = (bf16[656,128]{1,0:T(8,128)(2,1)S(1)}, bf16[656,128]{1,0:T(8,128)(2,1)S(1)}, u32[]{:S(2)}, u32[]{:S(2)}) collective-permute-start(bf16[656,128]{1,0:T(8,128)(2,1)S(1)} %collective-permute-done.9.refs_1_), channel_id=1, source_target_pairs={{0,4},{2,6},{4,0},{6,2},{8,12},{10,14},{12,8},{14,10},{1,5},{3,7},... | collective-permute-start | bytes 503816 | tf_op jit(solution)/shard_map/ppermute | solution.py:115
  67.6 6.1 %shard_map.110 = (bf16[576,5120]{1,0:T(8,128)(2,1)S(1)}, bf16[576,5120]{1,0:T(8,128)(2,1)S(1)}, bf16[576,5120]{1,0:T(8,128)(2,1)S(1)}) custom-call(bf16[1728,5120]{1,0:T(8,128)(2,1)} %refs_0_.7), custom_call_target="tpu_custom_call" | custom-call | flops 5308416000 | bytes 17694720 | tf_op jit(solution)/shard_map/pallas_call | solution.py:148
  73.7 1.6 %collective-permute-start.12 = (bf16[656,128]{1,0:T(8,128)(2,1)S(1)}, bf16[656,128]{1,0:T(8,128)(2,1)S(1)}, u32[]{:S(2)}, u32[]{:S(2)}) collective-permute-start(bf16[656,128]{1,0:T(8,128)(2,1)S(1)} %collective-permute-done.9.refs_1_), channel_id=1, source_target_pairs={{0,2},{2,0},{4,6},{6,4},{8,10},{10,8},{12,14},{14,12},{1,3},{3,1},... | collective-permute-start | bytes 503816 | tf_op jit(solution)/shard_map/ppermute | solution.py:115
  75.3 4.3 %shard_map.106 = (f32[1728,128]{1,0:T(8,128)S(1)}, f32[1728,128]{1,0:T(8,128)S(1)}, f32[8,128]{1,0:T(8,128)S(1)}) custom-call(s32[19]{0:T(128)S(1)} %pad_add_fusion.place, bf16[656,128]{1,0:T(8,128)(2,1)S(1)} %get-tuple-element.41.refs_0_, bf16[656,128]{1,0:T(8,128)(2,1)S(1)} %collective-permute-done.15.refs_1_, ...), custom_call_target="tpu_custom_call" | custom-call | flops 1698693120 | tf_op jit(solution)/shard_map/pallas_call | solution.py:98
  80.1 3.6 %shard_map.107 = (f32[1728,128]{1,0:T(8,128)S(1)}, f32[1728,128]{1,0:T(8,128)S(1)}, f32[8,128]{1,0:T(8,128)S(1)}) custom-call(s32[19]{0:T(128)S(1)} %pad_add_fusion.place, bf16[656,128]{1,0:T(8,128)(2,1)S(1)} %collective-permute-done.14.refs_0_, ...), custom_call_target="tpu_custom_call", output_to_operand_aliasing={{0}: (9, {}), {1}: (10, {}), {2}: (11, {})} | custom-call | flops 1132462080 | tf_op jit(solution)/shard_map/pallas_call | solution.py:98
  83.8 3.8 %shard_map.108 = (f32[1728,128]{1,0:T(8,128)S(1)}, f32[1728,128]{1,0:T(8,128)S(1)}, f32[8,128]{1,0:T(8,128)S(1)}) custom-call(s32[19]{0:T(128)S(1)} %pad_add_fusion.place, bf16[656,128]{1,0:T(8,128)(2,1)S(1)} %collective-permute-done.10.refs_0_, ...), custom_call_target="tpu_custom_call", output_to_operand_aliasing={{0}: (9, {}), {1}: (10, {}), {2}: (11, {})} | custom-call | flops 1132462080 | tf_op jit(solution)/shard_map/pallas_call | solution.py:98
  87.6 2.1 %shard_map.109.hidden = bf16[128,1728]{1,0:T(8,128)(2,1)S(1)} custom-call(s32[19]{0:T(128)S(1)} %pad_add_fusion.place, bf16[656,128]{1,0:T(8,128)(2,1)S(1)} %collective-permute-done.11.refs_0_, bf16[576,5120]{1,0:T(8,128)(2,1)S(1)} %get-tuple-element.42.refs_3_.refs_2_.refs_1_, bf16[576,5120]{1,0:T(8,128)(2,1)S(1)} %get-tuple-element.43.refs_4_.refs_3_.refs_2_, ...), custom_call_target="tpu_custom_call" | custom-call | flops 566231040 | tf_op jit(solution)/shard_map/pallas_call | solution.py:98
  90.9 1.6 %collective-permute-start.20 = (bf16[128,640]{1,0:T(8,128)(2,1)S(1)}, bf16[128,640]{1,0:T(8,128)(2,1)S(1)}, u32[]{:S(2)}, u32[]{:S(2)}) collective-permute-start(bf16[128,640]{1,0:T(8,128)(2,1)S(1)} %shard_map.116), channel_id=1, source_target_pairs={{0,2},{2,0},{4,6},{6,4},{8,10},{10,8},{12,14},{14,12},{1,3},{3,1},... | collective-permute-start | bytes 491528 | tf_op jit(solution)/shard_map/ppermute | solution.py:115
  92.5 1.7 %shard_map.112 = (f32[128,640]{1,0:T(8,128)S(1)}, bf16[128,640]{1,0:T(8,128)(2,1)S(1)}) custom-call(s32[19]{0:T(128)S(1)} %pad_add_fusion.place, bf16[128,1728]{1,0:T(8,128)(2,1)S(1)} %shard_map.109.hidden, bf16[576,5120]{1,0:T(8,128)(2,1)S(1)} %get-tuple-element.57.refs_0_, bf16[576,5120]{1,0:T(8,128)(2,1)S(1)} %get-tuple-element.58.refs_1_, ...), custom_call_target="tpu_custom_call" | custom-call | flops 566231040 | tf_op jit(solution)/shard_map/pallas_call | solution.py:98
  94.8 1.7 %shard_map.114 = (f32[128,640]{1,0:T(8,128)S(1)}, bf16[128,640]{1,0:T(8,128)(2,1)S(1)}) custom-call(s32[19]{0:T(128)S(1)} %pad_add_fusion.place, bf16[128,1728]{1,0:T(8,128)(2,1)S(1)} %shard_map.109.hidden, bf16[576,5120]{1,0:T(8,128)(2,1)S(1)} %get-tuple-element.57.refs_0_, bf16[576,5120]{1,0:T(8,128)(2,1)S(1)} %get-tuple-element.58.refs_1_, ...), custom_call_target="tpu_custom_call" | custom-call | flops 566231040 | tf_op jit(solution)/shard_map/pallas_call | solution.py:98
  96.5 1.7 %collective-permute-start.19 = (bf16[128,640]{1,0:T(8,128)(2,1)S(1)}, bf16[128,640]{1,0:T(8,128)(2,1)S(1)}, u32[]{:S(2)}, u32[]{:S(2)}) collective-permute-start(bf16[128,640]{1,0:T(8,128)(2,1)S(1)} %get-tuple-element.65), channel_id=1, source_target_pairs={{0,2},{2,0},{4,6},{6,4},{8,10},{10,8},{12,14},{14,12},{1,3},{3,1},... | collective-permute-start | bytes 491528 | tf_op jit(solution)/shard_map/ppermute | solution.py:115
  98.5 2.2 %shard_map.111 = (f32[128,640]{1,0:T(8,128)S(1)}, bf16[128,640]{1,0:T(8,128)(2,1)S(1)}, f32[128,640]{1,0:T(8,128)S(1)}) custom-call(s32[19]{0:T(128)S(1)} %pad_add_fusion.place, bf16[128,1728]{1,0:T(8,128)(2,1)S(1)} %shard_map.109.hidden, bf16[576,5120]{1,0:T(8,128)(2,1)S(1)} %get-tuple-element.57.refs_0_, bf16[576,5120]{1,0:T(8,128)(2,1)S(1)} %get-tuple-element.58.refs_1_, ...), custom_call_target="tpu_custom_call" | custom-call | flops 849346560 | tf_op jit(solution)/shard_map/pallas_call | solution.py:98
  101.8 1.6 %collective-permute-start.18 = (bf16[128,640]{1,0:T(8,128)(2,1)S(1)}, bf16[128,640]{1,0:T(8,128)(2,1)S(1)}, u32[]{:S(2)}, u32[]{:S(2)}) collective-permute-start(bf16[128,640]{1,0:T(8,128)(2,1)S(1)} %shard_map.113), channel_id=1, source_target_pairs={{0,4},{2,6},{4,0},{6,2},{8,12},{10,14},{12,8},{14,10},{1,5},{3,7},... | collective-permute-start | bytes 491528 | tf_op jit(solution)/shard_map/ppermute | solution.py:115
  103.4 1.6 %collective-permute-done.19.got = bf16[128,640]{1,0:T(8,128)(2,1)S(1)} collective-permute-done((bf16[128,640]{1,0:T(8,128)(2,1)S(1)}, bf16[128,640]{1,0:T(8,128)(2,1)S(1)}, u32[]{:S(2)}, u32[]{:S(2)}) %collective-permute-start.19) | collective-permute-done | bytes 163872 | tf_op jit(solution)/shard_map/ppermute | solution.py:115
  105.2 2.2 %collective-permute-start.22 = (bf16[128,640]{1,0:T(8,128)(2,1)S(1)}, bf16[128,640]{1,0:T(8,128)(2,1)S(1)}, u32[]{:S(2)}, u32[]{:S(2)}) collective-permute-start(bf16[128,640]{1,0:T(8,128)(2,1)S(1)} %shard_map.118), channel_id=1, source_target_pairs={{0,8},{2,10},{4,12},{6,14},{8,0},{10,2},{12,4},{14,6},{1,9},{3,11}... | collective-permute-start | bytes 491528 | tf_op jit(solution)/shard_map/ppermute | solution.py:115
  107.3 1.6 %collective-permute-done.18.refs_1_ = bf16[128,640]{1,0:T(8,128)(2,1)S(1)} collective-permute-done((bf16[128,640]{1,0:T(8,128)(2,1)S(1)}, bf16[128,640]{1,0:T(8,128)(2,1)S(1)}, u32[]{:S(2)}, u32[]{:S(2)}) %collective-permute-start.18) | collective-permute-done | bytes 163872 | tf_op jit(solution)/shard_map/ppermute | solution.py:115
  108.9 4.3 %collective-permute-done.22.refs_2_ = bf16[128,640]{1,0:T(8,128)(2,1)S(1)} collective-permute-done((bf16[128,640]{1,0:T(8,128)(2,1)S(1)}, bf16[128,640]{1,0:T(8,128)(2,1)S(1)}, u32[]{:S(2)}, u32[]{:S(2)}) %collective-permute-start.22) | collective-permute-done | bytes 163872 | tf_op jit(solution)/shard_map/ppermute | solution.py:115
  (41 shorter events, 13.2 us)
Async XLA Ops:
  1.0 15.5 %collective-permute-start.3 = (bf16[192,640]{1,0:T(8,128)(2,1)S(1)}, bf16[192,640]{1,0:T(8,128)(2,1)S(1)}, u32[]{:S(2)}, u32[]{:S(2)}) collective-permute-start(bf16[192,640]{1,0:T(8,128)(2,1)S(1)} %shard_map.100.refs_0_), channel_id=1, source_target_pairs={{0,8},{2,10},{4,12},{6,14},{8,0},{10,2},{12,4},{14,6},{1,9},{3,11}... | collective-permute-start | bytes 737288 | tf_op jit(solution)/shard_map/ppermute | solution.py:115
  5.1 14.0 %collective-permute-start.1 = (bf16[192,640]{1,0:T(8,128)(2,1)S(1)}, bf16[192,640]{1,0:T(8,128)(2,1)S(1)}, u32[]{:S(2)}, u32[]{:S(2)}) collective-permute-start(bf16[192,640]{1,0:T(8,128)(2,1)S(1)} %shard_map.100.refs_0_), channel_id=1, source_target_pairs={{0,4},{2,6},{4,0},{6,2},{8,12},{10,14},{12,8},{14,10},{1,5},{3,7},... | collective-permute-start | bytes 737288 | tf_op jit(solution)/shard_map/ppermute | solution.py:115
  16.5 7.1 %collective-permute-start.5 = (bf16[192,640]{1,0:T(8,128)(2,1)S(1)}, bf16[192,640]{1,0:T(8,128)(2,1)S(1)}, u32[]{:S(2)}, u32[]{:S(2)}) collective-permute-start(bf16[192,640]{1,0:T(8,128)(2,1)S(1)} %collective-permute-done.3.refs_4_), channel_id=1, source_target_pairs={{0,4},{2,6},{4,0},{6,2},{8,12},{10,14},{12,8},{14,10},{1,5},{3,7},... | collective-permute-start | bytes 737288 | tf_op jit(solution)/shard_map/ppermute | solution.py:115
  17.1 10.3 %collective-permute-start = (bf16[192,640]{1,0:T(8,128)(2,1)S(1)}, bf16[192,640]{1,0:T(8,128)(2,1)S(1)}, u32[]{:S(2)}, u32[]{:S(2)}) collective-permute-start(bf16[192,640]{1,0:T(8,128)(2,1)S(1)} %shard_map.100.refs_0_), channel_id=1, source_target_pairs={{0,2},{2,0},{4,6},{6,4},{8,10},{10,8},{12,14},{14,12},{1,3},{3,1},... | collective-permute-start | bytes 737288 | tf_op jit(solution)/shard_map/ppermute | solution.py:115
  18.6 12.6 %collective-permute-start.4 = (bf16[192,640]{1,0:T(8,128)(2,1)S(1)}, bf16[192,640]{1,0:T(8,128)(2,1)S(1)}, u32[]{:S(2)}, u32[]{:S(2)}) collective-permute-start(bf16[192,640]{1,0:T(8,128)(2,1)S(1)} %collective-permute-done.3.refs_4_), channel_id=1, source_target_pairs={{0,2},{2,0},{4,6},{6,4},{8,10},{10,8},{12,14},{14,12},{1,3},{3,1},... | collective-permute-start | bytes 737288 | tf_op jit(solution)/shard_map/ppermute | solution.py:115
  19.1 17.3 %collective-permute-start.2 = (bf16[192,640]{1,0:T(8,128)(2,1)S(1)}, bf16[192,640]{1,0:T(8,128)(2,1)S(1)}, u32[]{:S(2)}, u32[]{:S(2)}) collective-permute-start(bf16[192,640]{1,0:T(8,128)(2,1)S(1)} %collective-permute-done.1.refs_2_), channel_id=1, source_target_pairs={{0,2},{2,0},{4,6},{6,4},{8,10},{10,8},{12,14},{14,12},{1,3},{3,1},... | collective-permute-start | bytes 737288 | tf_op jit(solution)/shard_map/ppermute | solution.py:115
  23.5 17.0 %collective-permute-start.6 = (bf16[192,640]{1,0:T(8,128)(2,1)S(1)}, bf16[192,640]{1,0:T(8,128)(2,1)S(1)}, u32[]{:S(2)}, u32[]{:S(2)}) collective-permute-start(bf16[192,640]{1,0:T(8,128)(2,1)S(1)} %collective-permute-done.5.refs_6_), channel_id=1, source_target_pairs={{0,2},{2,0},{4,6},{6,4},{8,10},{10,8},{12,14},{14,12},{1,3},{3,1},... | collective-permute-start | bytes 737288 | tf_op jit(solution)/shard_map/ppermute | solution.py:115
  44.1 1.7 %collective-permute-start.7 = (bf16[640,256]{1,0:T(8,128)(2,1)S(1)}, bf16[640,256]{1,0:T(8,128)(2,1)S(1)}, u32[]{:S(2)}, u32[]{:S(2)}) collective-permute-start(bf16[640,256]{1,0:T(8,128)(2,1)S(1)} %get-tuple-element.37), channel_id=1, source_target_pairs={{0,1},{1,0},{2,3},{3,2},{4,5},{5,4},{6,7},{7,6},{8,9},{9,8},{10,11... | collective-permute-start | bytes 983048 | tf_op jit(solution)/shard_map/ppermute | solution.py:316
  45.9 7.7 %copy-start.1 = (bf16[640]{0:T(1024)(128)(2,1)S(1)}, bf16[640]{0:T(1024)(128)(2,1)}, u32[]{:S(2)}) copy-start(bf16[640]{0:T(1024)(128)(2,1)} %param.16) | copy-start | bytes 3844
  45.9 7.8 %copy-start = (bf16[1,640,128]{2,1,0:T(8,128)(2,1)S(1)}, bf16[1,640,128]{2,1,0:T(8,128)(2,1)}, u32[]{:S(2)}) copy-start(bf16[1,640,128]{2,1,0:T(8,128)(2,1)} %param.15) | copy-start | bytes 491524
  45.9 7.7 %collective-permute-start.8 = (bf16[640,128]{1,0:T(8,128)(2,1)S(1)}, bf16[640,128]{1,0:T(8,128)(2,1)S(1)}, u32[]{:S(2)}, u32[]{:S(2)}) collective-permute-start(bf16[640,128]{1,0:T(8,128)(2,1)S(1)} %get-tuple-element.39), channel_id=1, source_target_pairs={{0,16},{16,0},{1,17},{17,1},{2,18},{18,2},{3,19},{19,3},{4,20},{20... | collective-permute-start | bytes 491528 | tf_op jit(solution)/shard_map/ppermute | solution.py:320
  53.9 11.4 %collective-permute-start.13 = (bf16[656,128]{1,0:T(8,128)(2,1)S(1)}, bf16[656,128]{1,0:T(8,128)(2,1)S(1)}, u32[]{:S(2)}, u32[]{:S(2)}) collective-permute-start(bf16[656,128]{1,0:T(8,128)(2,1)S(1)} %get-tuple-element.41.refs_0_), channel_id=1, source_target_pairs={{0,4},{2,6},{4,0},{6,2},{8,12},{10,14},{12,8},{14,10},{1,5},{3,7},... | collective-permute-start | bytes 503816 | tf_op jit(solution)/shard_map/ppermute | solution.py:115
  54.3 11.5 %collective-permute-start.9 = (bf16[656,128]{1,0:T(8,128)(2,1)S(1)}, bf16[656,128]{1,0:T(8,128)(2,1)S(1)}, u32[]{:S(2)}, u32[]{:S(2)}) collective-permute-start(bf16[656,128]{1,0:T(8,128)(2,1)S(1)} %get-tuple-element.41.refs_0_), channel_id=1, source_target_pairs={{0,8},{2,10},{4,12},{6,14},{8,0},{10,2},{12,4},{14,6},{1,9},{3,11}... | collective-permute-start | bytes 503816 | tf_op jit(solution)/shard_map/ppermute | solution.py:115
  63.7 11.5 %collective-permute-start.15 = (bf16[656,128]{1,0:T(8,128)(2,1)S(1)}, bf16[656,128]{1,0:T(8,128)(2,1)S(1)}, u32[]{:S(2)}, u32[]{:S(2)}) collective-permute-start(bf16[656,128]{1,0:T(8,128)(2,1)S(1)} %get-tuple-element.41.refs_0_), channel_id=1, source_target_pairs={{0,2},{2,0},{4,6},{6,4},{8,10},{10,8},{12,14},{14,12},{1,3},{3,1},... | collective-permute-start | bytes 503816 | tf_op jit(solution)/shard_map/ppermute | solution.py:115
  65.3 14.8 %collective-permute-start.14 = (bf16[656,128]{1,0:T(8,128)(2,1)S(1)}, bf16[656,128]{1,0:T(8,128)(2,1)S(1)}, u32[]{:S(2)}, u32[]{:S(2)}) collective-permute-start(bf16[656,128]{1,0:T(8,128)(2,1)S(1)} %collective-permute-done.13.refs_2_), channel_id=1, source_target_pairs={{0,2},{2,0},{4,6},{6,4},{8,10},{10,8},{12,14},{14,12},{1,3},{3,1},... | collective-permute-start | bytes 503816 | tf_op jit(solution)/shard_map/ppermute | solution.py:115
  65.8 13.8 %collective-permute-start.10 = (bf16[656,128]{1,0:T(8,128)(2,1)S(1)}, bf16[656,128]{1,0:T(8,128)(2,1)S(1)}, u32[]{:S(2)}, u32[]{:S(2)}) collective-permute-start(bf16[656,128]{1,0:T(8,128)(2,1)S(1)} %collective-permute-done.9.refs_1_), channel_id=1, source_target_pairs={{0,4},{2,6},{4,0},{6,2},{8,12},{10,14},{12,8},{14,10},{1,5},{3,7},... | collective-permute-start | bytes 503816 | tf_op jit(solution)/shard_map/ppermute | solution.py:115
  73.7 10.1 %collective-permute-start.12 = (bf16[656,128]{1,0:T(8,128)(2,1)S(1)}, bf16[656,128]{1,0:T(8,128)(2,1)S(1)}, u32[]{:S(2)}, u32[]{:S(2)}) collective-permute-start(bf16[656,128]{1,0:T(8,128)(2,1)S(1)} %collective-permute-done.9.refs_1_), channel_id=1, source_target_pairs={{0,2},{2,0},{4,6},{6,4},{8,10},{10,8},{12,14},{14,12},{1,3},{3,1},... | collective-permute-start | bytes 503816 | tf_op jit(solution)/shard_map/ppermute | solution.py:115
  79.6 8.0 %collective-permute-start.11 = (bf16[656,128]{1,0:T(8,128)(2,1)S(1)}, bf16[656,128]{1,0:T(8,128)(2,1)S(1)}, u32[]{:S(2)}, u32[]{:S(2)}) collective-permute-start(bf16[656,128]{1,0:T(8,128)(2,1)S(1)} %collective-permute-done.10.refs_0_), channel_id=1, source_target_pairs={{0,2},{2,0},{4,6},{6,4},{8,10},{10,8},{12,14},{14,12},{1,3},{3,1},... | collective-permute-start | bytes 503816 | tf_op jit(solution)/shard_map/ppermute | solution.py:115
  90.9 7.3 %collective-permute-start.20 = (bf16[128,640]{1,0:T(8,128)(2,1)S(1)}, bf16[128,640]{1,0:T(8,128)(2,1)S(1)}, u32[]{:S(2)}, u32[]{:S(2)}) collective-permute-start(bf16[128,640]{1,0:T(8,128)(2,1)S(1)} %shard_map.116), channel_id=1, source_target_pairs={{0,2},{2,0},{4,6},{6,4},{8,10},{10,8},{12,14},{14,12},{1,3},{3,1},... | collective-permute-start | bytes 491528 | tf_op jit(solution)/shard_map/ppermute | solution.py:115
  94.3 7.5 %collective-permute-start.17 = (bf16[128,640]{1,0:T(8,128)(2,1)S(1)}, bf16[128,640]{1,0:T(8,128)(2,1)S(1)}, u32[]{:S(2)}, u32[]{:S(2)}) collective-permute-start(bf16[128,640]{1,0:T(8,128)(2,1)S(1)} %get-tuple-element.63), channel_id=1, source_target_pairs={{0,2},{2,0},{4,6},{6,4},{8,10},{10,8},{12,14},{14,12},{1,3},{3,1},... | collective-permute-start | bytes 491528 | tf_op jit(solution)/shard_map/ppermute | solution.py:115
  96.5 8.5 %collective-permute-start.19 = (bf16[128,640]{1,0:T(8,128)(2,1)S(1)}, bf16[128,640]{1,0:T(8,128)(2,1)S(1)}, u32[]{:S(2)}, u32[]{:S(2)}) collective-permute-start(bf16[128,640]{1,0:T(8,128)(2,1)S(1)} %get-tuple-element.65), channel_id=1, source_target_pairs={{0,2},{2,0},{4,6},{6,4},{8,10},{10,8},{12,14},{14,12},{1,3},{3,1},... | collective-permute-start | bytes 491528 | tf_op jit(solution)/shard_map/ppermute | solution.py:115
  98.2 6.8 %collective-permute-start.21 = (bf16[128,640]{1,0:T(8,128)(2,1)S(1)}, bf16[128,640]{1,0:T(8,128)(2,1)S(1)}, u32[]{:S(2)}, u32[]{:S(2)}) collective-permute-start(bf16[128,640]{1,0:T(8,128)(2,1)S(1)} %shard_map.117), channel_id=1, source_target_pairs={{0,4},{2,6},{4,0},{6,2},{8,12},{10,14},{12,8},{14,10},{1,5},{3,7},... | collective-permute-start | bytes 491528 | tf_op jit(solution)/shard_map/ppermute | solution.py:115
  100.7 6.6 %collective-permute-start.16 = (bf16[128,640]{1,0:T(8,128)(2,1)S(1)}, bf16[128,640]{1,0:T(8,128)(2,1)S(1)}, u32[]{:S(2)}, u32[]{:S(2)}) collective-permute-start(bf16[128,640]{1,0:T(8,128)(2,1)S(1)} %get-tuple-element.61), channel_id=1, source_target_pairs={{0,2},{2,0},{4,6},{6,4},{8,10},{10,8},{12,14},{14,12},{1,3},{3,1},... | collective-permute-start | bytes 491528 | tf_op jit(solution)/shard_map/ppermute | solution.py:115
  101.8 7.1 %collective-permute-start.18 = (bf16[128,640]{1,0:T(8,128)(2,1)S(1)}, bf16[128,640]{1,0:T(8,128)(2,1)S(1)}, u32[]{:S(2)}, u32[]{:S(2)}) collective-permute-start(bf16[128,640]{1,0:T(8,128)(2,1)S(1)} %shard_map.113), channel_id=1, source_target_pairs={{0,4},{2,6},{4,0},{6,2},{8,12},{10,14},{12,8},{14,10},{1,5},{3,7},... | collective-permute-start | bytes 491528 | tf_op jit(solution)/shard_map/ppermute | solution.py:115
  105.2 8.0 %collective-permute-start.22 = (bf16[128,640]{1,0:T(8,128)(2,1)S(1)}, bf16[128,640]{1,0:T(8,128)(2,1)S(1)}, u32[]{:S(2)}, u32[]{:S(2)}) collective-permute-start(bf16[128,640]{1,0:T(8,128)(2,1)S(1)} %shard_map.118), channel_id=1, source_target_pairs={{0,8},{2,10},{4,12},{6,14},{8,0},{10,2},{12,4},{14,6},{1,9},{3,11}... | collective-permute-start | bytes 491528 | tf_op jit(solution)/shard_map/ppermute | solution.py:115

commit v2 on v1

--- a/solution.py
+++ b/solution.py
@@ -1,5 +1,3 @@
-import math
-
 import jax
 import jax.numpy as jnp
 from jax import lax
@@ -7,12 +5,14 @@
 from jax.experimental.pallas import tpu as pltpu
 from jax.sharding import PartitionSpec as P
 
+
 D = 5120
 HEAD_DIM = 128
 EPS = 1e-05
 LOG2E = 1.4426950408889634
 MIB = 1 << 20
-FETCH_FLOPS = 300
+SEQ = 8
+SHARES = ((0, 1), (2, 4), (5, 6), (3, 7))
 VMEM = pl.BlockSpec(memory_space=pltpu.VMEM)
 HBM = pl.BlockSpec(memory_space=pltpu.MemorySpace.HBM)
 SMEM = pl.BlockSpec(memory_space=pltpu.SMEM)
@@ -91,7 +91,7 @@
     return (carried + down).astype(jnp.bfloat16).reshape(resid.shape)
 
 
-def call(body, outs, args, scalars=0, scratch=(), limit=7, flops=0, nbytes=0, aliases=None, in_place=()):
+def call(body, outs, args, scalars=0, scratch=(), limit=7, aliases=None, in_place=()):
     spaces = [SMEM] * scalars + [VMEM] * (len(args) - scalars)
     for i in in_place:
         spaces[i] = HBM
@@ -103,7 +103,7 @@
         scratch_shapes=list(scratch),
         input_output_aliases=aliases or {},
         compiler_params=pltpu.CompilerParams(vmem_limit_bytes=limit * MIB),
-        cost_estimate=pl.CostEstimate(flops=flops, bytes_accessed=nbytes, transcendentals=0),
+        cost_estimate=pl.CostEstimate(flops=0, bytes_accessed=0, transcendentals=0),
     )(*args)
 
 
@@ -116,10 +116,9 @@
 
 
 def gather(x, n_seq):
-    got = {4: swap(x, 4, n_seq), 2: swap(x, 2, n_seq), 1: swap(x, 1, n_seq)}
-    got[6] = swap(got[4], 2, n_seq)
-    for r in (2, 4, 6):
-        got[r + 1] = swap(got[r], 1, n_seq)
+    got = {r: swap(x, r, n_seq) for r in (4, 1, 2)}
+    for r, source, offset in ((5, 4, 1), (6, 4, 2), (3, 2, 1), (7, 5, 2)):
+        got[r] = swap(got[source], offset, n_seq)
     return [x] + [got[r] for r in range(1, n_seq)]
 
 
@@ -127,32 +126,50 @@
     return pltpu.with_memory_space_constraint(x, pltpu.MemorySpace.HBM)
 
 
-def fetch(arrays, outs):
-    def body(*refs):
-        ins, refs = refs[: len(arrays)], refs[len(arrays) :]
-        tiles, sems = refs[:-1], refs[-1]
-        rows_of = [(ref, k) for ref in ins for k in range(ref.shape[0] // step)]
-        spots = [(tile, k) for tile in tiles for k in range(tile.shape[0] // step)]
-        copies = [
-            pltpu.make_async_copy(a.at[pl.ds(i * step, step)], b.at[pl.ds(k * step, step)], sems.at[n])
-            for n, ((a, i), (b, k)) in enumerate(zip(rows_of, spots))
-        ]
+def fetch(place, arrays, rows, bases):
+    n, width = len(arrays), arrays[0].shape[1]
+
+    def body(place, *refs):
+        ins, out, sems = refs[:n], refs[n], refs[n + 1]
+        copies = []
+        for i, (source, base) in enumerate(zip(ins, bases)):
+            start = pl.multiple_of(base(place), 16)
+            copies.append(pltpu.make_async_copy(source.at[pl.ds(start, rows)], out.at[pl.ds(i * rows, rows)], sems.at[i]))
         for c in copies:
             c.start()
         for c in copies:
             c.wait()
 
-    step = math.gcd(*outs, *(a.shape[0] for a in arrays))
-    width, dtype = arrays[0].shape[1], arrays[0].dtype
-    nbytes = 2 * sum(outs) * width
     return pl.pallas_call(
         body,
-        out_shape=[pltpu.VMEM((rows, width), dtype) for rows in outs],
-        in_specs=[HBM] * len(arrays),
-        out_specs=[VMEM] * len(outs),
-        scratch_shapes=[pltpu.SemaphoreType.DMA((sum(outs) // step,))],
+        out_shape=pltpu.VMEM((n * rows, width), arrays[0].dtype),
+        in_specs=[SMEM] + [HBM] * n,
+        out_specs=VMEM,
+        scratch_shapes=[pltpu.SemaphoreType.DMA((n,))],
         compiler_params=pltpu.CompilerParams(vmem_limit_bytes=MIB),
-        cost_estimate=pl.CostEstimate(flops=FETCH_FLOPS * nbytes, bytes_accessed=nbytes, transcendentals=0),
+    )(place, *(in_hbm(a) for a in arrays))
+
+
+def stack(arrays):
+    rows, width = arrays[0].shape
+
+    def body(*refs):
+        ins, out, sems = refs[:-2], refs[-2], refs[-1]
+        copies = [pltpu.make_async_copy(ref, out.at[pl.ds(i * rows, rows)], sems.at[i]) for i, ref in enumerate(ins)]
+        for c in copies:
+            c.start()
+        for c in copies:
+            c.wait()
+
+    n = len(arrays)
+    return pl.pallas_call(
+        body,
+        name="stack",
+        out_shape=pltpu.VMEM((n * rows, width), arrays[0].dtype),
+        in_specs=[HBM] * n,
+        out_specs=VMEM,
+        scratch_shapes=[pltpu.SemaphoreType.DMA((n,))],
+        compiler_params=pltpu.CompilerParams(vmem_limit_bytes=MIB),
     )(*(in_hbm(a) for a in arrays))
 
 
@@ -224,57 +241,58 @@
     out[pl.ds(columns, 16), :] = both.astype(jnp.bfloat16)
 
 
-def row_tile(rows):
-    return max(t for t in range(16, 601, 16) if rows % t == 0)
-
-
-def gate_body(offsets, columns, tiles, first, last):
+def gate_body(offsets, columns, units, tile, first, last):
     n = len(offsets)
 
     def body(place, *refs):
-        xs, refs = refs[:n], refs[n:]
-        weights, refs = (refs[: len(tiles)], refs[len(tiles) : 2 * len(tiles)]), refs[2 * len(tiles) :]
+        pairs, weights, refs = list(zip(refs[:n], refs[n : 2 * n])), refs[2 * n], refs[2 * n + 1 :]
         sums, refs = (None, refs) if first else (refs[:3], refs[3:])
         spots = [pl.ds(pl.multiple_of((place[0] ^ r) * columns, 128), columns) for r in offsets]
-        squares = [jnp.sum(x[pl.ds(columns, 16), :].astype(jnp.float32), axis=0, keepdims=True) for x in xs]
-        squares = sum(squares[1:], squares[0])
+
+        def both(rows):
+            return [jnp.concatenate([own[rows, :], other[rows, :]], axis=1) for own, other in pairs]
+
+        squares = sum(jnp.sum(b.astype(jnp.float32), axis=0, keepdims=True) for b in both(pl.ds(columns, 16)))
         if not first:
             squares = squares + sums[2][pl.ds(0, 1), :]
         scale = lax.rsqrt(squares / D + EPS) if last else None
-        for i, tile in enumerate(tiles):
-            rows = pl.ds(sum(tiles[:i]), tile)
+        x = jnp.concatenate(both(pl.ds(0, columns)), axis=0)
+        for start in range(0, units, tile):
+            rows = pl.ds(start, tile)
             products = []
-            for j, weight in enumerate(weights):
-                total = None if first else sums[j][rows, :]
-                for x, at in zip(xs, spots):
-                    part = jnp.dot(weight[i][:, at], x[pl.ds(0, columns), :], preferred_element_type=jnp.float32)
-                    total = part if total is None else total + part
-                products.append(total)
+            for j in range(2):
+                weight = jnp.concatenate([weights[pl.ds(j * units + start, tile), at] for at in spots], axis=1)
+                part = jnp.dot(weight, x, preferred_element_type=jnp.float32)
+                products.append(part if first else part + sums[j][rows, :])
             if last:
                 gate, up = products[0] * scale, products[1] * scale
-                refs[1][rows, :] = gate / (1.0 + jnp.exp(-gate)) * up
+                refs[2][rows, :] = gate / (1.0 + jnp.exp(-gate)) * up
             else:
                 refs[0][rows, :], refs[1][rows, :] = products
         if last:
-            refs[0][...] = refs[1][...].T.astype(jnp.bfloat16)
+            tokens = x.shape[1] // 2
+            refs[0][...] = refs[2][:, :tokens].T.astype(jnp.bfloat16)
+            refs[1][...] = refs[2][:, tokens:].T.astype(jnp.bfloat16)
         else:
             refs[2][...] = jnp.broadcast_to(squares, refs[2].shape)
 
     return body
 
 
-def down_body(offsets, columns, tiles):
-    def body(place, hidden, *refs):
-        weights, outs = refs[: len(tiles)], refs[len(tiles) :]
+def down_body(offsets, columns):
+    def body(place, own, other, weights, *outs):
+        units = own.shape[1]
         for r, out in zip(offsets, outs):
             at = pl.ds(pl.multiple_of((place[0] ^ r) * columns, 128), columns)
-            total = None
-            for i, tile in enumerate(tiles):
-                part = jnp.dot(hidden[:, sum(tiles[:i]) : sum(tiles[: i + 1])], weights[i][:, at], preferred_element_type=jnp.float32)
-                total = part if total is None else total + part
+            total = jnp.dot(own[...], weights[pl.ds(0, units), at], preferred_element_type=jnp.float32)
+            total = total + jnp.dot(other[...], weights[pl.ds(units, units), at], preferred_element_type=jnp.float32)
             out[...] = total.astype(out.dtype)
 
     return body
+
+
+def turn_body(x, out):
+    out[...] = x[...].T
 
 
 def add_body(mine, got, out):
@@ -300,18 +318,19 @@
     place = jnp.stack([lax.axis_index(a).astype(jnp.int32) for a in ("seq", "section", "rep")])
     place = jnp.concatenate([place, block_order])
 
-    blocks = gather(fetch([queries, keys, values], [3 * seq_dev])[0], n_seq)
-    tile = row_tile(units)
-    tiles = [tile] * (units // tile)
-    w_gate, w_up, w_down = (fetch([w], tiles) for w in (w_gate, w_up, w_down))
+    share = units // reps
+    blocks = gather(stack([queries, keys, values]), n_seq)
+    mine, theirs = (lambda p: p[2] * share), (lambda p: (1 - p[2]) * share)
+    w_gate_up = fetch(place, [w_gate, w_up], share, (mine, mine))
+    w_down = fetch(place, [w_down, w_down], share, (mine, theirs))
+    wo_t = call(turn_body, struct(wo.shape[::-1], bf16), (wo,), limit=4)
     send, keep = call(
         attend_body(n_seq, seq_dev, heads_features // HEAD_DIM, groups, reps),
         (struct((columns, tokens // 2), bf16), struct((columns, tokens // 2), f32)),
-        (place, *blocks, wo.T),
+        (place, *blocks, wo_t),
         scalars=1,
         scratch=[pltpu.VMEM((tokens, heads_features), bf16)],
-        limit=7,
-        flops=6 * 10**9,
+        limit=8,
     )
     got = lax.ppermute(send, "rep", [(0, 1), (1, 0)])
     send, rest = call(
@@ -326,35 +345,36 @@
         limit=3,
     )
     xs = gather(x, n_seq)
-    acc = ()
-    shares = ((0, 1, 2), (3, 4), (6, 5), (7,))
-    for i, share in enumerate(shares):
-        last = i == len(shares) - 1
-        n = len(share)
+
+    def over_rep(x):
+        return lax.ppermute(x, "rep", [(0, 1), (1, 0)])
+
+    others = [over_rep(b) for b in xs]
+    acc, tile = (), max(t for t in range(16, 601, 16) if share % t == 0)
+    for i, offsets in enumerate(SHARES):
+        first, last, n = i == 0, i == len(SHARES) - 1, len(offsets)
         if last:
-            outs = struct((group_tokens, units), bf16)
+            outs = (struct((group_tokens, share), bf16),) * 2
         else:
-            outs = (struct((units, group_tokens), f32),) * 2 + (struct((8, group_tokens), f32),)
+            outs = (struct((share, 2 * group_tokens), f32),) * 2 + (struct((8, 2 * group_tokens), f32),)
         acc = call(
-            gate_body(share, columns, tiles, i == 0, last),
+            gate_body(offsets, columns, share, tile, first, last),
             outs,
-            (place, *(xs[r] for r in share), *w_gate, *w_up, *acc),
+            (place, *(xs[r] for r in offsets), *(others[r] for r in offsets), w_gate_up, *acc),
             scalars=1,
-            scratch=[pltpu.VMEM((units, group_tokens), f32)] if last else [],
-            limit=4,
-            flops=4 * units * columns * group_tokens * n,
-            aliases={} if last or i == 0 else {1 + n + 2 * len(tiles) + j: j for j in range(3)},
+            scratch=[pltpu.VMEM((share, 2 * group_tokens), f32)] if last else [],
+            limit=6,
+            aliases={} if first or last else {1 + 2 * n + 1 + j: j for j in range(3)},
         )
-    hidden = acc
+    hidden = (acc[0], over_rep(acc[1]))
 
     def down(*offsets_types):
         return call(
-            down_body([r for r, _ in offsets_types], columns, tiles),
+            down_body([r for r, _ in offsets_types], columns),
             tuple(struct((group_tokens, columns), t) for _, t in offsets_types),
-            (place, hidden, *w_down),
+            (place, *hidden, w_down),
             scalars=1,
             limit=3,
-            flops=2 * units * columns * group_tokens * len(offsets_types),
         )
 
     def plus(mine, got):
@@ -379,11 +399,12 @@
     groups = lax.axis_size("section") * lax.axis_size("rep")
     n_seq = lax.axis_size("seq")
     fits = (
-        n_seq == 8
+        n_seq == SEQ
         and groups == 4
         and lax.axis_size("rep") == 2
         and wo.shape[1] % 128 == 0
         and (queries.shape[0] // groups) % 16 == 0
+        and w_gate.shape[0] % 32 == 0
         and (queries.shape[0] * n_seq // groups) % 128 == 0
     )
     form = exchanged if fits else gathered

time: 114 us -> 117 us (1.026)
  waiting for transfers between devices: 34.9 us -> 46.6 us
  Pallas kernels: 44.8 us -> 33.5 us
    ppermute x21, waiting for transfers between devices: 33.2 us -> 40 us  [swap(): return lax.ppermute(x, 'seq', [(i, i ^ offset) for i in range(n_seq)])]
    pallas_call x16 -> x17, Pallas kernels: 25.5 us -> 19.3 us  [call(): pl.pallas_call(body, out_shape=outs, in_specs=spaces, out_specs=jax.tree....]
    pallas_call x4 -> x3, Pallas kernels: 19.3 us -> 14.2 us  [the longest x2 13.2 us: fetch(): pl.pallas_call(body, out_shape=pltpu.VMEM((n * rows, width), arrays[0].dt...]
    ppermute x1, waiting for transfers between devices: 0.01 us -> 4.95 us  [exchanged(): got = lax.ppermute(send, 'section', [(0, 1), (1, 0)])]
    ppermute x0 -> x9, starting transfers between devices: none -> 2.09 us  [over_rep(): return lax.ppermute(x, 'rep', [(0, 1), (1, 0)])]
  transfers between devices with their start and end apart: 23 -> 32, of which waited for: 9 -> 14; matrix products, arithmetic and copies ran while one was open for 2% -> 1% of each run, Pallas kernels for 31% -> 21%
where the time goes in v2:
time: 117 us; the launch traced here: 116 us
  waiting for transfers between devices  46.6 us (40%)
  Pallas kernels  33.5 us (29%)
  starting transfers between devices  32.5 us (28%)
  local copies, waits for them, and re-layouts  2.88 us (2%)
    ppermute x21, waiting for transfers between devices, swap(): return lax.ppermute(x, 'seq', [(i, i ^ offset) for i in range(n_seq)])  40 us
    ppermute x21, starting transfers between devices, swap(): return lax.ppermute(x, 'seq', [(i, i ^ offset) for i in range(n_seq)])  29 us
    pallas_call x17, Pallas kernels, call(): pl.pallas_call(body, out_shape=outs, in_specs=spaces, out_specs=jax.tree....  19.3 us
    pallas_call x2, Pallas kernels, fetch(): pl.pallas_call(body, out_shape=pltpu.VMEM((n * rows, width), arrays[0].dt...  13.2 us
    ppermute x1, waiting for transfers between devices, exchanged(): got = lax.ppermute(send, 'section', [(0, 1), (1, 0)])  4.95 us
  transfers between devices with their start and end apart: 32, of which 14 were waited for; matrix products, arithmetic and copies ran while one was open for 1% of the time, Pallas kernels for 21%

profile of v2, /device:TPU:0, one launch (start us, length us, event | category | flops | bytes accessed | tf_op | source)
XLA Modules:
  0.0 116.5 jit_solution(16407166943265967946)
XLA Ops:
  1.0 4.1 %collective-permute-start.3 = (bf16[192,640]{1,0:T(8,128)(2,1)S(1)}, bf16[192,640]{1,0:T(8,128)(2,1)S(1)}, u32[]{:S(2)}, u32[]{:S(2)}) collective-permute-start(bf16[192,640]{1,0:T(8,128)(2,1)S(1)} %stack.13.refs_0_), channel_id=1, source_target_pairs={{0,8},{2,10},{4,12},{6,14},{8,0},{10,2},{12,4},{14,6},{1,9},{3,11}... | collective-permute-start | bytes 737288 | tf_op jit(solution)/shard_map/ppermute | solution.py:115
  5.1 1.6 %collective-permute-start.1 = (bf16[192,640]{1,0:T(8,128)(2,1)S(1)}, bf16[192,640]{1,0:T(8,128)(2,1)S(1)}, u32[]{:S(2)}, u32[]{:S(2)}) collective-permute-start(bf16[192,640]{1,0:T(8,128)(2,1)S(1)} %stack.13.refs_0_), channel_id=1, source_target_pairs={{0,4},{2,6},{4,0},{6,2},{8,12},{10,14},{12,8},{14,10},{1,5},{3,7},... | collective-permute-start | bytes 737288 | tf_op jit(solution)/shard_map/ppermute | solution.py:115
  6.7 9.7 %collective-permute-done.3.refs_4_ = bf16[192,640]{1,0:T(8,128)(2,1)S(1)} collective-permute-done((bf16[192,640]{1,0:T(8,128)(2,1)S(1)}, bf16[192,640]{1,0:T(8,128)(2,1)S(1)}, u32[]{:S(2)}, u32[]{:S(2)}) %collective-permute-start.3) | collective-permute-done | bytes 245792 | tf_op jit(solution)/shard_map/ppermute | solution.py:115
  16.5 1.6 %collective-permute-start.4 = (bf16[192,640]{1,0:T(8,128)(2,1)S(1)}, bf16[192,640]{1,0:T(8,128)(2,1)S(1)}, u32[]{:S(2)}, u32[]{:S(2)}) collective-permute-start(bf16[192,640]{1,0:T(8,128)(2,1)S(1)} %collective-permute-done.3.refs_4_), channel_id=1, source_target_pairs={{0,2},{2,0},{4,6},{6,4},{8,10},{10,8},{12,14},{14,12},{1,3},{3,1},... | collective-permute-start | bytes 737288 | tf_op jit(solution)/shard_map/ppermute | solution.py:115
  19.1 1.5 %collective-permute-start.2 = (bf16[192,640]{1,0:T(8,128)(2,1)S(1)}, bf16[192,640]{1,0:T(8,128)(2,1)S(1)}, u32[]{:S(2)}, u32[]{:S(2)}) collective-permute-start(bf16[192,640]{1,0:T(8,128)(2,1)S(1)} %collective-permute-done.1.refs_2_), channel_id=1, source_target_pairs={{0,2},{2,0},{4,6},{6,4},{8,10},{10,8},{12,14},{14,12},{1,3},{3,1},... | collective-permute-start | bytes 737288 | tf_op jit(solution)/shard_map/ppermute | solution.py:115
  20.6 4.7 %collective-permute-done.4.refs_5_ = bf16[192,640]{1,0:T(8,128)(2,1)S(1)} collective-permute-done((bf16[192,640]{1,0:T(8,128)(2,1)S(1)}, bf16[192,640]{1,0:T(8,128)(2,1)S(1)}, u32[]{:S(2)}, u32[]{:S(2)}) %collective-permute-start.4) | collective-permute-done | bytes 245792 | tf_op jit(solution)/shard_map/ppermute | solution.py:115
  28.1 2.5 %collective-permute-done.refs_1_ = bf16[192,640]{1,0:T(8,128)(2,1)S(1)} collective-permute-done((bf16[192,640]{1,0:T(8,128)(2,1)S(1)}, bf16[192,640]{1,0:T(8,128)(2,1)S(1)}, u32[]{:S(2)}, u32[]{:S(2)}) %collective-permute-start) | collective-permute-done | bytes 245792 | tf_op jit(solution)/shard_map/ppermute | solution.py:115
  30.5 3.5 %collective-permute-done.2.refs_3_ = bf16[192,640]{1,0:T(8,128)(2,1)S(1)} collective-permute-done((bf16[192,640]{1,0:T(8,128)(2,1)S(1)}, bf16[192,640]{1,0:T(8,128)(2,1)S(1)}, u32[]{:S(2)}, u32[]{:S(2)}) %collective-permute-start.2) | collective-permute-done | bytes 245792 | tf_op jit(solution)/shard_map/ppermute | solution.py:115
  34.1 3.6 %shard_map.101 = (bf16[640,256]{1,0:T(8,128)(2,1)S(1)}, f32[640,256]{1,0:T(8,128)S(1)}) custom-call(s32[19]{0:T(128)S(1)} %pad_add_fusion.place, bf16[192,640]{1,0:T(8,128)(2,1)S(1)} %stack.13.refs_0_, bf16[192,640]{1,0:T(8,128)(2,1)S(1)} %collective-permute-done.refs_1_, bf16[192,640]{1,0:T(8,128)(2,1)S(1)} %collective-permute-done.1.refs_2_, ...), custom_call_target="tpu_custom_call" | custom-call | tf_op jit(solution)/shard_map/pallas_call | solution.py:98
  37.7 1.6 %collective-permute-done.7.got = bf16[640,256]{1,0:T(8,128)(2,1)S(1)} collective-permute-done((bf16[640,256]{1,0:T(8,128)(2,1)S(1)}, bf16[640,256]{1,0:T(8,128)(2,1)S(1)}, u32[]{:S(2)}, u32[]{:S(2)}) %collective-permute-start.7) | collective-permute-done | bytes 327712 | tf_op jit(solution)/shard_map/ppermute | solution.py:335
  40.8 5.0 %collective-permute-done.8.got = bf16[640,128]{1,0:T(8,128)(2,1)S(1)} collective-permute-done((bf16[640,128]{1,0:T(8,128)(2,1)S(1)}, bf16[640,128]{1,0:T(8,128)(2,1)S(1)}, u32[]{:S(2)}, u32[]{:S(2)}) %collective-permute-start.8) | collective-permute-done | bytes 163872 | tf_op jit(solution)/shard_map/ppermute | solution.py:339
  47.7 1.4 %collective-permute-start.21 = (bf16[656,128]{1,0:T(8,128)(2,1)S(1)}, bf16[656,128]{1,0:T(8,128)(2,1)S(1)}, u32[]{:S(2)}, u32[]{:S(2)}) collective-permute-start(bf16[656,128]{1,0:T(8,128)(2,1)S(1)} %get-tuple-element.34.refs_0_), channel_id=1, source_target_pairs={{0,2},{2,0},{4,6},{6,4},{8,10},{10,8},{12,14},{14,12},{1,3},{3,1},... | collective-permute-start | bytes 503816 | tf_op jit(solution)/shard_map/ppermute | solution.py:115
  49.0 4.9 %collective-permute-start.9 = (bf16[656,128]{1,0:T(8,128)(2,1)S(1)}, bf16[656,128]{1,0:T(8,128)(2,1)S(1)}, u32[]{:S(2)}, u32[]{:S(2)}) collective-permute-start(bf16[656,128]{1,0:T(8,128)(2,1)S(1)} %get-tuple-element.34.refs_0_), channel_id=1, source_target_pairs={{0,4},{2,6},{4,0},{6,2},{8,12},{10,14},{12,8},{14,10},{1,5},{3,7},... | collective-permute-start | bytes 503816 | tf_op jit(solution)/shard_map/ppermute | solution.py:115
  54.0 3.7 %collective-permute-done.11.refs_1_ = bf16[656,128]{1,0:T(8,128)(2,1)S(1)} collective-permute-done((bf16[656,128]{1,0:T(8,128)(2,1)S(1)}, bf16[656,128]{1,0:T(8,128)(2,1)S(1)}, u32[]{:S(2)}, u32[]{:S(2)}) %collective-permute-start.11) | collective-permute-done | bytes 167968 | tf_op jit(solution)/shard_map/ppermute | solution.py:115
  60.3 3.7 %collective-permute-done.12.refs_0_ = bf16[656,128]{1,0:T(8,128)(2,1)S(1)} collective-permute-done((bf16[656,128]{1,0:T(8,128)(2,1)S(1)}, bf16[656,128]{1,0:T(8,128)(2,1)S(1)}, u32[]{:S(2)}, u32[]{:S(2)}) %collective-permute-start.12) | collective-permute-done | bytes 167968 | tf_op jit(solution)/shard_map/ppermute | solution.py:115
  64.5 2.3 %collective-permute-done.16.refs_1_ = bf16[656,128]{1,0:T(8,128)(2,1)S(1)} collective-permute-done((bf16[656,128]{1,0:T(8,128)(2,1)S(1)}, bf16[656,128]{1,0:T(8,128)(2,1)S(1)}, u32[]{:S(2)}, u32[]{:S(2)}) %collective-permute-start.16) | collective-permute-done | bytes 167968 | tf_op jit(solution)/shard_map/ppermute | solution.py:115
  67.2 2.2 %collective-permute-done.13.refs_1_ = bf16[656,128]{1,0:T(8,128)(2,1)S(1)} collective-permute-done((bf16[656,128]{1,0:T(8,128)(2,1)S(1)}, bf16[656,128]{1,0:T(8,128)(2,1)S(1)}, u32[]{:S(2)}, u32[]{:S(2)}) %collective-permute-start.13) | collective-permute-done | bytes 167968 | tf_op jit(solution)/shard_map/ppermute | solution.py:115
  69.4 6.6 %shard_map.104.refs_4_ = bf16[1728,5120]{1,0:T(8,128)(2,1)S(1)} custom-call(s32[19]{0:T(128)S(1)} %pad_add_fusion.place, bf16[1728,5120]{1,0:T(8,128)(2,1)} %refs_0_.4, bf16[1728,5120]{1,0:T(8,128)(2,1)} %refs_1_.4), custom_call_target="tpu_custom_call" | custom-call | tf_op jit(solution)/shard_map/pallas_call | solution.py:143
  76.0 1.9 %shard_map.105 = (f32[864,256]{1,0:T(8,128)S(1)}, f32[864,256]{1,0:T(8,128)S(1)}, f32[8,256]{1,0:T(8,128)S(1)}) custom-call(s32[19]{0:T(128)S(1)} %pad_add_fusion.place, bf16[656,128]{1,0:T(8,128)(2,1)S(1)} %get-tuple-element.34.refs_0_, bf16[656,128]{1,0:T(8,128)(2,1)S(1)} %collective-permute-done.21.refs_1_, ...), custom_call_target="tpu_custom_call" | custom-call | tf_op jit(solution)/shard_map/pallas_call | solution.py:98
  77.9 2.0 %shard_map.106 = (f32[864,256]{1,0:T(8,128)S(1)}, f32[864,256]{1,0:T(8,128)S(1)}, f32[8,256]{1,0:T(8,128)S(1)}) custom-call(s32[19]{0:T(128)S(1)} %pad_add_fusion.place, bf16[656,128]{1,0:T(8,128)(2,1)S(1)} %collective-permute-done.9.refs_0_, ...), custom_call_target="tpu_custom_call", output_to_operand_aliasing={{0}: (6, {}), {1}: (7, {}), {2}: (8, {})} | custom-call | tf_op jit(solution)/shard_map/pallas_call | solution.py:98
  79.9 2.0 %shard_map.107 = (f32[864,256]{1,0:T(8,128)S(1)}, f32[864,256]{1,0:T(8,128)S(1)}, f32[8,256]{1,0:T(8,128)S(1)}) custom-call(s32[19]{0:T(128)S(1)} %pad_add_fusion.place, bf16[656,128]{1,0:T(8,128)(2,1)S(1)} %collective-permute-done.12.refs_0_, ...), custom_call_target="tpu_custom_call", output_to_operand_aliasing={{0}: (6, {}), {1}: (7, {}), {2}: (8, {})} | custom-call | tf_op jit(solution)/shard_map/pallas_call | solution.py:98
  81.9 2.2 %shard_map.108 = (bf16[128,864]{1,0:T(8,128)(2,1)S(1)}, bf16[128,864]{1,0:T(8,128)(2,1)S(1)}) custom-call(s32[19]{0:T(128)S(1)} %pad_add_fusion.place, bf16[656,128]{1,0:T(8,128)(2,1)S(1)} %collective-permute-done.10.refs_0_, bf16[656,128]{1,0:T(8,128)(2,1)S(1)} %collective-permute-done.13.refs_1_, bf16[656,128]{1,0:T(8,128)(2,1)S(1)} %collective-permute-done.14.refs_2_, ...), custom_call_target="tpu_custom_call" | custom-call | tf_op jit(solution)/shard_map/pallas_call | solution.py:98
  84.7 6.6 %shard_map.109.weights = bf16[1728,5120]{1,0:T(8,128)(2,1)S(1)} custom-call(s32[19]{0:T(128)S(1)} %pad_add_fusion.place, bf16[1728,5120]{1,0:T(8,128)(2,1)} %refs_1_.5, bf16[1728,5120]{1,0:T(8,128)(2,1)} %refs_1_.5), custom_call_target="tpu_custom_call" | custom-call | tf_op jit(solution)/shard_map/pallas_call | solution.py:143
  92.4 1.8 %collective-permute-start.29 = (bf16[128,640]{1,0:T(8,128)(2,1)S(1)}, bf16[128,640]{1,0:T(8,128)(2,1)S(1)}, u32[]{:S(2)}, u32[]{:S(2)}) collective-permute-start(bf16[128,640]{1,0:T(8,128)(2,1)S(1)} %shard_map.115), channel_id=1, source_target_pairs={{0,2},{2,0},{4,6},{6,4},{8,10},{10,8},{12,14},{14,12},{1,3},{3,1},... | collective-permute-start | bytes 491528 | tf_op jit(solution)/shard_map/ppermute | solution.py:115
  94.3 1.6 %shard_map.111 = (f32[128,640]{1,0:T(8,128)S(1)}, bf16[128,640]{1,0:T(8,128)(2,1)S(1)}) custom-call(s32[19]{0:T(128)S(1)} %pad_add_fusion.place, bf16[128,864]{1,0:T(8,128)(2,1)S(1)} %get-tuple-element.44.own, bf16[128,864]{1,0:T(8,128)(2,1)S(1)} %collective-permute-done.24.other, bf16[1728,5120]{1,0:T(8,128)(2,1)S(1)} %shard_map.109.weights), custom_call_target="tpu_custom_call" | custom-call | tf_op jit(solution)/shard_map/pallas_call | solution.py:98
  96.1 1.6 %shard_map.113 = (f32[128,640]{1,0:T(8,128)S(1)}, bf16[128,640]{1,0:T(8,128)(2,1)S(1)}) custom-call(s32[19]{0:T(128)S(1)} %pad_add_fusion.place, bf16[128,864]{1,0:T(8,128)(2,1)S(1)} %get-tuple-element.44.own, bf16[128,864]{1,0:T(8,128)(2,1)S(1)} %collective-permute-done.24.other, bf16[1728,5120]{1,0:T(8,128)(2,1)S(1)} %shard_map.109.weights), custom_call_target="tpu_custom_call" | custom-call | tf_op jit(solution)/shard_map/pallas_call | solution.py:98
  97.7 1.8 %collective-permute-start.28 = (bf16[128,640]{1,0:T(8,128)(2,1)S(1)}, bf16[128,640]{1,0:T(8,128)(2,1)S(1)}, u32[]{:S(2)}, u32[]{:S(2)}) collective-permute-start(bf16[128,640]{1,0:T(8,128)(2,1)S(1)} %get-tuple-element.51), channel_id=1, source_target_pairs={{0,2},{2,0},{4,6},{6,4},{8,10},{10,8},{12,14},{14,12},{1,3},{3,1},... | collective-permute-start | bytes 491528 | tf_op jit(solution)/shard_map/ppermute | solution.py:115
  99.7 2.0 %shard_map.110 = (f32[128,640]{1,0:T(8,128)S(1)}, bf16[128,640]{1,0:T(8,128)(2,1)S(1)}, f32[128,640]{1,0:T(8,128)S(1)}) custom-call(s32[19]{0:T(128)S(1)} %pad_add_fusion.place, bf16[128,864]{1,0:T(8,128)(2,1)S(1)} %get-tuple-element.44.own, bf16[128,864]{1,0:T(8,128)(2,1)S(1)} %collective-permute-done.24.other, bf16[1728,5120]{1,0:T(8,128)(2,1)S(1)} %shard_map.109.weights), custom_call_target="tpu_custom_call" | custom-call | tf_op jit(solution)/shard_map/pallas_call | solution.py:98
  101.7 1.8 %collective-permute-start.25 = (bf16[128,640]{1,0:T(8,128)(2,1)S(1)}, bf16[128,640]{1,0:T(8,128)(2,1)S(1)}, u32[]{:S(2)}, u32[]{:S(2)}) collective-permute-start(bf16[128,640]{1,0:T(8,128)(2,1)S(1)} %get-tuple-element.47), channel_id=1, source_target_pairs={{0,2},{2,0},{4,6},{6,4},{8,10},{10,8},{12,14},{14,12},{1,3},{3,1},... | collective-permute-start | bytes 491528 | tf_op jit(solution)/shard_map/ppermute | solution.py:115
  103.6 2.1 %collective-permute-start.27 = (bf16[128,640]{1,0:T(8,128)(2,1)S(1)}, bf16[128,640]{1,0:T(8,128)(2,1)S(1)}, u32[]{:S(2)}, u32[]{:S(2)}) collective-permute-start(bf16[128,640]{1,0:T(8,128)(2,1)S(1)} %shard_map.112), channel_id=1, source_target_pairs={{0,4},{2,6},{4,0},{6,2},{8,12},{10,14},{12,8},{14,10},{1,5},{3,7},... | collective-permute-start | bytes 491528 | tf_op jit(solution)/shard_map/ppermute | solution.py:115
  106.6 2.1 %collective-permute-start.31 = (bf16[128,640]{1,0:T(8,128)(2,1)S(1)}, bf16[128,640]{1,0:T(8,128)(2,1)S(1)}, u32[]{:S(2)}, u32[]{:S(2)}) collective-permute-start(bf16[128,640]{1,0:T(8,128)(2,1)S(1)} %shard_map.117), channel_id=1, source_target_pairs={{0,8},{2,10},{4,12},{6,14},{8,0},{10,2},{12,4},{14,6},{1,9},{3,11}... | collective-permute-start | bytes 491528 | tf_op jit(solution)/shard_map/ppermute | solution.py:115
  109.9 5.7 %collective-permute-done.31.refs_2_ = bf16[128,640]{1,0:T(8,128)(2,1)S(1)} collective-permute-done((bf16[128,640]{1,0:T(8,128)(2,1)S(1)}, bf16[128,640]{1,0:T(8,128)(2,1)S(1)}, u32[]{:S(2)}, u32[]{:S(2)}) %collective-permute-start.31) | collective-permute-done | bytes 163872 | tf_op jit(solution)/shard_map/ppermute | solution.py:115
  (58 shorter events, 17.0 us)
Async XLA Ops:
  1.0 15.5 %collective-permute-start.3 = (bf16[192,640]{1,0:T(8,128)(2,1)S(1)}, bf16[192,640]{1,0:T(8,128)(2,1)S(1)}, u32[]{:S(2)}, u32[]{:S(2)}) collective-permute-start(bf16[192,640]{1,0:T(8,128)(2,1)S(1)} %stack.13.refs_0_), channel_id=1, source_target_pairs={{0,8},{2,10},{4,12},{6,14},{8,0},{10,2},{12,4},{14,6},{1,9},{3,11}... | collective-permute-start | bytes 737288 | tf_op jit(solution)/shard_map/ppermute | solution.py:115
  5.1 14.0 %collective-permute-start.1 = (bf16[192,640]{1,0:T(8,128)(2,1)S(1)}, bf16[192,640]{1,0:T(8,128)(2,1)S(1)}, u32[]{:S(2)}, u32[]{:S(2)}) collective-permute-start(bf16[192,640]{1,0:T(8,128)(2,1)S(1)} %stack.13.refs_0_), channel_id=1, source_target_pairs={{0,4},{2,6},{4,0},{6,2},{8,12},{10,14},{12,8},{14,10},{1,5},{3,7},... | collective-permute-start | bytes 737288 | tf_op jit(solution)/shard_map/ppermute | solution.py:115
  16.5 8.8 %collective-permute-start.4 = (bf16[192,640]{1,0:T(8,128)(2,1)S(1)}, bf16[192,640]{1,0:T(8,128)(2,1)S(1)}, u32[]{:S(2)}, u32[]{:S(2)}) collective-permute-start(bf16[192,640]{1,0:T(8,128)(2,1)S(1)} %collective-permute-done.3.refs_4_), channel_id=1, source_target_pairs={{0,2},{2,0},{4,6},{6,4},{8,10},{10,8},{12,14},{14,12},{1,3},{3,1},... | collective-permute-start | bytes 737288 | tf_op jit(solution)/shard_map/ppermute | solution.py:115
  18.0 12.5 %collective-permute-start = (bf16[192,640]{1,0:T(8,128)(2,1)S(1)}, bf16[192,640]{1,0:T(8,128)(2,1)S(1)}, u32[]{:S(2)}, u32[]{:S(2)}) collective-permute-start(bf16[192,640]{1,0:T(8,128)(2,1)S(1)} %stack.13.refs_0_), channel_id=1, source_target_pairs={{0,2},{2,0},{4,6},{6,4},{8,10},{10,8},{12,14},{14,12},{1,3},{3,1},... | collective-permute-start | bytes 737288 | tf_op jit(solution)/shard_map/ppermute | solution.py:115
  18.5 12.1 %collective-permute-start.5 = (bf16[192,640]{1,0:T(8,128)(2,1)S(1)}, bf16[192,640]{1,0:T(8,128)(2,1)S(1)}, u32[]{:S(2)}, u32[]{:S(2)}) collective-permute-start(bf16[192,640]{1,0:T(8,128)(2,1)S(1)} %collective-permute-done.3.refs_4_), channel_id=1, source_target_pairs={{0,4},{2,6},{4,0},{6,2},{8,12},{10,14},{12,8},{14,10},{1,5},{3,7},... | collective-permute-start | bytes 737288 | tf_op jit(solution)/shard_map/ppermute | solution.py:115
  19.1 14.9 %collective-permute-start.2 = (bf16[192,640]{1,0:T(8,128)(2,1)S(1)}, bf16[192,640]{1,0:T(8,128)(2,1)S(1)}, u32[]{:S(2)}, u32[]{:S(2)}) collective-permute-start(bf16[192,640]{1,0:T(8,128)(2,1)S(1)} %collective-permute-done.1.refs_2_), channel_id=1, source_target_pairs={{0,2},{2,0},{4,6},{6,4},{8,10},{10,8},{12,14},{14,12},{1,3},{3,1},... | collective-permute-start | bytes 737288 | tf_op jit(solution)/shard_map/ppermute | solution.py:115
  25.3 8.8 %collective-permute-start.6 = (bf16[192,640]{1,0:T(8,128)(2,1)S(1)}, bf16[192,640]{1,0:T(8,128)(2,1)S(1)}, u32[]{:S(2)}, u32[]{:S(2)}) collective-permute-start(bf16[192,640]{1,0:T(8,128)(2,1)S(1)} %collective-permute-done.4.refs_5_), channel_id=1, source_target_pairs={{0,4},{2,6},{4,0},{6,2},{8,12},{10,14},{12,8},{14,10},{1,5},{3,7},... | collective-permute-start | bytes 737288 | tf_op jit(solution)/shard_map/ppermute | solution.py:115
  37.6 1.7 %collective-permute-start.7 = (bf16[640,256]{1,0:T(8,128)(2,1)S(1)}, bf16[640,256]{1,0:T(8,128)(2,1)S(1)}, u32[]{:S(2)}, u32[]{:S(2)}) collective-permute-start(bf16[640,256]{1,0:T(8,128)(2,1)S(1)} %get-tuple-element.30), channel_id=1, source_target_pairs={{0,1},{1,0},{2,3},{3,2},{4,5},{5,4},{6,7},{7,6},{8,9},{9,8},{10,11... | collective-permute-start | bytes 983048 | tf_op jit(solution)/shard_map/ppermute | solution.py:335
  39.4 6.3 %collective-permute-start.8 = (bf16[640,128]{1,0:T(8,128)(2,1)S(1)}, bf16[640,128]{1,0:T(8,128)(2,1)S(1)}, u32[]{:S(2)}, u32[]{:S(2)}) collective-permute-start(bf16[640,128]{1,0:T(8,128)(2,1)S(1)} %get-tuple-element.32), channel_id=1, source_target_pairs={{0,16},{16,0},{1,17},{17,1},{2,18},{18,2},{3,19},{19,3},{4,20},{20... | collective-permute-start | bytes 491528 | tf_op jit(solution)/shard_map/ppermute | solution.py:339
  47.6 10.1 %collective-permute-start.11 = (bf16[656,128]{1,0:T(8,128)(2,1)S(1)}, bf16[656,128]{1,0:T(8,128)(2,1)S(1)}, u32[]{:S(2)}, u32[]{:S(2)}) collective-permute-start(bf16[656,128]{1,0:T(8,128)(2,1)S(1)} %get-tuple-element.34.refs_0_), channel_id=1, source_target_pairs={{0,8},{2,10},{4,12},{6,14},{8,0},{10,2},{12,4},{14,6},{1,9},{3,11}... | collective-permute-start | bytes 503816 | tf_op jit(solution)/shard_map/ppermute | solution.py:115
  47.7 11.4 %collective-permute-start.21 = (bf16[656,128]{1,0:T(8,128)(2,1)S(1)}, bf16[656,128]{1,0:T(8,128)(2,1)S(1)}, u32[]{:S(2)}, u32[]{:S(2)}) collective-permute-start(bf16[656,128]{1,0:T(8,128)(2,1)S(1)} %get-tuple-element.34.refs_0_), channel_id=1, source_target_pairs={{0,2},{2,0},{4,6},{6,4},{8,10},{10,8},{12,14},{14,12},{1,3},{3,1},... | collective-permute-start | bytes 503816 | tf_op jit(solution)/shard_map/ppermute | solution.py:115
  49.0 10.0 %collective-permute-start.9 = (bf16[656,128]{1,0:T(8,128)(2,1)S(1)}, bf16[656,128]{1,0:T(8,128)(2,1)S(1)}, u32[]{:S(2)}, u32[]{:S(2)}) collective-permute-start(bf16[656,128]{1,0:T(8,128)(2,1)S(1)} %get-tuple-element.34.refs_0_), channel_id=1, source_target_pairs={{0,4},{2,6},{4,0},{6,2},{8,12},{10,14},{12,8},{14,10},{1,5},{3,7},... | collective-permute-start | bytes 503816 | tf_op jit(solution)/shard_map/ppermute | solution.py:115
  54.0 5.7 %collective-permute-start.22 = (bf16[656,128]{1,0:T(8,128)(2,1)S(1)}, bf16[656,128]{1,0:T(8,128)(2,1)S(1)}, u32[]{:S(2)}, u32[]{:S(2)}) collective-permute-start(bf16[656,128]{1,0:T(8,128)(2,1)S(1)} %get-tuple-element.34.refs_0_), channel_id=1, source_target_pairs={{0,1},{1,0},{2,3},{3,2},{4,5},{5,4},{6,7},{7,6},{8,9},{9,8},{10,11... | collective-permute-start | bytes 503816 | tf_op jit(solution)/shard_map/ppermute | solution.py:350
  57.7 6.2 %collective-permute-start.12 = (bf16[656,128]{1,0:T(8,128)(2,1)S(1)}, bf16[656,128]{1,0:T(8,128)(2,1)S(1)}, u32[]{:S(2)}, u32[]{:S(2)}) collective-permute-start(bf16[656,128]{1,0:T(8,128)(2,1)S(1)} %collective-permute-done.11.refs_1_), channel_id=1, source_target_pairs={{0,2},{2,0},{4,6},{6,4},{8,10},{10,8},{12,14},{14,12},{1,3},{3,1},... | collective-permute-start | bytes 503816 | tf_op jit(solution)/shard_map/ppermute | solution.py:115
  59.0 4.9 %collective-permute-start.23 = (bf16[656,128]{1,0:T(8,128)(2,1)S(1)}, bf16[656,128]{1,0:T(8,128)(2,1)S(1)}, u32[]{:S(2)}, u32[]{:S(2)}) collective-permute-start(bf16[656,128]{1,0:T(8,128)(2,1)S(1)} %collective-permute-done.21.refs_1_), channel_id=1, source_target_pairs={{0,1},{1,0},{2,3},{3,2},{4,5},{5,4},{6,7},{7,6},{8,9},{9,8},{10,11... | collective-permute-start | bytes 503816 | tf_op jit(solution)/shard_map/ppermute | solution.py:350
  59.0 4.9 %collective-permute-start.19 = (bf16[656,128]{1,0:T(8,128)(2,1)S(1)}, bf16[656,128]{1,0:T(8,128)(2,1)S(1)}, u32[]{:S(2)}, u32[]{:S(2)}) collective-permute-start(bf16[656,128]{1,0:T(8,128)(2,1)S(1)} %collective-permute-done.9.refs_0_), channel_id=1, source_target_pairs={{0,1},{1,0},{2,3},{3,2},{4,5},{5,4},{6,7},{7,6},{8,9},{9,8},{10,11... | collective-permute-start | bytes 503816 | tf_op jit(solution)/shard_map/ppermute | solution.py:350
  59.5 7.2 %collective-permute-start.16 = (bf16[656,128]{1,0:T(8,128)(2,1)S(1)}, bf16[656,128]{1,0:T(8,128)(2,1)S(1)}, u32[]{:S(2)}, u32[]{:S(2)}) collective-permute-start(bf16[656,128]{1,0:T(8,128)(2,1)S(1)} %collective-permute-done.11.refs_1_), channel_id=1, source_target_pairs={{0,4},{2,6},{4,0},{6,2},{8,12},{10,14},{12,8},{14,10},{1,5},{3,7},... | collective-permute-start | bytes 503816 | tf_op jit(solution)/shard_map/ppermute | solution.py:115
  59.6 7.1 %collective-permute-start.10 = (bf16[656,128]{1,0:T(8,128)(2,1)S(1)}, bf16[656,128]{1,0:T(8,128)(2,1)S(1)}, u32[]{:S(2)}, u32[]{:S(2)}) collective-permute-start(bf16[656,128]{1,0:T(8,128)(2,1)S(1)} %collective-permute-done.9.refs_0_), channel_id=1, source_target_pairs={{0,2},{2,0},{4,6},{6,4},{8,10},{10,8},{12,14},{14,12},{1,3},{3,1},... | collective-permute-start | bytes 503816 | tf_op jit(solution)/shard_map/ppermute | solution.py:115
  63.9 5.5 %collective-permute-start.13 = (bf16[656,128]{1,0:T(8,128)(2,1)S(1)}, bf16[656,128]{1,0:T(8,128)(2,1)S(1)}, u32[]{:S(2)}, u32[]{:S(2)}) collective-permute-start(bf16[656,128]{1,0:T(8,128)(2,1)S(1)} %collective-permute-done.12.refs_0_), channel_id=1, source_target_pairs={{0,4},{2,6},{4,0},{6,2},{8,12},{10,14},{12,8},{14,10},{1,5},{3,7},... | collective-permute-start | bytes 503816 | tf_op jit(solution)/shard_map/ppermute | solution.py:115
  63.9 14.0 %collective-permute-start.20 = (bf16[656,128]{1,0:T(8,128)(2,1)S(1)}, bf16[656,128]{1,0:T(8,128)(2,1)S(1)}, u32[]{:S(2)}, u32[]{:S(2)}) collective-permute-start(bf16[656,128]{1,0:T(8,128)(2,1)S(1)} %collective-permute-done.11.refs_1_), channel_id=1, source_target_pairs={{0,1},{1,0},{2,3},{3,2},{4,5},{5,4},{6,7},{7,6},{8,9},{9,8},{10,11... | collective-permute-start | bytes 503816 | tf_op jit(solution)/shard_map/ppermute | solution.py:350
  64.0 15.9 %collective-permute-start.17 = (bf16[656,128]{1,0:T(8,128)(2,1)S(1)}, bf16[656,128]{1,0:T(8,128)(2,1)S(1)}, u32[]{:S(2)}, u32[]{:S(2)}) collective-permute-start(bf16[656,128]{1,0:T(8,128)(2,1)S(1)} %collective-permute-done.12.refs_0_), channel_id=1, source_target_pairs={{0,1},{1,0},{2,3},{3,2},{4,5},{5,4},{6,7},{7,6},{8,9},{9,8},{10,11... | collective-permute-start | bytes 503816 | tf_op jit(solution)/shard_map/ppermute | solution.py:350
  66.7 13.2 %collective-permute-start.18 = (bf16[656,128]{1,0:T(8,128)(2,1)S(1)}, bf16[656,128]{1,0:T(8,128)(2,1)S(1)}, u32[]{:S(2)}, u32[]{:S(2)}) collective-permute-start(bf16[656,128]{1,0:T(8,128)(2,1)S(1)} %collective-permute-done.16.refs_1_), channel_id=1, source_target_pairs={{0,1},{1,0},{2,3},{3,2},{4,5},{5,4},{6,7},{7,6},{8,9},{9,8},{10,11... | collective-permute-start | bytes 503816 | tf_op jit(solution)/shard_map/ppermute | solution.py:350
  66.7 15.2 %collective-permute-start.14 = (bf16[656,128]{1,0:T(8,128)(2,1)S(1)}, bf16[656,128]{1,0:T(8,128)(2,1)S(1)}, u32[]{:S(2)}, u32[]{:S(2)}) collective-permute-start(bf16[656,128]{1,0:T(8,128)(2,1)S(1)} %collective-permute-done.10.refs_0_), channel_id=1, source_target_pairs={{0,1},{1,0},{2,3},{3,2},{4,5},{5,4},{6,7},{7,6},{8,9},{9,8},{10,11... | collective-permute-start | bytes 503816 | tf_op jit(solution)/shard_map/ppermute | solution.py:350
  69.4 12.5 %collective-permute-start.15 = (bf16[656,128]{1,0:T(8,128)(2,1)S(1)}, bf16[656,128]{1,0:T(8,128)(2,1)S(1)}, u32[]{:S(2)}, u32[]{:S(2)}) collective-permute-start(bf16[656,128]{1,0:T(8,128)(2,1)S(1)} %collective-permute-done.13.refs_1_), channel_id=1, source_target_pairs={{0,1},{1,0},{2,3},{3,2},{4,5},{5,4},{6,7},{7,6},{8,9},{9,8},{10,11... | collective-permute-start | bytes 503816 | tf_op jit(solution)/shard_map/ppermute | solution.py:350
  84.1 7.2 %collective-permute-start.24 = (bf16[128,864]{1,0:T(8,128)(2,1)S(1)}, bf16[128,864]{1,0:T(8,128)(2,1)S(1)}, u32[]{:S(2)}, u32[]{:S(2)}) collective-permute-start(bf16[128,864]{1,0:T(8,128)(2,1)S(1)} %get-tuple-element.45), channel_id=1, source_target_pairs={{0,1},{1,0},{2,3},{3,2},{4,5},{5,4},{6,7},{7,6},{8,9},{9,8},{10,11... | collective-permute-start | bytes 663560 | tf_op jit(solution)/shard_map/ppermute | solution.py:350
  92.4 7.1 %collective-permute-start.29 = (bf16[128,640]{1,0:T(8,128)(2,1)S(1)}, bf16[128,640]{1,0:T(8,128)(2,1)S(1)}, u32[]{:S(2)}, u32[]{:S(2)}) collective-permute-start(bf16[128,640]{1,0:T(8,128)(2,1)S(1)} %shard_map.115), channel_id=1, source_target_pairs={{0,2},{2,0},{4,6},{6,4},{8,10},{10,8},{12,14},{14,12},{1,3},{3,1},... | collective-permute-start | bytes 491528 | tf_op jit(solution)/shard_map/ppermute | solution.py:115
  95.8 7.7 %collective-permute-start.26 = (bf16[128,640]{1,0:T(8,128)(2,1)S(1)}, bf16[128,640]{1,0:T(8,128)(2,1)S(1)}, u32[]{:S(2)}, u32[]{:S(2)}) collective-permute-start(bf16[128,640]{1,0:T(8,128)(2,1)S(1)} %get-tuple-element.49), channel_id=1, source_target_pairs={{0,2},{2,0},{4,6},{6,4},{8,10},{10,8},{12,14},{14,12},{1,3},{3,1},... | collective-permute-start | bytes 491528 | tf_op jit(solution)/shard_map/ppermute | solution.py:115
  97.7 8.8 %collective-permute-start.28 = (bf16[128,640]{1,0:T(8,128)(2,1)S(1)}, bf16[128,640]{1,0:T(8,128)(2,1)S(1)}, u32[]{:S(2)}, u32[]{:S(2)}) collective-permute-start(bf16[128,640]{1,0:T(8,128)(2,1)S(1)} %get-tuple-element.51), channel_id=1, source_target_pairs={{0,2},{2,0},{4,6},{6,4},{8,10},{10,8},{12,14},{14,12},{1,3},{3,1},... | collective-permute-start | bytes 491528 | tf_op jit(solution)/shard_map/ppermute | solution.py:115
  99.6 6.9 %collective-permute-start.30 = (bf16[128,640]{1,0:T(8,128)(2,1)S(1)}, bf16[128,640]{1,0:T(8,128)(2,1)S(1)}, u32[]{:S(2)}, u32[]{:S(2)}) collective-permute-start(bf16[128,640]{1,0:T(8,128)(2,1)S(1)} %shard_map.116), channel_id=1, source_target_pairs={{0,4},{2,6},{4,0},{6,2},{8,12},{10,14},{12,8},{14,10},{1,5},{3,7},... | collective-permute-start | bytes 491528 | tf_op jit(solution)/shard_map/ppermute | solution.py:115
  101.7 7.5 %collective-permute-start.25 = (bf16[128,640]{1,0:T(8,128)(2,1)S(1)}, bf16[128,640]{1,0:T(8,128)(2,1)S(1)}, u32[]{:S(2)}, u32[]{:S(2)}) collective-permute-start(bf16[128,640]{1,0:T(8,128)(2,1)S(1)} %get-tuple-element.47), channel_id=1, source_target_pairs={{0,2},{2,0},{4,6},{6,4},{8,10},{10,8},{12,14},{14,12},{1,3},{3,1},... | collective-permute-start | bytes 491528 | tf_op jit(solution)/shard_map/ppermute | solution.py:115
  103.6 6.3 %collective-permute-start.27 = (bf16[128,640]{1,0:T(8,128)(2,1)S(1)}, bf16[128,640]{1,0:T(8,128)(2,1)S(1)}, u32[]{:S(2)}, u32[]{:S(2)}) collective-permute-start(bf16[128,640]{1,0:T(8,128)(2,1)S(1)} %shard_map.112), channel_id=1, source_target_pairs={{0,4},{2,6},{4,0},{6,2},{8,12},{10,14},{12,8},{14,10},{1,5},{3,7},... | collective-permute-start | bytes 491528 | tf_op jit(solution)/shard_map/ppermute | solution.py:115
  106.6 9.1 %collective-permute-start.31 = (bf16[128,640]{1,0:T(8,128)(2,1)S(1)}, bf16[128,640]{1,0:T(8,128)(2,1)S(1)}, u32[]{:S(2)}, u32[]{:S(2)}) collective-permute-start(bf16[128,640]{1,0:T(8,128)(2,1)S(1)} %shard_map.117), channel_id=1, source_target_pairs={{0,8},{2,10},{4,12},{6,14},{8,0},{10,2},{12,4},{14,6},{1,9},{3,11}... | collective-permute-start | bytes 491528 | tf_op jit(solution)/shard_map/ppermute | solution.py:115
  (2 other events, 2.1 us)

commit v3 on v2

--- a/solution.py
+++ b/solution.py
@@ -280,12 +280,11 @@
 
 
 def down_body(offsets, columns):
-    def body(place, own, other, weights, *outs):
-        units = own.shape[1]
+    def body(place, own, other, w_own, w_other, *outs):
         for r, out in zip(offsets, outs):
             at = pl.ds(pl.multiple_of((place[0] ^ r) * columns, 128), columns)
-            total = jnp.dot(own[...], weights[pl.ds(0, units), at], preferred_element_type=jnp.float32)
-            total = total + jnp.dot(other[...], weights[pl.ds(units, units), at], preferred_element_type=jnp.float32)
+            total = jnp.dot(own[...], w_own[:, at], preferred_element_type=jnp.float32)
+            total = total + jnp.dot(other[...], w_other[:, at], preferred_element_type=jnp.float32)
             out[...] = total.astype(out.dtype)
 
     return body
@@ -322,7 +321,7 @@
     blocks = gather(stack([queries, keys, values]), n_seq)
     mine, theirs = (lambda p: p[2] * share), (lambda p: (1 - p[2]) * share)
     w_gate_up = fetch(place, [w_gate, w_up], share, (mine, mine))
-    w_down = fetch(place, [w_down, w_down], share, (mine, theirs))
+    w_down = [fetch(place, [w_down], share, (base,)) for base in (mine, theirs)]
     wo_t = call(turn_body, struct(wo.shape[::-1], bf16), (wo,), limit=4)
     send, keep = call(
         attend_body(n_seq, seq_dev, heads_features // HEAD_DIM, groups, reps),
@@ -372,7 +371,7 @@
         return call(
             down_body([r for r, _ in offsets_types], columns),
             tuple(struct((group_tokens, columns), t) for _, t in offsets_types),
-            (place, *hidden, w_down),
+            (place, *hidden, *w_down),
             scalars=1,
             limit=3,
         )

time: 117 us -> 118 us (level)
  Pallas kernels: 33.5 us -> 35 us
    pallas_call x2 -> x3, Pallas kernels: 13.2 us -> 14.7 us  [fetch(): pl.pallas_call(body, out_shape=pltpu.VMEM((n * rows, width), arrays[0].dt...]
  transfers between devices with their start and end apart: 32 -> 32, of which waited for: 14 -> 14; matrix products, arithmetic and copies ran while one was open for 1% -> 1% of each run, Pallas kernels for 21% -> 22%
where the time goes in v3:
time: 118 us
  waiting for transfers between devices  46.6 us (39%)
  Pallas kernels  35 us (30%)
  starting transfers between devices  32.5 us (28%)
  local copies, waits for them, and re-layouts  2.88 us (2%)
    ppermute x21, waiting for transfers between devices, swap(): return lax.ppermute(x, 'seq', [(i, i ^ offset) for i in range(n_seq)])  40 us
    ppermute x21, starting transfers between devices, swap(): return lax.ppermute(x, 'seq', [(i, i ^ offset) for i in range(n_seq)])  29 us
    pallas_call x17, Pallas kernels, call(): pl.pallas_call(body, out_shape=outs, in_specs=spaces, out_specs=jax.tree....  19.3 us
    pallas_call x3, Pallas kernels, fetch(): pl.pallas_call(body, out_shape=pltpu.VMEM((n * rows, width), arrays[0].dt...  14.7 us
    ppermute x1, waiting for transfers between devices, exchanged(): got = lax.ppermute(send, 'section', [(0, 1), (1, 0)])  4.95 us
  transfers between devices with their start and end apart: 32, of which 14 were waited for; matrix products, arithmetic and copies ran while one was open for 1% of the time, Pallas kernels for 22%

profile of v3, /device:TPU:0, one launch (start us, length us, event | category | flops | bytes accessed | tf_op | source)
XLA Modules:
  0.0 118.0 jit_solution(16183163147083188122)
XLA Ops:
  1.0 4.1 %collective-permute-start.3 = (bf16[192,640]{1,0:T(8,128)(2,1)S(1)}, bf16[192,640]{1,0:T(8,128)(2,1)S(1)}, u32[]{:S(2)}, u32[]{:S(2)}) collective-permute-start(bf16[192,640]{1,0:T(8,128)(2,1)S(1)} %stack.13.refs_0_), channel_id=1, source_target_pairs={{0,8},{2,10},{4,12},{6,14},{8,0},{10,2},{12,4},{14,6},{1,9},{3,11}... | collective-permute-start | bytes 737288 | tf_op jit(solution)/shard_map/ppermute | solution.py:115
  5.1 1.6 %collective-permute-start.1 = (bf16[192,640]{1,0:T(8,128)(2,1)S(1)}, bf16[192,640]{1,0:T(8,128)(2,1)S(1)}, u32[]{:S(2)}, u32[]{:S(2)}) collective-permute-start(bf16[192,640]{1,0:T(8,128)(2,1)S(1)} %stack.13.refs_0_), channel_id=1, source_target_pairs={{0,4},{2,6},{4,0},{6,2},{8,12},{10,14},{12,8},{14,10},{1,5},{3,7},... | collective-permute-start | bytes 737288 | tf_op jit(solution)/shard_map/ppermute | solution.py:115
  6.7 9.7 %collective-permute-done.3.refs_4_ = bf16[192,640]{1,0:T(8,128)(2,1)S(1)} collective-permute-done((bf16[192,640]{1,0:T(8,128)(2,1)S(1)}, bf16[192,640]{1,0:T(8,128)(2,1)S(1)}, u32[]{:S(2)}, u32[]{:S(2)}) %collective-permute-start.3) | collective-permute-done | bytes 245792 | tf_op jit(solution)/shard_map/ppermute | solution.py:115
  16.5 1.6 %collective-permute-start.4 = (bf16[192,640]{1,0:T(8,128)(2,1)S(1)}, bf16[192,640]{1,0:T(8,128)(2,1)S(1)}, u32[]{:S(2)}, u32[]{:S(2)}) collective-permute-start(bf16[192,640]{1,0:T(8,128)(2,1)S(1)} %collective-permute-done.3.refs_4_), channel_id=1, source_target_pairs={{0,2},{2,0},{4,6},{6,4},{8,10},{10,8},{12,14},{14,12},{1,3},{3,1},... | collective-permute-start | bytes 737288 | tf_op jit(solution)/shard_map/ppermute | solution.py:115
  19.1 1.5 %collective-permute-start.2 = (bf16[192,640]{1,0:T(8,128)(2,1)S(1)}, bf16[192,640]{1,0:T(8,128)(2,1)S(1)}, u32[]{:S(2)}, u32[]{:S(2)}) collective-permute-start(bf16[192,640]{1,0:T(8,128)(2,1)S(1)} %collective-permute-done.1.refs_2_), channel_id=1, source_target_pairs={{0,2},{2,0},{4,6},{6,4},{8,10},{10,8},{12,14},{14,12},{1,3},{3,1},... | collective-permute-start | bytes 737288 | tf_op jit(solution)/shard_map/ppermute | solution.py:115
  20.6 4.7 %collective-permute-done.4.refs_5_ = bf16[192,640]{1,0:T(8,128)(2,1)S(1)} collective-permute-done((bf16[192,640]{1,0:T(8,128)(2,1)S(1)}, bf16[192,640]{1,0:T(8,128)(2,1)S(1)}, u32[]{:S(2)}, u32[]{:S(2)}) %collective-permute-start.4) | collective-permute-done | bytes 245792 | tf_op jit(solution)/shard_map/ppermute | solution.py:115
  28.1 2.5 %collective-permute-done.refs_1_ = bf16[192,640]{1,0:T(8,128)(2,1)S(1)} collective-permute-done((bf16[192,640]{1,0:T(8,128)(2,1)S(1)}, bf16[192,640]{1,0:T(8,128)(2,1)S(1)}, u32[]{:S(2)}, u32[]{:S(2)}) %collective-permute-start) | collective-permute-done | bytes 245792 | tf_op jit(solution)/shard_map/ppermute | solution.py:115
  30.5 3.5 %collective-permute-done.2.refs_3_ = bf16[192,640]{1,0:T(8,128)(2,1)S(1)} collective-permute-done((bf16[192,640]{1,0:T(8,128)(2,1)S(1)}, bf16[192,640]{1,0:T(8,128)(2,1)S(1)}, u32[]{:S(2)}, u32[]{:S(2)}) %collective-permute-start.2) | collective-permute-done | bytes 245792 | tf_op jit(solution)/shard_map/ppermute | solution.py:115
  34.1 3.6 %shard_map.101 = (bf16[640,256]{1,0:T(8,128)(2,1)S(1)}, f32[640,256]{1,0:T(8,128)S(1)}) custom-call(s32[19]{0:T(128)S(1)} %pad_add_fusion.place, bf16[192,640]{1,0:T(8,128)(2,1)S(1)} %stack.13.refs_0_, bf16[192,640]{1,0:T(8,128)(2,1)S(1)} %collective-permute-done.refs_1_, bf16[192,640]{1,0:T(8,128)(2,1)S(1)} %collective-permute-done.1.refs_2_, ...), custom_call_target="tpu_custom_call" | custom-call | tf_op jit(solution)/shard_map/pallas_call | solution.py:98
  37.7 1.6 %collective-permute-done.7.got = bf16[640,256]{1,0:T(8,128)(2,1)S(1)} collective-permute-done((bf16[640,256]{1,0:T(8,128)(2,1)S(1)}, bf16[640,256]{1,0:T(8,128)(2,1)S(1)}, u32[]{:S(2)}, u32[]{:S(2)}) %collective-permute-start.7) | collective-permute-done | bytes 327712 | tf_op jit(solution)/shard_map/ppermute | solution.py:334
  40.8 5.0 %collective-permute-done.8.got = bf16[640,128]{1,0:T(8,128)(2,1)S(1)} collective-permute-done((bf16[640,128]{1,0:T(8,128)(2,1)S(1)}, bf16[640,128]{1,0:T(8,128)(2,1)S(1)}, u32[]{:S(2)}, u32[]{:S(2)}) %collective-permute-start.8) | collective-permute-done | bytes 163872 | tf_op jit(solution)/shard_map/ppermute | solution.py:338
  49.0 4.9 %collective-permute-start.9 = (bf16[656,128]{1,0:T(8,128)(2,1)S(1)}, bf16[656,128]{1,0:T(8,128)(2,1)S(1)}, u32[]{:S(2)}, u32[]{:S(2)}) collective-permute-start(bf16[656,128]{1,0:T(8,128)(2,1)S(1)} %get-tuple-element.34.refs_0_), channel_id=1, source_target_pairs={{0,4},{2,6},{4,0},{6,2},{8,12},{10,14},{12,8},{14,10},{1,5},{3,7},... | collective-permute-start | bytes 503816 | tf_op jit(solution)/shard_map/ppermute | solution.py:115
  54.0 3.7 %collective-permute-done.11.refs_1_ = bf16[656,128]{1,0:T(8,128)(2,1)S(1)} collective-permute-done((bf16[656,128]{1,0:T(8,128)(2,1)S(1)}, bf16[656,128]{1,0:T(8,128)(2,1)S(1)}, u32[]{:S(2)}, u32[]{:S(2)}) %collective-permute-start.11) | collective-permute-done | bytes 167968 | tf_op jit(solution)/shard_map/ppermute | solution.py:115
  60.3 3.7 %collective-permute-done.12.refs_0_ = bf16[656,128]{1,0:T(8,128)(2,1)S(1)} collective-permute-done((bf16[656,128]{1,0:T(8,128)(2,1)S(1)}, bf16[656,128]{1,0:T(8,128)(2,1)S(1)}, u32[]{:S(2)}, u32[]{:S(2)}) %collective-permute-start.12) | collective-permute-done | bytes 167968 | tf_op jit(solution)/shard_map/ppermute | solution.py:115
  64.5 2.3 %collective-permute-done.16.refs_1_ = bf16[656,128]{1,0:T(8,128)(2,1)S(1)} collective-permute-done((bf16[656,128]{1,0:T(8,128)(2,1)S(1)}, bf16[656,128]{1,0:T(8,128)(2,1)S(1)}, u32[]{:S(2)}, u32[]{:S(2)}) %collective-permute-start.16) | collective-permute-done | bytes 167968 | tf_op jit(solution)/shard_map/ppermute | solution.py:115
  67.2 2.2 %collective-permute-done.13.refs_1_ = bf16[656,128]{1,0:T(8,128)(2,1)S(1)} collective-permute-done((bf16[656,128]{1,0:T(8,128)(2,1)S(1)}, bf16[656,128]{1,0:T(8,128)(2,1)S(1)}, u32[]{:S(2)}, u32[]{:S(2)}) %collective-permute-start.13) | collective-permute-done | bytes 167968 | tf_op jit(solution)/shard_map/ppermute | solution.py:115
  69.4 6.6 %shard_map.104.refs_4_ = bf16[1728,5120]{1,0:T(8,128)(2,1)S(1)} custom-call(s32[19]{0:T(128)S(1)} %pad_add_fusion.place, bf16[1728,5120]{1,0:T(8,128)(2,1)} %refs_0_.5, bf16[1728,5120]{1,0:T(8,128)(2,1)} %refs_1_.3), custom_call_target="tpu_custom_call" | custom-call | tf_op jit(solution)/shard_map/pallas_call | solution.py:143
  76.0 1.9 %shard_map.105 = (f32[864,256]{1,0:T(8,128)S(1)}, f32[864,256]{1,0:T(8,128)S(1)}, f32[8,256]{1,0:T(8,128)S(1)}) custom-call(s32[19]{0:T(128)S(1)} %pad_add_fusion.place, bf16[656,128]{1,0:T(8,128)(2,1)S(1)} %get-tuple-element.34.refs_0_, bf16[656,128]{1,0:T(8,128)(2,1)S(1)} %collective-permute-done.21.refs_1_, ...), custom_call_target="tpu_custom_call" | custom-call | tf_op jit(solution)/shard_map/pallas_call | solution.py:98
  77.9 2.0 %shard_map.106 = (f32[864,256]{1,0:T(8,128)S(1)}, f32[864,256]{1,0:T(8,128)S(1)}, f32[8,256]{1,0:T(8,128)S(1)}) custom-call(s32[19]{0:T(128)S(1)} %pad_add_fusion.place, bf16[656,128]{1,0:T(8,128)(2,1)S(1)} %collective-permute-done.9.refs_0_, ...), custom_call_target="tpu_custom_call", output_to_operand_aliasing={{0}: (6, {}), {1}: (7, {}), {2}: (8, {})} | custom-call | tf_op jit(solution)/shard_map/pallas_call | solution.py:98
  79.9 2.0 %shard_map.107 = (f32[864,256]{1,0:T(8,128)S(1)}, f32[864,256]{1,0:T(8,128)S(1)}, f32[8,256]{1,0:T(8,128)S(1)}) custom-call(s32[19]{0:T(128)S(1)} %pad_add_fusion.place, bf16[656,128]{1,0:T(8,128)(2,1)S(1)} %collective-permute-done.12.refs_0_, ...), custom_call_target="tpu_custom_call", output_to_operand_aliasing={{0}: (6, {}), {1}: (7, {}), {2}: (8, {})} | custom-call | tf_op jit(solution)/shard_map/pallas_call | solution.py:98
  81.9 2.2 %shard_map.108 = (bf16[128,864]{1,0:T(8,128)(2,1)S(1)}, bf16[128,864]{1,0:T(8,128)(2,1)S(1)}) custom-call(s32[19]{0:T(128)S(1)} %pad_add_fusion.place, bf16[656,128]{1,0:T(8,128)(2,1)S(1)} %collective-permute-done.10.refs_0_, bf16[656,128]{1,0:T(8,128)(2,1)S(1)} %collective-permute-done.13.refs_1_, bf16[656,128]{1,0:T(8,128)(2,1)S(1)} %collective-permute-done.14.refs_2_, ...), custom_call_target="tpu_custom_call" | custom-call | tf_op jit(solution)/shard_map/pallas_call | solution.py:98
  84.7 4.1 %shard_map.109.w_own = bf16[864,5120]{1,0:T(8,128)(2,1)S(1)} custom-call(s32[19]{0:T(128)S(1)} %pad_add_fusion.place, bf16[1728,5120]{1,0:T(8,128)(2,1)} %refs_0_.7), custom_call_target="tpu_custom_call" | custom-call | tf_op jit(solution)/shard_map/pallas_call | solution.py:143
  88.8 4.1 %shard_map.110.w_other = bf16[864,5120]{1,0:T(8,128)(2,1)S(1)} custom-call(s32[19]{0:T(128)S(1)} %pad_add_fusion.place, bf16[1728,5120]{1,0:T(8,128)(2,1)} %refs_0_.7), custom_call_target="tpu_custom_call" | custom-call | tf_op jit(solution)/shard_map/pallas_call | solution.py:143
  94.0 1.8 %collective-permute-start.29 = (bf16[128,640]{1,0:T(8,128)(2,1)S(1)}, bf16[128,640]{1,0:T(8,128)(2,1)S(1)}, u32[]{:S(2)}, u32[]{:S(2)}) collective-permute-start(bf16[128,640]{1,0:T(8,128)(2,1)S(1)} %shard_map.116), channel_id=1, source_target_pairs={{0,2},{2,0},{4,6},{6,4},{8,10},{10,8},{12,14},{14,12},{1,3},{3,1},... | collective-permute-start | bytes 491528 | tf_op jit(solution)/shard_map/ppermute | solution.py:115
  95.8 1.6 %shard_map.112 = (f32[128,640]{1,0:T(8,128)S(1)}, bf16[128,640]{1,0:T(8,128)(2,1)S(1)}) custom-call(s32[19]{0:T(128)S(1)} %pad_add_fusion.place, bf16[128,864]{1,0:T(8,128)(2,1)S(1)} %get-tuple-element.44.own, bf16[128,864]{1,0:T(8,128)(2,1)S(1)} %collective-permute-done.24.other, bf16[864,5120]{1,0:T(8,128)(2,1)S(1)} %shard_map.109.w_own, ...), custom_call_target="tpu_custom_call" | custom-call | tf_op jit(solution)/shard_map/pallas_call | solution.py:98
  97.7 1.6 %shard_map.114 = (f32[128,640]{1,0:T(8,128)S(1)}, bf16[128,640]{1,0:T(8,128)(2,1)S(1)}) custom-call(s32[19]{0:T(128)S(1)} %pad_add_fusion.place, bf16[128,864]{1,0:T(8,128)(2,1)S(1)} %get-tuple-element.44.own, bf16[128,864]{1,0:T(8,128)(2,1)S(1)} %collective-permute-done.24.other, bf16[864,5120]{1,0:T(8,128)(2,1)S(1)} %shard_map.109.w_own, ...), custom_call_target="tpu_custom_call" | custom-call | tf_op jit(solution)/shard_map/pallas_call | solution.py:98
  99.3 1.8 %collective-permute-start.28 = (bf16[128,640]{1,0:T(8,128)(2,1)S(1)}, bf16[128,640]{1,0:T(8,128)(2,1)S(1)}, u32[]{:S(2)}, u32[]{:S(2)}) collective-permute-start(bf16[128,640]{1,0:T(8,128)(2,1)S(1)} %get-tuple-element.51), channel_id=1, source_target_pairs={{0,2},{2,0},{4,6},{6,4},{8,10},{10,8},{12,14},{14,12},{1,3},{3,1},... | collective-permute-start | bytes 491528 | tf_op jit(solution)/shard_map/ppermute | solution.py:115
  101.2 2.0 %shard_map.111 = (f32[128,640]{1,0:T(8,128)S(1)}, bf16[128,640]{1,0:T(8,128)(2,1)S(1)}, f32[128,640]{1,0:T(8,128)S(1)}) custom-call(s32[19]{0:T(128)S(1)} %pad_add_fusion.place, bf16[128,864]{1,0:T(8,128)(2,1)S(1)} %get-tuple-element.44.own, bf16[128,864]{1,0:T(8,128)(2,1)S(1)} %collective-permute-done.24.other, bf16[864,5120]{1,0:T(8,128)(2,1)S(1)} %shard_map.109.w_own, ...), custom_call_target="tpu_custom_call" | custom-call | tf_op jit(solution)/shard_map/pallas_call | solution.py:98
  103.2 1.8 %collective-permute-start.25 = (bf16[128,640]{1,0:T(8,128)(2,1)S(1)}, bf16[128,640]{1,0:T(8,128)(2,1)S(1)}, u32[]{:S(2)}, u32[]{:S(2)}) collective-permute-start(bf16[128,640]{1,0:T(8,128)(2,1)S(1)} %get-tuple-element.47), channel_id=1, source_target_pairs={{0,2},{2,0},{4,6},{6,4},{8,10},{10,8},{12,14},{14,12},{1,3},{3,1},... | collective-permute-start | bytes 491528 | tf_op jit(solution)/shard_map/ppermute | solution.py:115
  105.1 2.1 %collective-permute-start.27 = (bf16[128,640]{1,0:T(8,128)(2,1)S(1)}, bf16[128,640]{1,0:T(8,128)(2,1)S(1)}, u32[]{:S(2)}, u32[]{:S(2)}) collective-permute-start(bf16[128,640]{1,0:T(8,128)(2,1)S(1)} %shard_map.113), channel_id=1, source_target_pairs={{0,4},{2,6},{4,0},{6,2},{8,12},{10,14},{12,8},{14,10},{1,5},{3,7},... | collective-permute-start | bytes 491528 | tf_op jit(solution)/shard_map/ppermute | solution.py:115
  108.1 2.1 %collective-permute-start.31 = (bf16[128,640]{1,0:T(8,128)(2,1)S(1)}, bf16[128,640]{1,0:T(8,128)(2,1)S(1)}, u32[]{:S(2)}, u32[]{:S(2)}) collective-permute-start(bf16[128,640]{1,0:T(8,128)(2,1)S(1)} %shard_map.118), channel_id=1, source_target_pairs={{0,8},{2,10},{4,12},{6,14},{8,0},{10,2},{12,4},{14,6},{1,9},{3,11}... | collective-permute-start | bytes 491528 | tf_op jit(solution)/shard_map/ppermute | solution.py:115
  111.4 5.7 %collective-permute-done.31.refs_2_ = bf16[128,640]{1,0:T(8,128)(2,1)S(1)} collective-permute-done((bf16[128,640]{1,0:T(8,128)(2,1)S(1)}, bf16[128,640]{1,0:T(8,128)(2,1)S(1)}, u32[]{:S(2)}, u32[]{:S(2)}) %collective-permute-start.31) | collective-permute-done | bytes 163872 | tf_op jit(solution)/shard_map/ppermute | solution.py:115
  (59 shorter events, 18.4 us)
Async XLA Ops:
  1.0 15.5 %collective-permute-start.3 = (bf16[192,640]{1,0:T(8,128)(2,1)S(1)}, bf16[192,640]{1,0:T(8,128)(2,1)S(1)}, u32[]{:S(2)}, u32[]{:S(2)}) collective-permute-start(bf16[192,640]{1,0:T(8,128)(2,1)S(1)} %stack.13.refs_0_), channel_id=1, source_target_pairs={{0,8},{2,10},{4,12},{6,14},{8,0},{10,2},{12,4},{14,6},{1,9},{3,11}... | collective-permute-start | bytes 737288 | tf_op jit(solution)/shard_map/ppermute | solution.py:115
  5.1 14.0 %collective-permute-start.1 = (bf16[192,640]{1,0:T(8,128)(2,1)S(1)}, bf16[192,640]{1,0:T(8,128)(2,1)S(1)}, u32[]{:S(2)}, u32[]{:S(2)}) collective-permute-start(bf16[192,640]{1,0:T(8,128)(2,1)S(1)} %stack.13.refs_0_), channel_id=1, source_target_pairs={{0,4},{2,6},{4,0},{6,2},{8,12},{10,14},{12,8},{14,10},{1,5},{3,7},... | collective-permute-start | bytes 737288 | tf_op jit(solution)/shard_map/ppermute | solution.py:115
  16.5 8.8 %collective-permute-start.4 = (bf16[192,640]{1,0:T(8,128)(2,1)S(1)}, bf16[192,640]{1,0:T(8,128)(2,1)S(1)}, u32[]{:S(2)}, u32[]{:S(2)}) collective-permute-start(bf16[192,640]{1,0:T(8,128)(2,1)S(1)} %collective-permute-done.3.refs_4_), channel_id=1, source_target_pairs={{0,2},{2,0},{4,6},{6,4},{8,10},{10,8},{12,14},{14,12},{1,3},{3,1},... | collective-permute-start | bytes 737288 | tf_op jit(solution)/shard_map/ppermute | solution.py:115
  18.0 12.5 %collective-permute-start = (bf16[192,640]{1,0:T(8,128)(2,1)S(1)}, bf16[192,640]{1,0:T(8,128)(2,1)S(1)}, u32[]{:S(2)}, u32[]{:S(2)}) collective-permute-start(bf16[192,640]{1,0:T(8,128)(2,1)S(1)} %stack.13.refs_0_), channel_id=1, source_target_pairs={{0,2},{2,0},{4,6},{6,4},{8,10},{10,8},{12,14},{14,12},{1,3},{3,1},... | collective-permute-start | bytes 737288 | tf_op jit(solution)/shard_map/ppermute | solution.py:115
  18.5 12.1 %collective-permute-start.5 = (bf16[192,640]{1,0:T(8,128)(2,1)S(1)}, bf16[192,640]{1,0:T(8,128)(2,1)S(1)}, u32[]{:S(2)}, u32[]{:S(2)}) collective-permute-start(bf16[192,640]{1,0:T(8,128)(2,1)S(1)} %collective-permute-done.3.refs_4_), channel_id=1, source_target_pairs={{0,4},{2,6},{4,0},{6,2},{8,12},{10,14},{12,8},{14,10},{1,5},{3,7},... | collective-permute-start | bytes 737288 | tf_op jit(solution)/shard_map/ppermute | solution.py:115
  19.1 14.9 %collective-permute-start.2 = (bf16[192,640]{1,0:T(8,128)(2,1)S(1)}, bf16[192,640]{1,0:T(8,128)(2,1)S(1)}, u32[]{:S(2)}, u32[]{:S(2)}) collective-permute-start(bf16[192,640]{1,0:T(8,128)(2,1)S(1)} %collective-permute-done.1.refs_2_), channel_id=1, source_target_pairs={{0,2},{2,0},{4,6},{6,4},{8,10},{10,8},{12,14},{14,12},{1,3},{3,1},... | collective-permute-start | bytes 737288 | tf_op jit(solution)/shard_map/ppermute | solution.py:115
  25.3 8.8 %collective-permute-start.6 = (bf16[192,640]{1,0:T(8,128)(2,1)S(1)}, bf16[192,640]{1,0:T(8,128)(2,1)S(1)}, u32[]{:S(2)}, u32[]{:S(2)}) collective-permute-start(bf16[192,640]{1,0:T(8,128)(2,1)S(1)} %collective-permute-done.4.refs_5_), channel_id=1, source_target_pairs={{0,4},{2,6},{4,0},{6,2},{8,12},{10,14},{12,8},{14,10},{1,5},{3,7},... | collective-permute-start | bytes 737288 | tf_op jit(solution)/shard_map/ppermute | solution.py:115
  37.6 1.7 %collective-permute-start.7 = (bf16[640,256]{1,0:T(8,128)(2,1)S(1)}, bf16[640,256]{1,0:T(8,128)(2,1)S(1)}, u32[]{:S(2)}, u32[]{:S(2)}) collective-permute-start(bf16[640,256]{1,0:T(8,128)(2,1)S(1)} %get-tuple-element.30), channel_id=1, source_target_pairs={{0,1},{1,0},{2,3},{3,2},{4,5},{5,4},{6,7},{7,6},{8,9},{9,8},{10,11... | collective-permute-start | bytes 983048 | tf_op jit(solution)/shard_map/ppermute | solution.py:334
  39.4 6.3 %collective-permute-start.8 = (bf16[640,128]{1,0:T(8,128)(2,1)S(1)}, bf16[640,128]{1,0:T(8,128)(2,1)S(1)}, u32[]{:S(2)}, u32[]{:S(2)}) collective-permute-start(bf16[640,128]{1,0:T(8,128)(2,1)S(1)} %get-tuple-element.32), channel_id=1, source_target_pairs={{0,16},{16,0},{1,17},{17,1},{2,18},{18,2},{3,19},{19,3},{4,20},{20... | collective-permute-start | bytes 491528 | tf_op jit(solution)/shard_map/ppermute | solution.py:338
  47.6 10.1 %collective-permute-start.11 = (bf16[656,128]{1,0:T(8,128)(2,1)S(1)}, bf16[656,128]{1,0:T(8,128)(2,1)S(1)}, u32[]{:S(2)}, u32[]{:S(2)}) collective-permute-start(bf16[656,128]{1,0:T(8,128)(2,1)S(1)} %get-tuple-element.34.refs_0_), channel_id=1, source_target_pairs={{0,8},{2,10},{4,12},{6,14},{8,0},{10,2},{12,4},{14,6},{1,9},{3,11}... | collective-permute-start | bytes 503816 | tf_op jit(solution)/shard_map/ppermute | solution.py:115
  47.7 11.4 %collective-permute-start.21 = (bf16[656,128]{1,0:T(8,128)(2,1)S(1)}, bf16[656,128]{1,0:T(8,128)(2,1)S(1)}, u32[]{:S(2)}, u32[]{:S(2)}) collective-permute-start(bf16[656,128]{1,0:T(8,128)(2,1)S(1)} %get-tuple-element.34.refs_0_), channel_id=1, source_target_pairs={{0,2},{2,0},{4,6},{6,4},{8,10},{10,8},{12,14},{14,12},{1,3},{3,1},... | collective-permute-start | bytes 503816 | tf_op jit(solution)/shard_map/ppermute | solution.py:115
  49.0 10.0 %collective-permute-start.9 = (bf16[656,128]{1,0:T(8,128)(2,1)S(1)}, bf16[656,128]{1,0:T(8,128)(2,1)S(1)}, u32[]{:S(2)}, u32[]{:S(2)}) collective-permute-start(bf16[656,128]{1,0:T(8,128)(2,1)S(1)} %get-tuple-element.34.refs_0_), channel_id=1, source_target_pairs={{0,4},{2,6},{4,0},{6,2},{8,12},{10,14},{12,8},{14,10},{1,5},{3,7},... | collective-permute-start | bytes 503816 | tf_op jit(solution)/shard_map/ppermute | solution.py:115
  54.0 5.7 %collective-permute-start.22 = (bf16[656,128]{1,0:T(8,128)(2,1)S(1)}, bf16[656,128]{1,0:T(8,128)(2,1)S(1)}, u32[]{:S(2)}, u32[]{:S(2)}) collective-permute-start(bf16[656,128]{1,0:T(8,128)(2,1)S(1)} %get-tuple-element.34.refs_0_), channel_id=1, source_target_pairs={{0,1},{1,0},{2,3},{3,2},{4,5},{5,4},{6,7},{7,6},{8,9},{9,8},{10,11... | collective-permute-start | bytes 503816 | tf_op jit(solution)/shard_map/ppermute | solution.py:349
  57.7 6.2 %collective-permute-start.12 = (bf16[656,128]{1,0:T(8,128)(2,1)S(1)}, bf16[656,128]{1,0:T(8,128)(2,1)S(1)}, u32[]{:S(2)}, u32[]{:S(2)}) collective-permute-start(bf16[656,128]{1,0:T(8,128)(2,1)S(1)} %collective-permute-done.11.refs_1_), channel_id=1, source_target_pairs={{0,2},{2,0},{4,6},{6,4},{8,10},{10,8},{12,14},{14,12},{1,3},{3,1},... | collective-permute-start | bytes 503816 | tf_op jit(solution)/shard_map/ppermute | solution.py:115
  59.0 4.9 %collective-permute-start.23 = (bf16[656,128]{1,0:T(8,128)(2,1)S(1)}, bf16[656,128]{1,0:T(8,128)(2,1)S(1)}, u32[]{:S(2)}, u32[]{:S(2)}) collective-permute-start(bf16[656,128]{1,0:T(8,128)(2,1)S(1)} %collective-permute-done.21.refs_1_), channel_id=1, source_target_pairs={{0,1},{1,0},{2,3},{3,2},{4,5},{5,4},{6,7},{7,6},{8,9},{9,8},{10,11... | collective-permute-start | bytes 503816 | tf_op jit(solution)/shard_map/ppermute | solution.py:349
  59.0 4.9 %collective-permute-start.19 = (bf16[656,128]{1,0:T(8,128)(2,1)S(1)}, bf16[656,128]{1,0:T(8,128)(2,1)S(1)}, u32[]{:S(2)}, u32[]{:S(2)}) collective-permute-start(bf16[656,128]{1,0:T(8,128)(2,1)S(1)} %collective-permute-done.9.refs_0_), channel_id=1, source_target_pairs={{0,1},{1,0},{2,3},{3,2},{4,5},{5,4},{6,7},{7,6},{8,9},{9,8},{10,11... | collective-permute-start | bytes 503816 | tf_op jit(solution)/shard_map/ppermute | solution.py:349
  59.5 7.2 %collective-permute-start.16 = (bf16[656,128]{1,0:T(8,128)(2,1)S(1)}, bf16[656,128]{1,0:T(8,128)(2,1)S(1)}, u32[]{:S(2)}, u32[]{:S(2)}) collective-permute-start(bf16[656,128]{1,0:T(8,128)(2,1)S(1)} %collective-permute-done.11.refs_1_), channel_id=1, source_target_pairs={{0,4},{2,6},{4,0},{6,2},{8,12},{10,14},{12,8},{14,10},{1,5},{3,7},... | collective-permute-start | bytes 503816 | tf_op jit(solution)/shard_map/ppermute | solution.py:115
  59.6 7.1 %collective-permute-start.10 = (bf16[656,128]{1,0:T(8,128)(2,1)S(1)}, bf16[656,128]{1,0:T(8,128)(2,1)S(1)}, u32[]{:S(2)}, u32[]{:S(2)}) collective-permute-start(bf16[656,128]{1,0:T(8,128)(2,1)S(1)} %collective-permute-done.9.refs_0_), channel_id=1, source_target_pairs={{0,2},{2,0},{4,6},{6,4},{8,10},{10,8},{12,14},{14,12},{1,3},{3,1},... | collective-permute-start | bytes 503816 | tf_op jit(solution)/shard_map/ppermute | solution.py:115
  63.9 5.5 %collective-permute-start.13 = (bf16[656,128]{1,0:T(8,128)(2,1)S(1)}, bf16[656,128]{1,0:T(8,128)(2,1)S(1)}, u32[]{:S(2)}, u32[]{:S(2)}) collective-permute-start(bf16[656,128]{1,0:T(8,128)(2,1)S(1)} %collective-permute-done.12.refs_0_), channel_id=1, source_target_pairs={{0,4},{2,6},{4,0},{6,2},{8,12},{10,14},{12,8},{14,10},{1,5},{3,7},... | collective-permute-start | bytes 503816 | tf_op jit(solution)/shard_map/ppermute | solution.py:115
  63.9 14.0 %collective-permute-start.20 = (bf16[656,128]{1,0:T(8,128)(2,1)S(1)}, bf16[656,128]{1,0:T(8,128)(2,1)S(1)}, u32[]{:S(2)}, u32[]{:S(2)}) collective-permute-start(bf16[656,128]{1,0:T(8,128)(2,1)S(1)} %collective-permute-done.11.refs_1_), channel_id=1, source_target_pairs={{0,1},{1,0},{2,3},{3,2},{4,5},{5,4},{6,7},{7,6},{8,9},{9,8},{10,11... | collective-permute-start | bytes 503816 | tf_op jit(solution)/shard_map/ppermute | solution.py:349
  64.0 15.9 %collective-permute-start.17 = (bf16[656,128]{1,0:T(8,128)(2,1)S(1)}, bf16[656,128]{1,0:T(8,128)(2,1)S(1)}, u32[]{:S(2)}, u32[]{:S(2)}) collective-permute-start(bf16[656,128]{1,0:T(8,128)(2,1)S(1)} %collective-permute-done.12.refs_0_), channel_id=1, source_target_pairs={{0,1},{1,0},{2,3},{3,2},{4,5},{5,4},{6,7},{7,6},{8,9},{9,8},{10,11... | collective-permute-start | bytes 503816 | tf_op jit(solution)/shard_map/ppermute | solution.py:349
  66.7 13.2 %collective-permute-start.18 = (bf16[656,128]{1,0:T(8,128)(2,1)S(1)}, bf16[656,128]{1,0:T(8,128)(2,1)S(1)}, u32[]{:S(2)}, u32[]{:S(2)}) collective-permute-start(bf16[656,128]{1,0:T(8,128)(2,1)S(1)} %collective-permute-done.16.refs_1_), channel_id=1, source_target_pairs={{0,1},{1,0},{2,3},{3,2},{4,5},{5,4},{6,7},{7,6},{8,9},{9,8},{10,11... | collective-permute-start | bytes 503816 | tf_op jit(solution)/shard_map/ppermute | solution.py:349
  66.7 15.2 %collective-permute-start.14 = (bf16[656,128]{1,0:T(8,128)(2,1)S(1)}, bf16[656,128]{1,0:T(8,128)(2,1)S(1)}, u32[]{:S(2)}, u32[]{:S(2)}) collective-permute-start(bf16[656,128]{1,0:T(8,128)(2,1)S(1)} %collective-permute-done.10.refs_0_), channel_id=1, source_target_pairs={{0,1},{1,0},{2,3},{3,2},{4,5},{5,4},{6,7},{7,6},{8,9},{9,8},{10,11... | collective-permute-start | bytes 503816 | tf_op jit(solution)/shard_map/ppermute | solution.py:349
  69.4 12.5 %collective-permute-start.15 = (bf16[656,128]{1,0:T(8,128)(2,1)S(1)}, bf16[656,128]{1,0:T(8,128)(2,1)S(1)}, u32[]{:S(2)}, u32[]{:S(2)}) collective-permute-start(bf16[656,128]{1,0:T(8,128)(2,1)S(1)} %collective-permute-done.13.refs_1_), channel_id=1, source_target_pairs={{0,1},{1,0},{2,3},{3,2},{4,5},{5,4},{6,7},{7,6},{8,9},{9,8},{10,11... | collective-permute-start | bytes 503816 | tf_op jit(solution)/shard_map/ppermute | solution.py:349
  84.1 8.7 %collective-permute-start.24 = (bf16[128,864]{1,0:T(8,128)(2,1)S(1)}, bf16[128,864]{1,0:T(8,128)(2,1)S(1)}, u32[]{:S(2)}, u32[]{:S(2)}) collective-permute-start(bf16[128,864]{1,0:T(8,128)(2,1)S(1)} %get-tuple-element.45), channel_id=1, source_target_pairs={{0,1},{1,0},{2,3},{3,2},{4,5},{5,4},{6,7},{7,6},{8,9},{9,8},{10,11... | collective-permute-start | bytes 663560 | tf_op jit(solution)/shard_map/ppermute | solution.py:349
  94.0 7.1 %collective-permute-start.29 = (bf16[128,640]{1,0:T(8,128)(2,1)S(1)}, bf16[128,640]{1,0:T(8,128)(2,1)S(1)}, u32[]{:S(2)}, u32[]{:S(2)}) collective-permute-start(bf16[128,640]{1,0:T(8,128)(2,1)S(1)} %shard_map.116), channel_id=1, source_target_pairs={{0,2},{2,0},{4,6},{6,4},{8,10},{10,8},{12,14},{14,12},{1,3},{3,1},... | collective-permute-start | bytes 491528 | tf_op jit(solution)/shard_map/ppermute | solution.py:115
  97.4 7.7 %collective-permute-start.26 = (bf16[128,640]{1,0:T(8,128)(2,1)S(1)}, bf16[128,640]{1,0:T(8,128)(2,1)S(1)}, u32[]{:S(2)}, u32[]{:S(2)}) collective-permute-start(bf16[128,640]{1,0:T(8,128)(2,1)S(1)} %get-tuple-element.49), channel_id=1, source_target_pairs={{0,2},{2,0},{4,6},{6,4},{8,10},{10,8},{12,14},{14,12},{1,3},{3,1},... | collective-permute-start | bytes 491528 | tf_op jit(solution)/shard_map/ppermute | solution.py:115
  99.3 8.8 %collective-permute-start.28 = (bf16[128,640]{1,0:T(8,128)(2,1)S(1)}, bf16[128,640]{1,0:T(8,128)(2,1)S(1)}, u32[]{:S(2)}, u32[]{:S(2)}) collective-permute-start(bf16[128,640]{1,0:T(8,128)(2,1)S(1)} %get-tuple-element.51), channel_id=1, source_target_pairs={{0,2},{2,0},{4,6},{6,4},{8,10},{10,8},{12,14},{14,12},{1,3},{3,1},... | collective-permute-start | bytes 491528 | tf_op jit(solution)/shard_map/ppermute | solution.py:115
  101.2 6.9 %collective-permute-start.30 = (bf16[128,640]{1,0:T(8,128)(2,1)S(1)}, bf16[128,640]{1,0:T(8,128)(2,1)S(1)}, u32[]{:S(2)}, u32[]{:S(2)}) collective-permute-start(bf16[128,640]{1,0:T(8,128)(2,1)S(1)} %shard_map.117), channel_id=1, source_target_pairs={{0,4},{2,6},{4,0},{6,2},{8,12},{10,14},{12,8},{14,10},{1,5},{3,7},... | collective-permute-start | bytes 491528 | tf_op jit(solution)/shard_map/ppermute | solution.py:115
  103.2 7.5 %collective-permute-start.25 = (bf16[128,640]{1,0:T(8,128)(2,1)S(1)}, bf16[128,640]{1,0:T(8,128)(2,1)S(1)}, u32[]{:S(2)}, u32[]{:S(2)}) collective-permute-start(bf16[128,640]{1,0:T(8,128)(2,1)S(1)} %get-tuple-element.47), channel_id=1, source_target_pairs={{0,2},{2,0},{4,6},{6,4},{8,10},{10,8},{12,14},{14,12},{1,3},{3,1},... | collective-permute-start | bytes 491528 | tf_op jit(solution)/shard_map/ppermute | solution.py:115
  105.1 6.3 %collective-permute-start.27 = (bf16[128,640]{1,0:T(8,128)(2,1)S(1)}, bf16[128,640]{1,0:T(8,128)(2,1)S(1)}, u32[]{:S(2)}, u32[]{:S(2)}) collective-permute-start(bf16[128,640]{1,0:T(8,128)(2,1)S(1)} %shard_map.113), channel_id=1, source_target_pairs={{0,4},{2,6},{4,0},{6,2},{8,12},{10,14},{12,8},{14,10},{1,5},{3,7},... | collective-permute-start | bytes 491528 | tf_op jit(solution)/shard_map/ppermute | solution.py:115
  108.1 9.1 %collective-permute-start.31 = (bf16[128,640]{1,0:T(8,128)(2,1)S(1)}, bf16[128,640]{1,0:T(8,128)(2,1)S(1)}, u32[]{:S(2)}, u32[]{:S(2)}) collective-permute-start(bf16[128,640]{1,0:T(8,128)(2,1)S(1)} %shard_map.118), channel_id=1, source_target_pairs={{0,8},{2,10},{4,12},{6,14},{8,0},{10,2},{12,4},{14,6},{1,9},{3,11}... | collective-permute-start | bytes 491528 | tf_op jit(solution)/shard_map/ppermute | solution.py:115
  (2 other events, 2.1 us)

commit v4 on v3

--- a/solution.py
+++ b/solution.py
@@ -12,6 +12,7 @@
 LOG2E = 1.4426950408889634
 MIB = 1 << 20
 SEQ = 8
+PRE = (7, 6, 3)
 SHARES = ((0, 1), (2, 4), (5, 6), (3, 7))
 VMEM = pl.BlockSpec(memory_space=pltpu.VMEM)
 HBM = pl.BlockSpec(memory_space=pltpu.MemorySpace.HBM)
@@ -279,23 +280,31 @@
     return body
 
 
-def down_body(offsets, columns):
-    def body(place, own, other, w_own, w_other, *outs):
-        for r, out in zip(offsets, outs):
+def down_body(offsets, columns, parts):
+    def body(place, *refs):
+        hidden, weights, refs = refs[:parts], refs[parts : 2 * parts], refs[2 * parts :]
+        outs, given = refs[-len(offsets) :], refs[: -len(offsets)]
+        for i, (r, out) in enumerate(zip(offsets, outs)):
             at = pl.ds(pl.multiple_of((place[0] ^ r) * columns, 128), columns)
-            total = jnp.dot(own[...], w_own[:, at], preferred_element_type=jnp.float32)
-            total = total + jnp.dot(other[...], w_other[:, at], preferred_element_type=jnp.float32)
+            total = given[i][...] if given else None
+            for units, weight in zip(hidden, weights):
+                part = jnp.dot(units[...], weight[:, at], preferred_element_type=jnp.float32)
+                total = part if total is None else total + part
             out[...] = total.astype(out.dtype)
 
     return body
 
 
-def turn_body(x, out):
+def turn_body(x, gain, out, gain_wide):
     out[...] = x[...].T
-
-
-def add_body(mine, got, out):
-    out[...] = (mine[...].astype(jnp.float32) + got[...].astype(jnp.float32)).astype(out.dtype)
+    gain_wide[...] = jnp.broadcast_to(gain[...].astype(jnp.float32), gain_wide.shape[::-1]).T
+
+
+def add_body(*refs):
+    total = refs[0][...].astype(jnp.float32)
+    for ref in refs[1:-1]:
+        total = total + ref[...].astype(jnp.float32)
+    refs[-1][...] = total.astype(refs[-1].dtype)
 
 
 def finish_body(carried, mine, *refs):
@@ -322,7 +331,12 @@
     mine, theirs = (lambda p: p[2] * share), (lambda p: (1 - p[2]) * share)
     w_gate_up = fetch(place, [w_gate, w_up], share, (mine, mine))
     w_down = [fetch(place, [w_down], share, (base,)) for base in (mine, theirs)]
-    wo_t = call(turn_body, struct(wo.shape[::-1], bf16), (wo,), limit=4)
+    wo_t, gain_wide = call(
+        turn_body,
+        (struct(wo.shape[::-1], bf16), struct((columns, group_tokens), f32)),
+        (wo, gain.reshape(1, columns)),
+        limit=4,
+    )
     send, keep = call(
         attend_body(n_seq, seq_dev, heads_features // HEAD_DIM, groups, reps),
         (struct((columns, tokens // 2), bf16), struct((columns, tokens // 2), f32)),
@@ -336,7 +350,6 @@
         halve_body, (struct((columns, group_tokens), bf16), struct((columns, group_tokens), f32)), (keep, got), limit=3
     )
     got = lax.ppermute(send, "section", [(0, 1), (1, 0)])
-    gain_wide = jnp.broadcast_to(gain.astype(f32)[:, None], (columns, group_tokens))
     carried, x = call(
         carry_body,
         (struct((columns, group_tokens), f32), struct((columns + 16, group_tokens), bf16)),
@@ -366,31 +379,45 @@
             aliases={} if first or last else {1 + 2 * n + 1 + j: j for j in range(3)},
         )
     hidden = (acc[0], over_rep(acc[1]))
+    block = (group_tokens, columns)
+    before = dict(
+        zip(
+            PRE,
+            call(
+                down_body(PRE, columns, 1),
+                (struct(block, f32),) * len(PRE),
+                (place, hidden[0], w_down[0]),
+                scalars=1,
+                limit=3,
+            ),
+        )
+    )
 
     def down(*offsets_types):
+        offsets = [r for r, _ in offsets_types]
+        given = [before[r] for r in offsets if r in before]
+        units = ((hidden[1], w_down[1]) if given else (*hidden, *w_down))
         return call(
-            down_body([r for r, _ in offsets_types], columns),
-            tuple(struct((group_tokens, columns), t) for _, t in offsets_types),
-            (place, *hidden, *w_down),
+            down_body(offsets, columns, len(units) // 2),
+            tuple(struct(block, t) for _, t in offsets_types),
+            (place, *units, *given),
             scalars=1,
             limit=3,
         )
 
-    def plus(mine, got):
-        return call(add_body, struct((group_tokens, columns), bf16), (mine, got), limit=3)
-
-    own, far = {}, {}
-    far[6], = down((7, bf16))
-    own[6], far[4] = down((6, f32), (5, bf16))
-    own[4], far[2] = down((4, f32), (3, bf16))
-    own[2], far[0], own[0] = down((2, f32), (1, bf16), (0, f32))
-    got = {r: swap(far[r], 1, n_seq) for r in (6, 4, 2, 0)}
-    sums = {6: plus(own[6], got[6])}
-    onward = swap(sums[6], 2, n_seq)
-    sums[2] = plus(own[2], got[2])
-    sums[4] = plus(plus(own[4], got[4]), onward)
-    parts = [got[0], swap(sums[2], 2, n_seq), swap(sums[4], 4, n_seq)]
-    out = call(finish_body, struct((columns, group_tokens), bf16), (carried, own[0], *parts), limit=3)
+    def plus(*terms):
+        return call(add_body, struct(block, bf16), terms, limit=3)
+
+    (p7,) = down((7, bf16))
+    p6, p3 = down((6, bf16), (3, bf16))
+    p5, p2 = down((5, f32), (2, f32))
+    p4, p1, p0 = down((4, f32), (1, bf16), (0, f32))
+    got7, got6, got3, got1 = (swap(p, offset, n_seq) for p, offset in ((p7, 2), (p6, 2), (p3, 1), (p1, 1)))
+    got5 = swap(plus(p5, got7), 1, n_seq)
+    got2 = swap(plus(p2, got3), 2, n_seq)
+    got4 = swap(plus(p4, got6, got5), 4, n_seq)
+    parts = (got1, got2, got4)
+    out = call(finish_body, struct((columns, group_tokens), bf16), (carried, p0, *parts), limit=3)
     return out.reshape(resid.shape)
 
 

time: 118 us -> 117 us (level)
  starting transfers between devices: 32.5 us -> 31.3 us
    ppermute x21, starting transfers between devices: 29 us -> 27.7 us  [swap(): return lax.ppermute(x, 'seq', [(i, i ^ offset) for i in range(n_seq)])]
  transfers between devices with their start and end apart: 32 -> 32, of which waited for: 14 -> 15; matrix products, arithmetic and copies ran while one was open for 1% -> 1% of each run, Pallas kernels for 22% -> 23%
where the time goes in v4:
time: 117 us
  waiting for transfers between devices  45.8 us (39%)
  Pallas kernels  36 us (31%)
  starting transfers between devices  31.3 us (27%)
  local copies, waits for them, and re-layouts  2.74 us (2%)
    ppermute x21, waiting for transfers between devices, swap(): return lax.ppermute(x, 'seq', [(i, i ^ offset) for i in range(n_seq)])  39.2 us
    ppermute x21, starting transfers between devices, swap(): return lax.ppermute(x, 'seq', [(i, i ^ offset) for i in range(n_seq)])  27.7 us
    pallas_call x17, Pallas kernels, call(): pl.pallas_call(body, out_shape=outs, in_specs=spaces, out_specs=jax.tree....  20.3 us
    pallas_call x3, Pallas kernels, fetch(): pl.pallas_call(body, out_shape=pltpu.VMEM((n * rows, width), arrays[0].dt...  14.7 us
    ppermute x1, waiting for transfers between devices, exchanged(): got = lax.ppermute(send, 'section', [(0, 1), (1, 0)])  4.95 us
  transfers between devices with their start and end apart: 32, of which 15 were waited for; matrix products, arithmetic and copies ran while one was open for 1% of the time, Pallas kernels for 23%

profile of v4, /device:TPU:0, one launch (start us, length us, event | category | flops | bytes accessed | tf_op | source)
XLA Modules:
  0.0 116.8 jit_solution(12044053352538835518)
XLA Ops:
  1.0 4.1 %collective-permute-start.3 = (bf16[192,640]{1,0:T(8,128)(2,1)S(1)}, bf16[192,640]{1,0:T(8,128)(2,1)S(1)}, u32[]{:S(2)}, u32[]{:S(2)}) collective-permute-start(bf16[192,640]{1,0:T(8,128)(2,1)S(1)} %stack.13.refs_0_), channel_id=1, source_target_pairs={{0,8},{2,10},{4,12},{6,14},{8,0},{10,2},{12,4},{14,6},{1,9},{3,11}... | collective-permute-start | bytes 737288 | tf_op jit(solution)/shard_map/ppermute | solution.py:116
  5.1 1.6 %collective-permute-start.1 = (bf16[192,640]{1,0:T(8,128)(2,1)S(1)}, bf16[192,640]{1,0:T(8,128)(2,1)S(1)}, u32[]{:S(2)}, u32[]{:S(2)}) collective-permute-start(bf16[192,640]{1,0:T(8,128)(2,1)S(1)} %stack.13.refs_0_), channel_id=1, source_target_pairs={{0,4},{2,6},{4,0},{6,2},{8,12},{10,14},{12,8},{14,10},{1,5},{3,7},... | collective-permute-start | bytes 737288 | tf_op jit(solution)/shard_map/ppermute | solution.py:116
  6.7 9.7 %collective-permute-done.3.refs_4_ = bf16[192,640]{1,0:T(8,128)(2,1)S(1)} collective-permute-done((bf16[192,640]{1,0:T(8,128)(2,1)S(1)}, bf16[192,640]{1,0:T(8,128)(2,1)S(1)}, u32[]{:S(2)}, u32[]{:S(2)}) %collective-permute-start.3) | collective-permute-done | bytes 245792 | tf_op jit(solution)/shard_map/ppermute | solution.py:116
  16.5 1.6 %collective-permute-start.4 = (bf16[192,640]{1,0:T(8,128)(2,1)S(1)}, bf16[192,640]{1,0:T(8,128)(2,1)S(1)}, u32[]{:S(2)}, u32[]{:S(2)}) collective-permute-start(bf16[192,640]{1,0:T(8,128)(2,1)S(1)} %collective-permute-done.3.refs_4_), channel_id=1, source_target_pairs={{0,2},{2,0},{4,6},{6,4},{8,10},{10,8},{12,14},{14,12},{1,3},{3,1},... | collective-permute-start | bytes 737288 | tf_op jit(solution)/shard_map/ppermute | solution.py:116
  19.1 1.5 %collective-permute-start.2 = (bf16[192,640]{1,0:T(8,128)(2,1)S(1)}, bf16[192,640]{1,0:T(8,128)(2,1)S(1)}, u32[]{:S(2)}, u32[]{:S(2)}) collective-permute-start(bf16[192,640]{1,0:T(8,128)(2,1)S(1)} %collective-permute-done.1.refs_2_), channel_id=1, source_target_pairs={{0,2},{2,0},{4,6},{6,4},{8,10},{10,8},{12,14},{14,12},{1,3},{3,1},... | collective-permute-start | bytes 737288 | tf_op jit(solution)/shard_map/ppermute | solution.py:116
  20.6 4.7 %collective-permute-done.4.refs_5_ = bf16[192,640]{1,0:T(8,128)(2,1)S(1)} collective-permute-done((bf16[192,640]{1,0:T(8,128)(2,1)S(1)}, bf16[192,640]{1,0:T(8,128)(2,1)S(1)}, u32[]{:S(2)}, u32[]{:S(2)}) %collective-permute-start.4) | collective-permute-done | bytes 245792 | tf_op jit(solution)/shard_map/ppermute | solution.py:116
  28.8 1.7 %collective-permute-done.refs_1_ = bf16[192,640]{1,0:T(8,128)(2,1)S(1)} collective-permute-done((bf16[192,640]{1,0:T(8,128)(2,1)S(1)}, bf16[192,640]{1,0:T(8,128)(2,1)S(1)}, u32[]{:S(2)}, u32[]{:S(2)}) %collective-permute-start) | collective-permute-done | bytes 245792 | tf_op jit(solution)/shard_map/ppermute | solution.py:116
  30.5 3.5 %collective-permute-done.2.refs_3_ = bf16[192,640]{1,0:T(8,128)(2,1)S(1)} collective-permute-done((bf16[192,640]{1,0:T(8,128)(2,1)S(1)}, bf16[192,640]{1,0:T(8,128)(2,1)S(1)}, u32[]{:S(2)}, u32[]{:S(2)}) %collective-permute-start.2) | collective-permute-done | bytes 245792 | tf_op jit(solution)/shard_map/ppermute | solution.py:116
  34.1 3.6 %shard_map.101 = (bf16[640,256]{1,0:T(8,128)(2,1)S(1)}, f32[640,256]{1,0:T(8,128)S(1)}) custom-call(s32[19]{0:T(128)S(1)} %pad_add_fusion.place, bf16[192,640]{1,0:T(8,128)(2,1)S(1)} %stack.13.refs_0_, bf16[192,640]{1,0:T(8,128)(2,1)S(1)} %collective-permute-done.refs_1_, bf16[192,640]{1,0:T(8,128)(2,1)S(1)} %collective-permute-done.1.refs_2_, ...), custom_call_target="tpu_custom_call" | custom-call | tf_op jit(solution)/shard_map/pallas_call | solution.py:99
  37.7 1.6 %collective-permute-done.7.got = bf16[640,256]{1,0:T(8,128)(2,1)S(1)} collective-permute-done((bf16[640,256]{1,0:T(8,128)(2,1)S(1)}, bf16[640,256]{1,0:T(8,128)(2,1)S(1)}, u32[]{:S(2)}, u32[]{:S(2)}) %collective-permute-start.7) | collective-permute-done | bytes 327712 | tf_op jit(solution)/shard_map/ppermute | solution.py:348
  40.8 5.0 %collective-permute-done.8.got = bf16[640,128]{1,0:T(8,128)(2,1)S(1)} collective-permute-done((bf16[640,128]{1,0:T(8,128)(2,1)S(1)}, bf16[640,128]{1,0:T(8,128)(2,1)S(1)}, u32[]{:S(2)}, u32[]{:S(2)}) %collective-permute-start.8) | collective-permute-done | bytes 163872 | tf_op jit(solution)/shard_map/ppermute | solution.py:352
  46.8 1.4 %collective-permute-start.21 = (bf16[656,128]{1,0:T(8,128)(2,1)S(1)}, bf16[656,128]{1,0:T(8,128)(2,1)S(1)}, u32[]{:S(2)}, u32[]{:S(2)}) collective-permute-start(bf16[656,128]{1,0:T(8,128)(2,1)S(1)} %get-tuple-element.41.refs_0_), channel_id=1, source_target_pairs={{0,2},{2,0},{4,6},{6,4},{8,10},{10,8},{12,14},{14,12},{1,3},{3,1},... | collective-permute-start | bytes 503816 | tf_op jit(solution)/shard_map/ppermute | solution.py:116
  48.2 4.9 %collective-permute-start.9 = (bf16[656,128]{1,0:T(8,128)(2,1)S(1)}, bf16[656,128]{1,0:T(8,128)(2,1)S(1)}, u32[]{:S(2)}, u32[]{:S(2)}) collective-permute-start(bf16[656,128]{1,0:T(8,128)(2,1)S(1)} %get-tuple-element.41.refs_0_), channel_id=1, source_target_pairs={{0,4},{2,6},{4,0},{6,2},{8,12},{10,14},{12,8},{14,10},{1,5},{3,7},... | collective-permute-start | bytes 503816 | tf_op jit(solution)/shard_map/ppermute | solution.py:116
  53.2 3.7 %collective-permute-done.11.refs_1_ = bf16[656,128]{1,0:T(8,128)(2,1)S(1)} collective-permute-done((bf16[656,128]{1,0:T(8,128)(2,1)S(1)}, bf16[656,128]{1,0:T(8,128)(2,1)S(1)}, u32[]{:S(2)}, u32[]{:S(2)}) %collective-permute-start.11) | collective-permute-done | bytes 167968 | tf_op jit(solution)/shard_map/ppermute | solution.py:116
  59.4 3.6 %collective-permute-done.12.refs_0_ = bf16[656,128]{1,0:T(8,128)(2,1)S(1)} collective-permute-done((bf16[656,128]{1,0:T(8,128)(2,1)S(1)}, bf16[656,128]{1,0:T(8,128)(2,1)S(1)}, u32[]{:S(2)}, u32[]{:S(2)}) %collective-permute-start.12) | collective-permute-done | bytes 167968 | tf_op jit(solution)/shard_map/ppermute | solution.py:116
  63.6 2.3 %collective-permute-done.16.refs_1_ = bf16[656,128]{1,0:T(8,128)(2,1)S(1)} collective-permute-done((bf16[656,128]{1,0:T(8,128)(2,1)S(1)}, bf16[656,128]{1,0:T(8,128)(2,1)S(1)}, u32[]{:S(2)}, u32[]{:S(2)}) %collective-permute-start.16) | collective-permute-done | bytes 167968 | tf_op jit(solution)/shard_map/ppermute | solution.py:116
  66.4 2.2 %collective-permute-done.13.refs_1_ = bf16[656,128]{1,0:T(8,128)(2,1)S(1)} collective-permute-done((bf16[656,128]{1,0:T(8,128)(2,1)S(1)}, bf16[656,128]{1,0:T(8,128)(2,1)S(1)}, u32[]{:S(2)}, u32[]{:S(2)}) %collective-permute-start.13) | collective-permute-done | bytes 167968 | tf_op jit(solution)/shard_map/ppermute | solution.py:116
  68.6 6.6 %shard_map.104.refs_4_ = bf16[1728,5120]{1,0:T(8,128)(2,1)S(1)} custom-call(s32[19]{0:T(128)S(1)} %pad_add_fusion.place, bf16[1728,5120]{1,0:T(8,128)(2,1)} %refs_0_.5, bf16[1728,5120]{1,0:T(8,128)(2,1)} %refs_1_.3), custom_call_target="tpu_custom_call" | custom-call | tf_op jit(solution)/shard_map/pallas_call | solution.py:144
  75.2 1.9 %shard_map.105 = (f32[864,256]{1,0:T(8,128)S(1)}, f32[864,256]{1,0:T(8,128)S(1)}, f32[8,256]{1,0:T(8,128)S(1)}) custom-call(s32[19]{0:T(128)S(1)} %pad_add_fusion.place, bf16[656,128]{1,0:T(8,128)(2,1)S(1)} %get-tuple-element.41.refs_0_, bf16[656,128]{1,0:T(8,128)(2,1)S(1)} %collective-permute-done.21.refs_1_, ...), custom_call_target="tpu_custom_call" | custom-call | tf_op jit(solution)/shard_map/pallas_call | solution.py:99
  77.1 2.0 %shard_map.106 = (f32[864,256]{1,0:T(8,128)S(1)}, f32[864,256]{1,0:T(8,128)S(1)}, f32[8,256]{1,0:T(8,128)S(1)}) custom-call(s32[19]{0:T(128)S(1)} %pad_add_fusion.place, bf16[656,128]{1,0:T(8,128)(2,1)S(1)} %collective-permute-done.9.refs_0_, ...), custom_call_target="tpu_custom_call", output_to_operand_aliasing={{0}: (6, {}), {1}: (7, {}), {2}: (8, {})} | custom-call | tf_op jit(solution)/shard_map/pallas_call | solution.py:99
  79.1 2.0 %shard_map.107 = (f32[864,256]{1,0:T(8,128)S(1)}, f32[864,256]{1,0:T(8,128)S(1)}, f32[8,256]{1,0:T(8,128)S(1)}) custom-call(s32[19]{0:T(128)S(1)} %pad_add_fusion.place, bf16[656,128]{1,0:T(8,128)(2,1)S(1)} %collective-permute-done.12.refs_0_, ...), custom_call_target="tpu_custom_call", output_to_operand_aliasing={{0}: (6, {}), {1}: (7, {}), {2}: (8, {})} | custom-call | tf_op jit(solution)/shard_map/pallas_call | solution.py:99
  81.1 2.2 %shard_map.108 = (bf16[128,864]{1,0:T(8,128)(2,1)S(1)}, bf16[128,864]{1,0:T(8,128)(2,1)S(1)}) custom-call(s32[19]{0:T(128)S(1)} %pad_add_fusion.place, bf16[656,128]{1,0:T(8,128)(2,1)S(1)} %collective-permute-done.10.refs_0_, bf16[656,128]{1,0:T(8,128)(2,1)S(1)} %collective-permute-done.13.refs_1_, bf16[656,128]{1,0:T(8,128)(2,1)S(1)} %collective-permute-done.14.refs_2_, ...), custom_call_target="tpu_custom_call" | custom-call | tf_op jit(solution)/shard_map/pallas_call | solution.py:99
  83.8 4.1 %shard_map.109.refs_2_.refs_1_ = bf16[864,5120]{1,0:T(8,128)(2,1)S(1)} custom-call(s32[19]{0:T(128)S(1)} %pad_add_fusion.place, bf16[1728,5120]{1,0:T(8,128)(2,1)} %refs_0_.7), custom_call_target="tpu_custom_call" | custom-call | tf_op jit(solution)/shard_map/pallas_call | solution.py:144
  87.9 4.1 %shard_map.110.refs_3_.refs_1_ = bf16[864,5120]{1,0:T(8,128)(2,1)S(1)} custom-call(s32[19]{0:T(128)S(1)} %pad_add_fusion.place, bf16[1728,5120]{1,0:T(8,128)(2,1)} %refs_0_.7), custom_call_target="tpu_custom_call" | custom-call | tf_op jit(solution)/shard_map/pallas_call | solution.py:144
  95.7 1.8 %collective-permute-start.28 = (bf16[128,640]{1,0:T(8,128)(2,1)S(1)}, bf16[128,640]{1,0:T(8,128)(2,1)S(1)}, u32[]{:S(2)}, u32[]{:S(2)}) collective-permute-start(bf16[128,640]{1,0:T(8,128)(2,1)S(1)} %get-tuple-element.60), channel_id=1, source_target_pairs={{0,4},{2,6},{4,0},{6,2},{8,12},{10,14},{12,8},{14,10},{1,5},{3,7},... | collective-permute-start | bytes 491528 | tf_op jit(solution)/shard_map/ppermute | solution.py:116
  97.6 1.8 %collective-permute-start.26 = (bf16[128,640]{1,0:T(8,128)(2,1)S(1)}, bf16[128,640]{1,0:T(8,128)(2,1)S(1)}, u32[]{:S(2)}, u32[]{:S(2)}) collective-permute-start(bf16[128,640]{1,0:T(8,128)(2,1)S(1)} %get-tuple-element.58), channel_id=1, source_target_pairs={{0,2},{2,0},{4,6},{6,4},{8,10},{10,8},{12,14},{14,12},{1,3},{3,1},... | collective-permute-start | bytes 491528 | tf_op jit(solution)/shard_map/ppermute | solution.py:116
  99.3 1.8 %shard_map.112 = (f32[128,640]{1,0:T(8,128)S(1)}, f32[128,640]{1,0:T(8,128)S(1)}) custom-call(s32[19]{0:T(128)S(1)} %pad_add_fusion.place, bf16[128,864]{1,0:T(8,128)(2,1)S(1)} %get-tuple-element.51.refs_0_, bf16[128,864]{1,0:T(8,128)(2,1)S(1)} %collective-permute-done.24.refs_1_.refs_0_, bf16[864,5120]{1,0:T(8,128)(2,1)S(1)} %shard_map.109.refs_2_.refs_1_, ...), custom_call_target="tpu_custom_call" | custom-call | tf_op jit(solution)/shard_map/pallas_call | solution.py:99
  101.4 1.8 %collective-permute-start.30 = (bf16[128,640]{1,0:T(8,128)(2,1)S(1)}, bf16[128,640]{1,0:T(8,128)(2,1)S(1)}, u32[]{:S(2)}, u32[]{:S(2)}) collective-permute-start(bf16[128,640]{1,0:T(8,128)(2,1)S(1)} %shard_map.117), channel_id=1, source_target_pairs={{0,2},{2,0},{4,6},{6,4},{8,10},{10,8},{12,14},{14,12},{1,3},{3,1},... | collective-permute-start | bytes 491528 | tf_op jit(solution)/shard_map/ppermute | solution.py:116
  103.3 2.0 %shard_map.111 = (f32[128,640]{1,0:T(8,128)S(1)}, bf16[128,640]{1,0:T(8,128)(2,1)S(1)}, f32[128,640]{1,0:T(8,128)S(1)}) custom-call(s32[19]{0:T(128)S(1)} %pad_add_fusion.place, bf16[128,864]{1,0:T(8,128)(2,1)S(1)} %get-tuple-element.51.refs_0_, bf16[128,864]{1,0:T(8,128)(2,1)S(1)} %collective-permute-done.24.refs_1_.refs_0_, ...), custom_call_target="tpu_custom_call" | custom-call | tf_op jit(solution)/shard_map/pallas_call | solution.py:99
  105.8 2.0 %collective-permute-done.30.refs_2_ = bf16[128,640]{1,0:T(8,128)(2,1)S(1)} collective-permute-done((bf16[128,640]{1,0:T(8,128)(2,1)S(1)}, bf16[128,640]{1,0:T(8,128)(2,1)S(1)}, u32[]{:S(2)}, u32[]{:S(2)}) %collective-permute-start.30) | collective-permute-done | bytes 163872 | tf_op jit(solution)/shard_map/ppermute | solution.py:116
  107.9 2.5 %collective-permute-start.31 = (bf16[128,640]{1,0:T(8,128)(2,1)S(1)}, bf16[128,640]{1,0:T(8,128)(2,1)S(1)}, u32[]{:S(2)}, u32[]{:S(2)}) collective-permute-start(bf16[128,640]{1,0:T(8,128)(2,1)S(1)} %shard_map.118), channel_id=1, source_target_pairs={{0,8},{2,10},{4,12},{6,14},{8,0},{10,2},{12,4},{14,6},{1,9},{3,11}... | collective-permute-start | bytes 491528 | tf_op jit(solution)/shard_map/ppermute | solution.py:116
  111.3 4.6 %collective-permute-done.31.refs_2_ = bf16[128,640]{1,0:T(8,128)(2,1)S(1)} collective-permute-done((bf16[128,640]{1,0:T(8,128)(2,1)S(1)}, bf16[128,640]{1,0:T(8,128)(2,1)S(1)}, u32[]{:S(2)}, u32[]{:S(2)}) %collective-permute-start.31) | collective-permute-done | bytes 163872 | tf_op jit(solution)/shard_map/ppermute | solution.py:116
  (59 shorter events, 18.9 us)
Async XLA Ops:
  1.0 15.5 %collective-permute-start.3 = (bf16[192,640]{1,0:T(8,128)(2,1)S(1)}, bf16[192,640]{1,0:T(8,128)(2,1)S(1)}, u32[]{:S(2)}, u32[]{:S(2)}) collective-permute-start(bf16[192,640]{1,0:T(8,128)(2,1)S(1)} %stack.13.refs_0_), channel_id=1, source_target_pairs={{0,8},{2,10},{4,12},{6,14},{8,0},{10,2},{12,4},{14,6},{1,9},{3,11}... | collective-permute-start | bytes 737288 | tf_op jit(solution)/shard_map/ppermute | solution.py:116
  5.1 14.0 %collective-permute-start.1 = (bf16[192,640]{1,0:T(8,128)(2,1)S(1)}, bf16[192,640]{1,0:T(8,128)(2,1)S(1)}, u32[]{:S(2)}, u32[]{:S(2)}) collective-permute-start(bf16[192,640]{1,0:T(8,128)(2,1)S(1)} %stack.13.refs_0_), channel_id=1, source_target_pairs={{0,4},{2,6},{4,0},{6,2},{8,12},{10,14},{12,8},{14,10},{1,5},{3,7},... | collective-permute-start | bytes 737288 | tf_op jit(solution)/shard_map/ppermute | solution.py:116
  16.5 8.8 %collective-permute-start.4 = (bf16[192,640]{1,0:T(8,128)(2,1)S(1)}, bf16[192,640]{1,0:T(8,128)(2,1)S(1)}, u32[]{:S(2)}, u32[]{:S(2)}) collective-permute-start(bf16[192,640]{1,0:T(8,128)(2,1)S(1)} %collective-permute-done.3.refs_4_), channel_id=1, source_target_pairs={{0,2},{2,0},{4,6},{6,4},{8,10},{10,8},{12,14},{14,12},{1,3},{3,1},... | collective-permute-start | bytes 737288 | tf_op jit(solution)/shard_map/ppermute | solution.py:116
  18.0 12.5 %collective-permute-start = (bf16[192,640]{1,0:T(8,128)(2,1)S(1)}, bf16[192,640]{1,0:T(8,128)(2,1)S(1)}, u32[]{:S(2)}, u32[]{:S(2)}) collective-permute-start(bf16[192,640]{1,0:T(8,128)(2,1)S(1)} %stack.13.refs_0_), channel_id=1, source_target_pairs={{0,2},{2,0},{4,6},{6,4},{8,10},{10,8},{12,14},{14,12},{1,3},{3,1},... | collective-permute-start | bytes 737288 | tf_op jit(solution)/shard_map/ppermute | solution.py:116
  18.5 12.1 %collective-permute-start.5 = (bf16[192,640]{1,0:T(8,128)(2,1)S(1)}, bf16[192,640]{1,0:T(8,128)(2,1)S(1)}, u32[]{:S(2)}, u32[]{:S(2)}) collective-permute-start(bf16[192,640]{1,0:T(8,128)(2,1)S(1)} %collective-permute-done.3.refs_4_), channel_id=1, source_target_pairs={{0,4},{2,6},{4,0},{6,2},{8,12},{10,14},{12,8},{14,10},{1,5},{3,7},... | collective-permute-start | bytes 737288 | tf_op jit(solution)/shard_map/ppermute | solution.py:116
  19.1 14.9 %collective-permute-start.2 = (bf16[192,640]{1,0:T(8,128)(2,1)S(1)}, bf16[192,640]{1,0:T(8,128)(2,1)S(1)}, u32[]{:S(2)}, u32[]{:S(2)}) collective-permute-start(bf16[192,640]{1,0:T(8,128)(2,1)S(1)} %collective-permute-done.1.refs_2_), channel_id=1, source_target_pairs={{0,2},{2,0},{4,6},{6,4},{8,10},{10,8},{12,14},{14,12},{1,3},{3,1},... | collective-permute-start | bytes 737288 | tf_op jit(solution)/shard_map/ppermute | solution.py:116
  25.3 8.8 %collective-permute-start.6 = (bf16[192,640]{1,0:T(8,128)(2,1)S(1)}, bf16[192,640]{1,0:T(8,128)(2,1)S(1)}, u32[]{:S(2)}, u32[]{:S(2)}) collective-permute-start(bf16[192,640]{1,0:T(8,128)(2,1)S(1)} %collective-permute-done.4.refs_5_), channel_id=1, source_target_pairs={{0,4},{2,6},{4,0},{6,2},{8,12},{10,14},{12,8},{14,10},{1,5},{3,7},... | collective-permute-start | bytes 737288 | tf_op jit(solution)/shard_map/ppermute | solution.py:116
  37.6 1.7 %collective-permute-start.7 = (bf16[640,256]{1,0:T(8,128)(2,1)S(1)}, bf16[640,256]{1,0:T(8,128)(2,1)S(1)}, u32[]{:S(2)}, u32[]{:S(2)}) collective-permute-start(bf16[640,256]{1,0:T(8,128)(2,1)S(1)} %get-tuple-element.36), channel_id=1, source_target_pairs={{0,1},{1,0},{2,3},{3,2},{4,5},{5,4},{6,7},{7,6},{8,9},{9,8},{10,11... | collective-permute-start | bytes 983048 | tf_op jit(solution)/shard_map/ppermute | solution.py:348
  39.4 6.3 %collective-permute-start.8 = (bf16[640,128]{1,0:T(8,128)(2,1)S(1)}, bf16[640,128]{1,0:T(8,128)(2,1)S(1)}, u32[]{:S(2)}, u32[]{:S(2)}) collective-permute-start(bf16[640,128]{1,0:T(8,128)(2,1)S(1)} %get-tuple-element.38), channel_id=1, source_target_pairs={{0,16},{16,0},{1,17},{17,1},{2,18},{18,2},{3,19},{19,3},{4,20},{20... | collective-permute-start | bytes 491528 | tf_op jit(solution)/shard_map/ppermute | solution.py:352
  46.8 10.1 %collective-permute-start.11 = (bf16[656,128]{1,0:T(8,128)(2,1)S(1)}, bf16[656,128]{1,0:T(8,128)(2,1)S(1)}, u32[]{:S(2)}, u32[]{:S(2)}) collective-permute-start(bf16[656,128]{1,0:T(8,128)(2,1)S(1)} %get-tuple-element.41.refs_0_), channel_id=1, source_target_pairs={{0,8},{2,10},{4,12},{6,14},{8,0},{10,2},{12,4},{14,6},{1,9},{3,11}... | collective-permute-start | bytes 503816 | tf_op jit(solution)/shard_map/ppermute | solution.py:116
  46.8 11.4 %collective-permute-start.21 = (bf16[656,128]{1,0:T(8,128)(2,1)S(1)}, bf16[656,128]{1,0:T(8,128)(2,1)S(1)}, u32[]{:S(2)}, u32[]{:S(2)}) collective-permute-start(bf16[656,128]{1,0:T(8,128)(2,1)S(1)} %get-tuple-element.41.refs_0_), channel_id=1, source_target_pairs={{0,2},{2,0},{4,6},{6,4},{8,10},{10,8},{12,14},{14,12},{1,3},{3,1},... | collective-permute-start | bytes 503816 | tf_op jit(solution)/shard_map/ppermute | solution.py:116
  48.2 10.0 %collective-permute-start.9 = (bf16[656,128]{1,0:T(8,128)(2,1)S(1)}, bf16[656,128]{1,0:T(8,128)(2,1)S(1)}, u32[]{:S(2)}, u32[]{:S(2)}) collective-permute-start(bf16[656,128]{1,0:T(8,128)(2,1)S(1)} %get-tuple-element.41.refs_0_), channel_id=1, source_target_pairs={{0,4},{2,6},{4,0},{6,2},{8,12},{10,14},{12,8},{14,10},{1,5},{3,7},... | collective-permute-start | bytes 503816 | tf_op jit(solution)/shard_map/ppermute | solution.py:116
  53.1 5.7 %collective-permute-start.22 = (bf16[656,128]{1,0:T(8,128)(2,1)S(1)}, bf16[656,128]{1,0:T(8,128)(2,1)S(1)}, u32[]{:S(2)}, u32[]{:S(2)}) collective-permute-start(bf16[656,128]{1,0:T(8,128)(2,1)S(1)} %get-tuple-element.41.refs_0_), channel_id=1, source_target_pairs={{0,1},{1,0},{2,3},{3,2},{4,5},{5,4},{6,7},{7,6},{8,9},{9,8},{10,11... | collective-permute-start | bytes 503816 | tf_op jit(solution)/shard_map/ppermute | solution.py:362
  56.9 6.2 %collective-permute-start.12 = (bf16[656,128]{1,0:T(8,128)(2,1)S(1)}, bf16[656,128]{1,0:T(8,128)(2,1)S(1)}, u32[]{:S(2)}, u32[]{:S(2)}) collective-permute-start(bf16[656,128]{1,0:T(8,128)(2,1)S(1)} %collective-permute-done.11.refs_1_), channel_id=1, source_target_pairs={{0,2},{2,0},{4,6},{6,4},{8,10},{10,8},{12,14},{14,12},{1,3},{3,1},... | collective-permute-start | bytes 503816 | tf_op jit(solution)/shard_map/ppermute | solution.py:116
  58.2 4.9 %collective-permute-start.23 = (bf16[656,128]{1,0:T(8,128)(2,1)S(1)}, bf16[656,128]{1,0:T(8,128)(2,1)S(1)}, u32[]{:S(2)}, u32[]{:S(2)}) collective-permute-start(bf16[656,128]{1,0:T(8,128)(2,1)S(1)} %collective-permute-done.21.refs_1_), channel_id=1, source_target_pairs={{0,1},{1,0},{2,3},{3,2},{4,5},{5,4},{6,7},{7,6},{8,9},{9,8},{10,11... | collective-permute-start | bytes 503816 | tf_op jit(solution)/shard_map/ppermute | solution.py:362
  58.2 4.9 %collective-permute-start.19 = (bf16[656,128]{1,0:T(8,128)(2,1)S(1)}, bf16[656,128]{1,0:T(8,128)(2,1)S(1)}, u32[]{:S(2)}, u32[]{:S(2)}) collective-permute-start(bf16[656,128]{1,0:T(8,128)(2,1)S(1)} %collective-permute-done.9.refs_0_), channel_id=1, source_target_pairs={{0,1},{1,0},{2,3},{3,2},{4,5},{5,4},{6,7},{7,6},{8,9},{9,8},{10,11... | collective-permute-start | bytes 503816 | tf_op jit(solution)/shard_map/ppermute | solution.py:362
  58.7 7.2 %collective-permute-start.16 = (bf16[656,128]{1,0:T(8,128)(2,1)S(1)}, bf16[656,128]{1,0:T(8,128)(2,1)S(1)}, u32[]{:S(2)}, u32[]{:S(2)}) collective-permute-start(bf16[656,128]{1,0:T(8,128)(2,1)S(1)} %collective-permute-done.11.refs_1_), channel_id=1, source_target_pairs={{0,4},{2,6},{4,0},{6,2},{8,12},{10,14},{12,8},{14,10},{1,5},{3,7},... | collective-permute-start | bytes 503816 | tf_op jit(solution)/shard_map/ppermute | solution.py:116
  58.8 7.1 %collective-permute-start.10 = (bf16[656,128]{1,0:T(8,128)(2,1)S(1)}, bf16[656,128]{1,0:T(8,128)(2,1)S(1)}, u32[]{:S(2)}, u32[]{:S(2)}) collective-permute-start(bf16[656,128]{1,0:T(8,128)(2,1)S(1)} %collective-permute-done.9.refs_0_), channel_id=1, source_target_pairs={{0,2},{2,0},{4,6},{6,4},{8,10},{10,8},{12,14},{14,12},{1,3},{3,1},... | collective-permute-start | bytes 503816 | tf_op jit(solution)/shard_map/ppermute | solution.py:116
  63.1 5.5 %collective-permute-start.13 = (bf16[656,128]{1,0:T(8,128)(2,1)S(1)}, bf16[656,128]{1,0:T(8,128)(2,1)S(1)}, u32[]{:S(2)}, u32[]{:S(2)}) collective-permute-start(bf16[656,128]{1,0:T(8,128)(2,1)S(1)} %collective-permute-done.12.refs_0_), channel_id=1, source_target_pairs={{0,4},{2,6},{4,0},{6,2},{8,12},{10,14},{12,8},{14,10},{1,5},{3,7},... | collective-permute-start | bytes 503816 | tf_op jit(solution)/shard_map/ppermute | solution.py:116
  63.1 14.0 %collective-permute-start.20 = (bf16[656,128]{1,0:T(8,128)(2,1)S(1)}, bf16[656,128]{1,0:T(8,128)(2,1)S(1)}, u32[]{:S(2)}, u32[]{:S(2)}) collective-permute-start(bf16[656,128]{1,0:T(8,128)(2,1)S(1)} %collective-permute-done.11.refs_1_), channel_id=1, source_target_pairs={{0,1},{1,0},{2,3},{3,2},{4,5},{5,4},{6,7},{7,6},{8,9},{9,8},{10,11... | collective-permute-start | bytes 503816 | tf_op jit(solution)/shard_map/ppermute | solution.py:362
  63.1 15.9 %collective-permute-start.17 = (bf16[656,128]{1,0:T(8,128)(2,1)S(1)}, bf16[656,128]{1,0:T(8,128)(2,1)S(1)}, u32[]{:S(2)}, u32[]{:S(2)}) collective-permute-start(bf16[656,128]{1,0:T(8,128)(2,1)S(1)} %collective-permute-done.12.refs_0_), channel_id=1, source_target_pairs={{0,1},{1,0},{2,3},{3,2},{4,5},{5,4},{6,7},{7,6},{8,9},{9,8},{10,11... | collective-permute-start | bytes 503816 | tf_op jit(solution)/shard_map/ppermute | solution.py:362
  65.9 13.2 %collective-permute-start.18 = (bf16[656,128]{1,0:T(8,128)(2,1)S(1)}, bf16[656,128]{1,0:T(8,128)(2,1)S(1)}, u32[]{:S(2)}, u32[]{:S(2)}) collective-permute-start(bf16[656,128]{1,0:T(8,128)(2,1)S(1)} %collective-permute-done.16.refs_1_), channel_id=1, source_target_pairs={{0,1},{1,0},{2,3},{3,2},{4,5},{5,4},{6,7},{7,6},{8,9},{9,8},{10,11... | collective-permute-start | bytes 503816 | tf_op jit(solution)/shard_map/ppermute | solution.py:362
  65.9 15.2 %collective-permute-start.14 = (bf16[656,128]{1,0:T(8,128)(2,1)S(1)}, bf16[656,128]{1,0:T(8,128)(2,1)S(1)}, u32[]{:S(2)}, u32[]{:S(2)}) collective-permute-start(bf16[656,128]{1,0:T(8,128)(2,1)S(1)} %collective-permute-done.10.refs_0_), channel_id=1, source_target_pairs={{0,1},{1,0},{2,3},{3,2},{4,5},{5,4},{6,7},{7,6},{8,9},{9,8},{10,11... | collective-permute-start | bytes 503816 | tf_op jit(solution)/shard_map/ppermute | solution.py:362
  68.6 12.5 %collective-permute-start.15 = (bf16[656,128]{1,0:T(8,128)(2,1)S(1)}, bf16[656,128]{1,0:T(8,128)(2,1)S(1)}, u32[]{:S(2)}, u32[]{:S(2)}) collective-permute-start(bf16[656,128]{1,0:T(8,128)(2,1)S(1)} %collective-permute-done.13.refs_1_), channel_id=1, source_target_pairs={{0,1},{1,0},{2,3},{3,2},{4,5},{5,4},{6,7},{7,6},{8,9},{9,8},{10,11... | collective-permute-start | bytes 503816 | tf_op jit(solution)/shard_map/ppermute | solution.py:362
  83.3 10.1 %collective-permute-start.24 = (bf16[128,864]{1,0:T(8,128)(2,1)S(1)}, bf16[128,864]{1,0:T(8,128)(2,1)S(1)}, u32[]{:S(2)}, u32[]{:S(2)}) collective-permute-start(bf16[128,864]{1,0:T(8,128)(2,1)S(1)} %get-tuple-element.52), channel_id=1, source_target_pairs={{0,1},{1,0},{2,3},{3,2},{4,5},{5,4},{6,7},{7,6},{8,9},{9,8},{10,11... | collective-permute-start | bytes 663560 | tf_op jit(solution)/shard_map/ppermute | solution.py:362
  94.3 7.1 %collective-permute-start.29 = (bf16[128,640]{1,0:T(8,128)(2,1)S(1)}, bf16[128,640]{1,0:T(8,128)(2,1)S(1)}, u32[]{:S(2)}, u32[]{:S(2)}) collective-permute-start(bf16[128,640]{1,0:T(8,128)(2,1)S(1)} %shard_map.116), channel_id=1, source_target_pairs={{0,4},{2,6},{4,0},{6,2},{8,12},{10,14},{12,8},{14,10},{1,5},{3,7},... | collective-permute-start | bytes 491528 | tf_op jit(solution)/shard_map/ppermute | solution.py:116
  95.7 10.1 %collective-permute-start.28 = (bf16[128,640]{1,0:T(8,128)(2,1)S(1)}, bf16[128,640]{1,0:T(8,128)(2,1)S(1)}, u32[]{:S(2)}, u32[]{:S(2)}) collective-permute-start(bf16[128,640]{1,0:T(8,128)(2,1)S(1)} %get-tuple-element.60), channel_id=1, source_target_pairs={{0,4},{2,6},{4,0},{6,2},{8,12},{10,14},{12,8},{14,10},{1,5},{3,7},... | collective-permute-start | bytes 491528 | tf_op jit(solution)/shard_map/ppermute | solution.py:116
  97.6 8.0 %collective-permute-start.26 = (bf16[128,640]{1,0:T(8,128)(2,1)S(1)}, bf16[128,640]{1,0:T(8,128)(2,1)S(1)}, u32[]{:S(2)}, u32[]{:S(2)}) collective-permute-start(bf16[128,640]{1,0:T(8,128)(2,1)S(1)} %get-tuple-element.58), channel_id=1, source_target_pairs={{0,2},{2,0},{4,6},{6,4},{8,10},{10,8},{12,14},{14,12},{1,3},{3,1},... | collective-permute-start | bytes 491528 | tf_op jit(solution)/shard_map/ppermute | solution.py:116
  101.4 6.4 %collective-permute-start.30 = (bf16[128,640]{1,0:T(8,128)(2,1)S(1)}, bf16[128,640]{1,0:T(8,128)(2,1)S(1)}, u32[]{:S(2)}, u32[]{:S(2)}) collective-permute-start(bf16[128,640]{1,0:T(8,128)(2,1)S(1)} %shard_map.117), channel_id=1, source_target_pairs={{0,2},{2,0},{4,6},{6,4},{8,10},{10,8},{12,14},{14,12},{1,3},{3,1},... | collective-permute-start | bytes 491528 | tf_op jit(solution)/shard_map/ppermute | solution.py:116
  105.3 5.4 %collective-permute-start.25 = (bf16[128,640]{1,0:T(8,128)(2,1)S(1)}, bf16[128,640]{1,0:T(8,128)(2,1)S(1)}, u32[]{:S(2)}, u32[]{:S(2)}) collective-permute-start(bf16[128,640]{1,0:T(8,128)(2,1)S(1)} %get-tuple-element.54), channel_id=1, source_target_pairs={{0,2},{2,0},{4,6},{6,4},{8,10},{10,8},{12,14},{14,12},{1,3},{3,1},... | collective-permute-start | bytes 491528 | tf_op jit(solution)/shard_map/ppermute | solution.py:116
  105.6 5.7 %collective-permute-start.27 = (bf16[128,640]{1,0:T(8,128)(2,1)S(1)}, bf16[128,640]{1,0:T(8,128)(2,1)S(1)}, u32[]{:S(2)}, u32[]{:S(2)}) collective-permute-start(bf16[128,640]{1,0:T(8,128)(2,1)S(1)} %shard_map.115), channel_id=1, source_target_pairs={{0,4},{2,6},{4,0},{6,2},{8,12},{10,14},{12,8},{14,10},{1,5},{3,7},... | collective-permute-start | bytes 491528 | tf_op jit(solution)/shard_map/ppermute | solution.py:116
  107.9 8.0 %collective-permute-start.31 = (bf16[128,640]{1,0:T(8,128)(2,1)S(1)}, bf16[128,640]{1,0:T(8,128)(2,1)S(1)}, u32[]{:S(2)}, u32[]{:S(2)}) collective-permute-start(bf16[128,640]{1,0:T(8,128)(2,1)S(1)} %shard_map.118), channel_id=1, source_target_pairs={{0,8},{2,10},{4,12},{6,14},{8,0},{10,2},{12,4},{14,6},{1,9},{3,11}... | collective-permute-start | bytes 491528 | tf_op jit(solution)/shard_map/ppermute | solution.py:116
  (2 other events, 2.1 us)
